TPU v7x, 256 devices: a whole 4x4x8 slice. The times are simulated.
256 devices in a mesh: row: 16 (over z, core), col: 16 (over y, x).
Axes of the slice: x: 4, y: 4, z: 8, core: 2. Of those that a mesh axis runs over, the one named last changes fastest.
Arguments:
- matrix: float32 [12288, 12288], P('row', 'col'), may hold values from -8 to 8
Outputs:
- updated: float32 [12288, 12288], P('row', 'col')
- reflectors: float32 [16, 12288], replicated
- coefficients: float32 [2, 16], replicated
All inputs are finite; a program needn't handle non-finite values.
Results may differ from a plain program's by a relative error of at most 0.0003.
Values sent between devices are 32-bit elements; how exact they have to be, the bound alone decides.
No kernel may reach another device: no remote copies, remote signals or barrier semaphores. Data moves between devices by JAX's collectives and lax.ppermute only.
A program may use at most 64 MiB of HBM per device.

v0:
```python
import jax
import jax.numpy as jnp
from jax import lax
from jax.sharding import PartitionSpec as P

PANEL_COLUMNS = 16


HIGH = lax.Precision.HIGHEST


def from_root(shard, axis, root):
    return lax.dynamic_index_in_dim(lax.all_gather(shard, axis), root, 0, keepdims=False)


def sent_to_all(shard, axis):
    copies = jnp.broadcast_to(shard, (lax.axis_size(axis), *shard.shape))
    return lax.all_to_all(copies, axis, split_axis=0, concat_axis=0, tiled=True)


def taken_together(shard, axis):
    everything = sent_to_all(shard, axis)
    return jnp.sum(everything, axis=0)


def laid_out(blocks, dim):
    blocks = jnp.moveaxis(blocks, 0, dim)
    shape = blocks.shape
    return blocks.reshape(*shape[:dim], shape[dim] * shape[dim + 1], *shape[dim + 2 :])


def gather_directly(shard, axis, dim):
    return laid_out(sent_to_all(shard, axis), dim)


def per_device(matrix):
    tile_rows, tile_cols = matrix.shape
    order = tile_rows * lax.axis_size("row")
    row_start = lax.axis_index("row") * tile_rows
    col_start = lax.axis_index("col") * tile_cols
    panel = from_root(jnp.transpose(matrix[:, :PANEL_COLUMNS]), "col", 0)
    whole_panel = lax.all_gather(panel, "row", axis=1, tiled=True)
    everywhere = jnp.arange(order, dtype=jnp.int32)

    def single_column(step, loop_carry_state):
        reflectors, reflected_images, reflector_scales, below_diagonal = loop_carry_state
        local_reflectors = lax.dynamic_slice_in_dim(reflectors, row_start, tile_rows, 1)
        local_images = lax.dynamic_slice_in_dim(reflected_images, row_start, tile_rows, 1)
        reflector_entries = lax.dynamic_index_in_dim(reflectors, step, 1, False)
        image_entries = lax.dynamic_index_in_dim(reflected_images, step, 1, False)
        column_now = lax.dynamic_index_in_dim(whole_panel, step, 0, False)
        full_column = (
            column_now
            - jnp.dot(image_entries, reflectors, precision=HIGH)
            - jnp.dot(reflector_entries, reflected_images, precision=HIGH)
        )
        below = jnp.where(everywhere > step, full_column, 0.0)
        leading = lax.dynamic_index_in_dim(full_column, step + 1, 0, False)
        norm_value = jnp.sqrt(jnp.sum(below * below))
        reflector = jnp.where(everywhere == step + 1, 1.0, below / (leading + norm_value))
        reflector_scale = 1.0 + leading / norm_value
        reflector_cols = lax.dynamic_slice_in_dim(reflector, col_start, tile_cols, 0)
        images_dot = jnp.dot(reflected_images, reflector, precision=HIGH)
        reflect_dot = jnp.dot(reflectors, reflector, precision=HIGH)
        product = taken_together(jnp.dot(matrix, reflector_cols, precision=HIGH), "col")
        local_image = reflector_scale * (
            product
            - jnp.dot(images_dot, local_reflectors, precision=HIGH)
            - jnp.dot(reflect_dot, local_images, precision=HIGH)
        )
        image = gather_directly(local_image, "row", 0)
        image = image - 0.5 * reflector_scale * jnp.sum(image * reflector) * reflector
        reflectors = reflectors.at[step].set(reflector)
        reflected_images = reflected_images.at[step].set(image)
        reflector_scales = reflector_scales.at[step].set(reflector_scale)
        below_diagonal = below_diagonal.at[step].set(-norm_value)
        return (reflectors, reflected_images, reflector_scales, below_diagonal)

    initial_state = (
        jnp.zeros((PANEL_COLUMNS, order), jnp.float32),
        jnp.zeros((PANEL_COLUMNS, order), jnp.float32),
        jnp.zeros((PANEL_COLUMNS,), jnp.float32),
        jnp.zeros((PANEL_COLUMNS,), jnp.float32),
    )
    reflectors, reflected_images, reflector_scales, below_diagonal = lax.fori_loop(
        0, PANEL_COLUMNS, single_column, initial_state
    )
    left_side = jnp.concatenate(
        [
            lax.dynamic_slice_in_dim(reflectors, row_start, tile_rows, 1),
            lax.dynamic_slice_in_dim(reflected_images, row_start, tile_rows, 1),
        ],
        axis=0,
    )
    right_side = jnp.concatenate(
        [
            lax.dynamic_slice_in_dim(reflected_images, col_start, tile_cols, 1),
            lax.dynamic_slice_in_dim(reflectors, col_start, tile_cols, 1),
        ],
        axis=0,
    )
    updated = matrix - jnp.einsum("kr,kc->rc", left_side, right_side, precision=HIGH)
    return (updated, reflectors, jnp.stack([reflector_scales, below_diagonal]))


def solution(mesh):
    placed = (P("row", "col"),)
    return jax.shard_map(
        per_device,
        mesh=mesh,
        in_specs=placed,
        out_specs=(P("row", "col"), P(), P()),
        check_vma=False,
    )
```

profile of v0, /device:TPU:1, one launch (start us, length us, event | category | flops | bytes accessed | tf_op | source)
XLA Modules:
  0.0 622.1 jit_solution(10111150208953763046)
XLA Ops:
  1.8 20.3 %all-gather = f32[256,768]{1,0:T(8,128)S(1)} all-gather(f32[16,768]{1,0:T(8,128)S(1)} %bitcast.96), channel_id=2, replica_groups=mesh['row'=16,'col'=16] {'col'}, dimensions={0}, use_global_device_ids=true | all-gather | bytes 835584 | tf_op jit(solution)/shard_map/all_gather | solution.py:13
  22.1 27.8 %all-gather.2 = f32[16,12288]{1,0:T(8,128)S(1)} all-gather(f32[16,768]{1,0:T(8,128)S(1)} %slice.92), channel_id=4, replica_groups=mesh['row'=16,'col'=16] {'row'}, dimensions={1}, use_global_device_ids=true | all-gather | bytes 835584 | tf_op jit(solution)/shard_map/all_gather | solution.py:42
  50.1 566.2 %while.27 = (s32[]{:T(128)}, f32[16,12288]{1,0:T(8,128)S(1)}, f32[16,12288]{1,0:T(8,128)S(1)}, f32[16]{0:T(128)S(1)}, f32[16]{0:T(128)S(1)}, /*index=5*/f32[16,1...) while((s32[]{:T(128)}, f32[16,12288]{1,0:T(8,128)S(1)}, ...), condition=%wide.region_5.6_spmd.clone.clone, body=%wide.region_0.5_spmd.clone.clone.sunk | while | flops 17155600 | bytes 7421153 | solution.py:85
  70.4 5.2 all-to-all-start.1
  76.4 6.7 %all-to-all-done.1 = f32[16,1,768]{2,1,0:T(1,128)S(1)} async-done(((f32[16,1,768]{2,1,0:T(1,128)}), f32[16,1,768]{2,1,0:T(1,128)S(1)}, u32[]{:S(2)}, u32[]{:S(2)}) %all-to-all-start.1) | async-done | bytes 49184 | tf_op jit(solution)/shard_map/while/body/eval_jaxpr/all_to_all | solution.py:18
  106.1 4.8 all-to-all-start.1
  111.6 6.8 %all-to-all-done.1 = f32[16,1,768]{2,1,0:T(1,128)S(1)} async-done(((f32[16,1,768]{2,1,0:T(1,128)}), f32[16,1,768]{2,1,0:T(1,128)S(1)}, u32[]{:S(2)}, u32[]{:S(2)}) %all-to-all-start.1) | async-done | bytes 49184 | tf_op jit(solution)/shard_map/while/body/eval_jaxpr/all_to_all | solution.py:18
  141.4 4.8 all-to-all-start.1
  146.9 6.8 %all-to-all-done.1 = f32[16,1,768]{2,1,0:T(1,128)S(1)} async-done(((f32[16,1,768]{2,1,0:T(1,128)}), f32[16,1,768]{2,1,0:T(1,128)S(1)}, u32[]{:S(2)}, u32[]{:S(2)}) %all-to-all-start.1) | async-done | bytes 49184 | tf_op jit(solution)/shard_map/while/body/eval_jaxpr/all_to_all | solution.py:18
  176.7 4.8 all-to-all-start.1
  182.2 6.8 %all-to-all-done.1 = f32[16,1,768]{2,1,0:T(1,128)S(1)} async-done(((f32[16,1,768]{2,1,0:T(1,128)}), f32[16,1,768]{2,1,0:T(1,128)S(1)}, u32[]{:S(2)}, u32[]{:S(2)}) %all-to-all-start.1) | async-done | bytes 49184 | tf_op jit(solution)/shard_map/while/body/eval_jaxpr/all_to_all | solution.py:18
  212.0 4.8 all-to-all-start.1
  217.5 6.8 %all-to-all-done.1 = f32[16,1,768]{2,1,0:T(1,128)S(1)} async-done(((f32[16,1,768]{2,1,0:T(1,128)}), f32[16,1,768]{2,1,0:T(1,128)S(1)}, u32[]{:S(2)}, u32[]{:S(2)}) %all-to-all-start.1) | async-done | bytes 49184 | tf_op jit(solution)/shard_map/while/body/eval_jaxpr/all_to_all | solution.py:18
  247.3 4.8 all-to-all-start.1
  252.8 6.8 %all-to-all-done.1 = f32[16,1,768]{2,1,0:T(1,128)S(1)} async-done(((f32[16,1,768]{2,1,0:T(1,128)}), f32[16,1,768]{2,1,0:T(1,128)S(1)}, u32[]{:S(2)}, u32[]{:S(2)}) %all-to-all-start.1) | async-done | bytes 49184 | tf_op jit(solution)/shard_map/while/body/eval_jaxpr/all_to_all | solution.py:18
  282.6 4.8 all-to-all-start.1
  288.1 6.8 %all-to-all-done.1 = f32[16,1,768]{2,1,0:T(1,128)S(1)} async-done(((f32[16,1,768]{2,1,0:T(1,128)}), f32[16,1,768]{2,1,0:T(1,128)S(1)}, u32[]{:S(2)}, u32[]{:S(2)}) %all-to-all-start.1) | async-done | bytes 49184 | tf_op jit(solution)/shard_map/while/body/eval_jaxpr/all_to_all | solution.py:18
  317.8 4.8 all-to-all-start.1
  323.3 6.8 %all-to-all-done.1 = f32[16,1,768]{2,1,0:T(1,128)S(1)} async-done(((f32[16,1,768]{2,1,0:T(1,128)}), f32[16,1,768]{2,1,0:T(1,128)S(1)}, u32[]{:S(2)}, u32[]{:S(2)}) %all-to-all-start.1) | async-done | bytes 49184 | tf_op jit(solution)/shard_map/while/body/eval_jaxpr/all_to_all | solution.py:18
  353.1 4.8 all-to-all-start.1
  358.6 6.8 %all-to-all-done.1 = f32[16,1,768]{2,1,0:T(1,128)S(1)} async-done(((f32[16,1,768]{2,1,0:T(1,128)}), f32[16,1,768]{2,1,0:T(1,128)S(1)}, u32[]{:S(2)}, u32[]{:S(2)}) %all-to-all-start.1) | async-done | bytes 49184 | tf_op jit(solution)/shard_map/while/body/eval_jaxpr/all_to_all | solution.py:18
  388.4 4.8 all-to-all-start.1
  393.9 6.8 %all-to-all-done.1 = f32[16,1,768]{2,1,0:T(1,128)S(1)} async-done(((f32[16,1,768]{2,1,0:T(1,128)}), f32[16,1,768]{2,1,0:T(1,128)S(1)}, u32[]{:S(2)}, u32[]{:S(2)}) %all-to-all-start.1) | async-done | bytes 49184 | tf_op jit(solution)/shard_map/while/body/eval_jaxpr/all_to_all | solution.py:18
  423.7 4.8 all-to-all-start.1
  429.2 6.8 %all-to-all-done.1 = f32[16,1,768]{2,1,0:T(1,128)S(1)} async-done(((f32[16,1,768]{2,1,0:T(1,128)}), f32[16,1,768]{2,1,0:T(1,128)S(1)}, u32[]{:S(2)}, u32[]{:S(2)}) %all-to-all-start.1) | async-done | bytes 49184 | tf_op jit(solution)/shard_map/while/body/eval_jaxpr/all_to_all | solution.py:18
  459.0 4.8 all-to-all-start.1
  464.5 6.8 %all-to-all-done.1 = f32[16,1,768]{2,1,0:T(1,128)S(1)} async-done(((f32[16,1,768]{2,1,0:T(1,128)}), f32[16,1,768]{2,1,0:T(1,128)S(1)}, u32[]{:S(2)}, u32[]{:S(2)}) %all-to-all-start.1) | async-done | bytes 49184 | tf_op jit(solution)/shard_map/while/body/eval_jaxpr/all_to_all | solution.py:18
  499.8 6.8 %all-to-all-done.1 = f32[16,1,768]{2,1,0:T(1,128)S(1)} async-done(((f32[16,1,768]{2,1,0:T(1,128)}), f32[16,1,768]{2,1,0:T(1,128)S(1)}, u32[]{:S(2)}, u32[]{:S(2)}) %all-to-all-start.1) | async-done | bytes 49184 | tf_op jit(solution)/shard_map/while/body/eval_jaxpr/all_to_all | solution.py:18
  535.1 6.8 %all-to-all-done.1 = f32[16,1,768]{2,1,0:T(1,128)S(1)} async-done(((f32[16,1,768]{2,1,0:T(1,128)}), f32[16,1,768]{2,1,0:T(1,128)S(1)}, u32[]{:S(2)}, u32[]{:S(2)}) %all-to-all-start.1) | async-done | bytes 49184 | tf_op jit(solution)/shard_map/while/body/eval_jaxpr/all_to_all | solution.py:18
  570.3 6.8 %all-to-all-done.1 = f32[16,1,768]{2,1,0:T(1,128)S(1)} async-done(((f32[16,1,768]{2,1,0:T(1,128)}), f32[16,1,768]{2,1,0:T(1,128)S(1)}, u32[]{:S(2)}, u32[]{:S(2)}) %all-to-all-start.1) | async-done | bytes 49184 | tf_op jit(solution)/shard_map/while/body/eval_jaxpr/all_to_all | solution.py:18
  605.6 6.8 %all-to-all-done.1 = f32[16,1,768]{2,1,0:T(1,128)S(1)} async-done(((f32[16,1,768]{2,1,0:T(1,128)}), f32[16,1,768]{2,1,0:T(1,128)S(1)}, u32[]{:S(2)}, u32[]{:S(2)}) %all-to-all-start.1) | async-done | bytes 49184 | tf_op jit(solution)/shard_map/while/body/eval_jaxpr/all_to_all | solution.py:18
  616.9 5.1 convolution_subtract_fusion
  (465 shorter events, 357.8 us)
Async XLA Ops:
  58.5 11.1 %all-to-all-start = ((f32[16,1,768]{2,1,0:T(1,128)}), f32[16,1,768]{2,1,0:T(1,128)S(1)}, u32[]{:S(2)}, u32[]{:S(2)}) async-start(f32[16,1,768]{2,1,0:T(1,128)} %broadcast_in_dim.73), calls=%async_computation | async-start | bytes 98304 | tf_op jit(solution)/shard_map/while/body/eval_jaxpr/all_to_all | solution.py:18
  70.4 12.7 %all-to-all-start.1 = ((f32[16,1,768]{2,1,0:T(1,128)}), f32[16,1,768]{2,1,0:T(1,128)S(1)}, u32[]{:S(2)}, u32[]{:S(2)}) async-start(f32[16,1,768]{2,1,0:T(1,128)} %broadcast_in_dim.74), calls=%async_computation.1 | async-start | bytes 98304 | tf_op jit(solution)/shard_map/while/body/eval_jaxpr/all_to_all | solution.py:18
  95.5 9.9 %all-to-all-start = ((f32[16,1,768]{2,1,0:T(1,128)}), f32[16,1,768]{2,1,0:T(1,128)S(1)}, u32[]{:S(2)}, u32[]{:S(2)}) async-start(f32[16,1,768]{2,1,0:T(1,128)} %broadcast_in_dim.73), calls=%async_computation | async-start | bytes 98304 | tf_op jit(solution)/shard_map/while/body/eval_jaxpr/all_to_all | solution.py:18
  106.1 12.3 %all-to-all-start.1 = ((f32[16,1,768]{2,1,0:T(1,128)}), f32[16,1,768]{2,1,0:T(1,128)S(1)}, u32[]{:S(2)}, u32[]{:S(2)}) async-start(f32[16,1,768]{2,1,0:T(1,128)} %broadcast_in_dim.74), calls=%async_computation.1 | async-start | bytes 98304 | tf_op jit(solution)/shard_map/while/body/eval_jaxpr/all_to_all | solution.py:18
  130.8 9.9 %all-to-all-start = ((f32[16,1,768]{2,1,0:T(1,128)}), f32[16,1,768]{2,1,0:T(1,128)S(1)}, u32[]{:S(2)}, u32[]{:S(2)}) async-start(f32[16,1,768]{2,1,0:T(1,128)} %broadcast_in_dim.73), calls=%async_computation | async-start | bytes 98304 | tf_op jit(solution)/shard_map/while/body/eval_jaxpr/all_to_all | solution.py:18
  141.4 12.3 %all-to-all-start.1 = ((f32[16,1,768]{2,1,0:T(1,128)}), f32[16,1,768]{2,1,0:T(1,128)S(1)}, u32[]{:S(2)}, u32[]{:S(2)}) async-start(f32[16,1,768]{2,1,0:T(1,128)} %broadcast_in_dim.74), calls=%async_computation.1 | async-start | bytes 98304 | tf_op jit(solution)/shard_map/while/body/eval_jaxpr/all_to_all | solution.py:18
  166.1 9.9 %all-to-all-start = ((f32[16,1,768]{2,1,0:T(1,128)}), f32[16,1,768]{2,1,0:T(1,128)S(1)}, u32[]{:S(2)}, u32[]{:S(2)}) async-start(f32[16,1,768]{2,1,0:T(1,128)} %broadcast_in_dim.73), calls=%async_computation | async-start | bytes 98304 | tf_op jit(solution)/shard_map/while/body/eval_jaxpr/all_to_all | solution.py:18
  176.7 12.3 %all-to-all-start.1 = ((f32[16,1,768]{2,1,0:T(1,128)}), f32[16,1,768]{2,1,0:T(1,128)S(1)}, u32[]{:S(2)}, u32[]{:S(2)}) async-start(f32[16,1,768]{2,1,0:T(1,128)} %broadcast_in_dim.74), calls=%async_computation.1 | async-start | bytes 98304 | tf_op jit(solution)/shard_map/while/body/eval_jaxpr/all_to_all | solution.py:18
  201.4 9.9 %all-to-all-start = ((f32[16,1,768]{2,1,0:T(1,128)}), f32[16,1,768]{2,1,0:T(1,128)S(1)}, u32[]{:S(2)}, u32[]{:S(2)}) async-start(f32[16,1,768]{2,1,0:T(1,128)} %broadcast_in_dim.73), calls=%async_computation | async-start | bytes 98304 | tf_op jit(solution)/shard_map/while/body/eval_jaxpr/all_to_all | solution.py:18
  212.0 12.3 %all-to-all-start.1 = ((f32[16,1,768]{2,1,0:T(1,128)}), f32[16,1,768]{2,1,0:T(1,128)S(1)}, u32[]{:S(2)}, u32[]{:S(2)}) async-start(f32[16,1,768]{2,1,0:T(1,128)} %broadcast_in_dim.74), calls=%async_computation.1 | async-start | bytes 98304 | tf_op jit(solution)/shard_map/while/body/eval_jaxpr/all_to_all | solution.py:18
  236.7 9.9 %all-to-all-start = ((f32[16,1,768]{2,1,0:T(1,128)}), f32[16,1,768]{2,1,0:T(1,128)S(1)}, u32[]{:S(2)}, u32[]{:S(2)}) async-start(f32[16,1,768]{2,1,0:T(1,128)} %broadcast_in_dim.73), calls=%async_computation | async-start | bytes 98304 | tf_op jit(solution)/shard_map/while/body/eval_jaxpr/all_to_all | solution.py:18
  247.3 12.3 %all-to-all-start.1 = ((f32[16,1,768]{2,1,0:T(1,128)}), f32[16,1,768]{2,1,0:T(1,128)S(1)}, u32[]{:S(2)}, u32[]{:S(2)}) async-start(f32[16,1,768]{2,1,0:T(1,128)} %broadcast_in_dim.74), calls=%async_computation.1 | async-start | bytes 98304 | tf_op jit(solution)/shard_map/while/body/eval_jaxpr/all_to_all | solution.py:18
  271.9 9.9 %all-to-all-start = ((f32[16,1,768]{2,1,0:T(1,128)}), f32[16,1,768]{2,1,0:T(1,128)S(1)}, u32[]{:S(2)}, u32[]{:S(2)}) async-start(f32[16,1,768]{2,1,0:T(1,128)} %broadcast_in_dim.73), calls=%async_computation | async-start | bytes 98304 | tf_op jit(solution)/shard_map/while/body/eval_jaxpr/all_to_all | solution.py:18
  282.6 12.3 %all-to-all-start.1 = ((f32[16,1,768]{2,1,0:T(1,128)}), f32[16,1,768]{2,1,0:T(1,128)S(1)}, u32[]{:S(2)}, u32[]{:S(2)}) async-start(f32[16,1,768]{2,1,0:T(1,128)} %broadcast_in_dim.74), calls=%async_computation.1 | async-start | bytes 98304 | tf_op jit(solution)/shard_map/while/body/eval_jaxpr/all_to_all | solution.py:18
  307.2 9.9 %all-to-all-start = ((f32[16,1,768]{2,1,0:T(1,128)}), f32[16,1,768]{2,1,0:T(1,128)S(1)}, u32[]{:S(2)}, u32[]{:S(2)}) async-start(f32[16,1,768]{2,1,0:T(1,128)} %broadcast_in_dim.73), calls=%async_computation | async-start | bytes 98304 | tf_op jit(solution)/shard_map/while/body/eval_jaxpr/all_to_all | solution.py:18
  317.8 12.3 %all-to-all-start.1 = ((f32[16,1,768]{2,1,0:T(1,128)}), f32[16,1,768]{2,1,0:T(1,128)S(1)}, u32[]{:S(2)}, u32[]{:S(2)}) async-start(f32[16,1,768]{2,1,0:T(1,128)} %broadcast_in_dim.74), calls=%async_computation.1 | async-start | bytes 98304 | tf_op jit(solution)/shard_map/while/body/eval_jaxpr/all_to_all | solution.py:18
  342.5 9.9 %all-to-all-start = ((f32[16,1,768]{2,1,0:T(1,128)}), f32[16,1,768]{2,1,0:T(1,128)S(1)}, u32[]{:S(2)}, u32[]{:S(2)}) async-start(f32[16,1,768]{2,1,0:T(1,128)} %broadcast_in_dim.73), calls=%async_computation | async-start | bytes 98304 | tf_op jit(solution)/shard_map/while/body/eval_jaxpr/all_to_all | solution.py:18
  353.1 12.3 %all-to-all-start.1 = ((f32[16,1,768]{2,1,0:T(1,128)}), f32[16,1,768]{2,1,0:T(1,128)S(1)}, u32[]{:S(2)}, u32[]{:S(2)}) async-start(f32[16,1,768]{2,1,0:T(1,128)} %broadcast_in_dim.74), calls=%async_computation.1 | async-start | bytes 98304 | tf_op jit(solution)/shard_map/while/body/eval_jaxpr/all_to_all | solution.py:18
  377.8 9.9 %all-to-all-start = ((f32[16,1,768]{2,1,0:T(1,128)}), f32[16,1,768]{2,1,0:T(1,128)S(1)}, u32[]{:S(2)}, u32[]{:S(2)}) async-start(f32[16,1,768]{2,1,0:T(1,128)} %broadcast_in_dim.73), calls=%async_computation | async-start | bytes 98304 | tf_op jit(solution)/shard_map/while/body/eval_jaxpr/all_to_all | solution.py:18
  388.4 12.3 %all-to-all-start.1 = ((f32[16,1,768]{2,1,0:T(1,128)}), f32[16,1,768]{2,1,0:T(1,128)S(1)}, u32[]{:S(2)}, u32[]{:S(2)}) async-start(f32[16,1,768]{2,1,0:T(1,128)} %broadcast_in_dim.74), calls=%async_computation.1 | async-start | bytes 98304 | tf_op jit(solution)/shard_map/while/body/eval_jaxpr/all_to_all | solution.py:18
  413.1 9.9 %all-to-all-start = ((f32[16,1,768]{2,1,0:T(1,128)}), f32[16,1,768]{2,1,0:T(1,128)S(1)}, u32[]{:S(2)}, u32[]{:S(2)}) async-start(f32[16,1,768]{2,1,0:T(1,128)} %broadcast_in_dim.73), calls=%async_computation | async-start | bytes 98304 | tf_op jit(solution)/shard_map/while/body/eval_jaxpr/all_to_all | solution.py:18
  423.7 12.3 %all-to-all-start.1 = ((f32[16,1,768]{2,1,0:T(1,128)}), f32[16,1,768]{2,1,0:T(1,128)S(1)}, u32[]{:S(2)}, u32[]{:S(2)}) async-start(f32[16,1,768]{2,1,0:T(1,128)} %broadcast_in_dim.74), calls=%async_computation.1 | async-start | bytes 98304 | tf_op jit(solution)/shard_map/while/body/eval_jaxpr/all_to_all | solution.py:18
  448.4 9.9 %all-to-all-start = ((f32[16,1,768]{2,1,0:T(1,128)}), f32[16,1,768]{2,1,0:T(1,128)S(1)}, u32[]{:S(2)}, u32[]{:S(2)}) async-start(f32[16,1,768]{2,1,0:T(1,128)} %broadcast_in_dim.73), calls=%async_computation | async-start | bytes 98304 | tf_op jit(solution)/shard_map/while/body/eval_jaxpr/all_to_all | solution.py:18
  459.0 12.3 %all-to-all-start.1 = ((f32[16,1,768]{2,1,0:T(1,128)}), f32[16,1,768]{2,1,0:T(1,128)S(1)}, u32[]{:S(2)}, u32[]{:S(2)}) async-start(f32[16,1,768]{2,1,0:T(1,128)} %broadcast_in_dim.74), calls=%async_computation.1 | async-start | bytes 98304 | tf_op jit(solution)/shard_map/while/body/eval_jaxpr/all_to_all | solution.py:18
  483.6 9.9 %all-to-all-start = ((f32[16,1,768]{2,1,0:T(1,128)}), f32[16,1,768]{2,1,0:T(1,128)S(1)}, u32[]{:S(2)}, u32[]{:S(2)}) async-start(f32[16,1,768]{2,1,0:T(1,128)} %broadcast_in_dim.73), calls=%async_computation | async-start | bytes 98304 | tf_op jit(solution)/shard_map/while/body/eval_jaxpr/all_to_all | solution.py:18
  494.3 12.3 %all-to-all-start.1 = ((f32[16,1,768]{2,1,0:T(1,128)}), f32[16,1,768]{2,1,0:T(1,128)S(1)}, u32[]{:S(2)}, u32[]{:S(2)}) async-start(f32[16,1,768]{2,1,0:T(1,128)} %broadcast_in_dim.74), calls=%async_computation.1 | async-start | bytes 98304 | tf_op jit(solution)/shard_map/while/body/eval_jaxpr/all_to_all | solution.py:18
  518.9 9.9 %all-to-all-start = ((f32[16,1,768]{2,1,0:T(1,128)}), f32[16,1,768]{2,1,0:T(1,128)S(1)}, u32[]{:S(2)}, u32[]{:S(2)}) async-start(f32[16,1,768]{2,1,0:T(1,128)} %broadcast_in_dim.73), calls=%async_computation | async-start | bytes 98304 | tf_op jit(solution)/shard_map/while/body/eval_jaxpr/all_to_all | solution.py:18
  529.5 12.3 %all-to-all-start.1 = ((f32[16,1,768]{2,1,0:T(1,128)}), f32[16,1,768]{2,1,0:T(1,128)S(1)}, u32[]{:S(2)}, u32[]{:S(2)}) async-start(f32[16,1,768]{2,1,0:T(1,128)} %broadcast_in_dim.74), calls=%async_computation.1 | async-start | bytes 98304 | tf_op jit(solution)/shard_map/while/body/eval_jaxpr/all_to_all | solution.py:18
  554.2 9.9 %all-to-all-start = ((f32[16,1,768]{2,1,0:T(1,128)}), f32[16,1,768]{2,1,0:T(1,128)S(1)}, u32[]{:S(2)}, u32[]{:S(2)}) async-start(f32[16,1,768]{2,1,0:T(1,128)} %broadcast_in_dim.73), calls=%async_computation | async-start | bytes 98304 | tf_op jit(solution)/shard_map/while/body/eval_jaxpr/all_to_all | solution.py:18
  564.8 12.3 %all-to-all-start.1 = ((f32[16,1,768]{2,1,0:T(1,128)}), f32[16,1,768]{2,1,0:T(1,128)S(1)}, u32[]{:S(2)}, u32[]{:S(2)}) async-start(f32[16,1,768]{2,1,0:T(1,128)} %broadcast_in_dim.74), calls=%async_computation.1 | async-start | bytes 98304 | tf_op jit(solution)/shard_map/while/body/eval_jaxpr/all_to_all | solution.py:18
  589.5 9.9 %all-to-all-start = ((f32[16,1,768]{2,1,0:T(1,128)}), f32[16,1,768]{2,1,0:T(1,128)S(1)}, u32[]{:S(2)}, u32[]{:S(2)}) async-start(f32[16,1,768]{2,1,0:T(1,128)} %broadcast_in_dim.73), calls=%async_computation | async-start | bytes 98304 | tf_op jit(solution)/shard_map/while/body/eval_jaxpr/all_to_all | solution.py:18
  600.1 12.3 %all-to-all-start.1 = ((f32[16,1,768]{2,1,0:T(1,128)}), f32[16,1,768]{2,1,0:T(1,128)S(1)}, u32[]{:S(2)}, u32[]{:S(2)}) async-start(f32[16,1,768]{2,1,0:T(1,128)} %broadcast_in_dim.74), calls=%async_computation.1 | async-start | bytes 98304 | tf_op jit(solution)/shard_map/while/body/eval_jaxpr/all_to_all | solution.py:18
  (2 other events, 55.2 us)
where the time goes:
time: 626 us; the launch traced here: 622 us
  waiting for transfers between devices  159 us (25%)
  starting transfers between devices  134 us (21%)
  matrix products  118 us (19%)
  local copies, waits for them, and re-layouts  69.4 us (11%)
  other arithmetic  48.4 us (8%)
  blocking collectives  48.1 us (8%)
  loops' own time  44.1 us (7%)
    all_to_all x32, waiting for transfers between devices, sent_to_all(): return lax.all_to_all(copies, axis, split_axis=0, concat_axis=0, tiled=True)  159 us
    all_to_all x32, starting transfers between devices, sent_to_all(): return lax.all_to_all(copies, axis, split_axis=0, concat_axis=0, tiled=True)  134 us
    dot_general x16, matrix products, single_column(): jnp.dot(matrix, reflector_cols, precision=HIGH)  58.7 us
    another operation x1, loops' own time, per_device(): lax.fori_loop(0, PANEL_COLUMNS, single_column, initial_state)  44.1 us
    all_gather x1, blocking collectives, per_device(): whole_panel = lax.all_gather(panel, 'row', axis=1, tiled=True)  27.8 us
    another operation x32, other arithmetic  23.7 us
    broadcast_in_dim x32, local copies, waits for them, and re-layouts, sent_to_all(): copies = jnp.broadcast_to(shard, (lax.axis_size(axis), *shard.shape))  20.7 us
    all_gather x1, blocking collectives, from_root(): lax.all_gather(shard, axis)  20.3 us
  transfers between devices with their start and end apart: 32, of which 32 were waited for; matrix products, arithmetic and copies ran while one was open for 8% of the time, Pallas kernels for 0%

commit v1 on v0

v1 whole, which is shorter than its diff:
```python
import jax
import jax.numpy as jnp
from jax import lax
from jax.experimental import pallas as pl
from jax.experimental.pallas import tpu as pltpu
from jax.sharding import PartitionSpec as P

PANEL_COLUMNS = 16
LANES = 128
TILES = 12
SCALE, COEF = TILES, TILES + 1
OWN = 48

VMEM = pl.BlockSpec(memory_space=pltpu.VMEM)
SMEM = pl.BlockSpec(memory_space=pltpu.SMEM)
ANY = pl.BlockSpec(memory_space=pl.ANY)


def total(x):
    return jnp.sum(jnp.sum(x, axis=0, keepdims=True), axis=1, keepdims=True)


def iota(shape, dim):
    return lax.broadcasted_iota(jnp.int32, shape, dim)


def unpack(load):
    lane = iota((8, LANES), 1)
    tiles = []
    for gm in range(4):
        q = [load(8 * gm + k) for k in range(8)]
        tiles.append(jnp.where(lane < 48, q[0], jnp.where(lane < 96, q[1], q[2])))
        tiles.append(jnp.where(lane < 16, q[2], jnp.where(lane < 64, q[3], jnp.where(lane < 112, q[4], q[5]))))
        tiles.append(jnp.where(lane < 32, q[5], jnp.where(lane < 80, q[6], q[7])))
    return tiles


def tree_sum(xs):
    xs = list(xs)
    while len(xs) > 1:
        xs = [xs[i] + xs[i + 1] if i + 1 < len(xs) else xs[i] for i in range(0, len(xs), 2)]
    return xs[0]


def position(m):
    return (iota((8, LANES), 0) * TILES + m) * LANES + iota((8, LANES), 1)


def message(first, second, offset):
    row, lane = iota((OWN, LANES), 0), iota((OWN, LANES), 1)
    here = (row + offset) & (LANES - 1)
    there = (row + offset + OWN) & (LANES - 1)
    picked = jnp.where(lane == here, first, 0.0) + jnp.where(lane == there, second, 0.0)
    return jnp.sum(picked, axis=0, keepdims=True)


def own_column(rows_ref, k):
    head = rows_ref[0, :, 0:LANES]
    return jnp.sum(jnp.where(iota((OWN, LANES), 1) == k, head, 0.0), axis=1, keepdims=True)


def first_body(own, rows_ref, out_ref):
    out_ref[...] = jnp.broadcast_to(
        message(own_column(rows_ref, 0), own_column(rows_ref, 1), own[0]), out_ref.shape
    )


def image_of(got_ref, h_ref, u, scale):
    y = unpack(lambda first: got_ref[pl.ds(first, 8, stride=32), :])
    p = [scale * (y[m] - h_ref[m]) for m in range(TILES)]
    kappa = 0.5 * scale * total(tree_sum(p[m] * u[m] for m in range(TILES)))
    return p, kappa


def step_body(col, own, got_ref, base_ref, h_ref, u_ref, rows_ref, w_ref, un_ref, out_ref, flat_ref):
    j = col[0]
    u = [u_ref[m] for m in range(TILES)]
    scale = u_ref[SCALE, 0:1, 0:1]
    p, kappa = image_of(got_ref, h_ref, u, scale)
    lane1 = iota((1, LANES), 1)

    def at(x, k):
        return jnp.sum(jnp.where(lane1 == k, x[0:1, :], 0.0), axis=1, keepdims=True)

    factor = at(p[0], j) - kappa * at(u[0], j) - kappa
    leading = at(base_ref[0], j + 1) - at(p[0], j + 1) - factor * at(u[0], j + 1)
    below = []
    for m in range(TILES):
        column = base_ref[m] - p[m] - factor * u[m]
        if m == 0:
            column = jnp.where(position(m) > j, column, 0.0)
        below.append(column)
        rest = jnp.where(position(m) == j + 1, 0.0, column) if m == 0 else column
        flat_ref[pl.ds(m, 8, stride=TILES), :] = rest
    norm = jnp.sqrt(total(tree_sum(b * b for b in below)))
    inverse = 1.0 / (leading + norm)
    scale_now = 1.0 + leading / norm
    acc = [jnp.zeros((OWN, LANES), jnp.float32) for _ in range(2)]
    for s in range(96):
        k, t = divmod(s, 6)
        acc[s % 2] = acc[s % 2] + rows_ref[k, :, LANES * t : LANES * (t + 1)] * flat_ref[s : s + 1, :]
    product = jnp.sum(acc[0] + acc[1], axis=1, keepdims=True) * inverse + own_column(rows_ref, j + 1)
    out_ref[...] = jnp.broadcast_to(
        message(product, own_column(rows_ref, j + 2), own[0]), out_ref.shape
    )
    for m in range(TILES):
        w_ref[m] = p[m] - kappa * u[m]
        r = below[m] * inverse
        un_ref[m] = jnp.where(position(m) == j + 1, 1.0, r) if m == 0 else r
    un_ref[SCALE] = jnp.broadcast_to(scale_now, (8, LANES))
    lane8, row8 = iota((8, LANES), 1), iota((8, LANES), 0)
    un_ref[COEF] = jnp.where(lane8 == j, jnp.where(row8 == 0, scale_now, -norm), u_ref[COEF])


def history_body(col, got_ref, w_ref, u_ref, un_ref, hist_ref, base_ref, h_ref, hist_out, hist, sems):
    j = col[0]
    row = (j + PANEL_COLUMNS - 1) % PANEL_COLUMNS
    whole = pltpu.make_async_copy(hist_ref, hist, sems.at[0])
    whole.start()
    lane1 = iota((1, LANES), 1)
    h = [jnp.zeros((8, LANES), jnp.float32) for _ in range(TILES)]
    base = unpack(lambda first: pltpu.roll(got_ref[pl.ds(first, 8, stride=32), :], LANES - OWN, 1))
    un = [un_ref[m] for m in range(TILES)]
    whole.wait()
    keep_v = pltpu.make_async_copy(u_ref.at[pl.ds(0, TILES)], hist_out.at[0, row], sems.at[1])
    keep_w = pltpu.make_async_copy(w_ref, hist_out.at[1, row], sems.at[2])
    keep_v.start()
    keep_w.start()
    for m in range(TILES):
        hist[0, row, m] = u_ref[m]
        hist[1, row, m] = w_ref[m]
    for i in range(PANEL_COLUMNS):
        v = [hist[0, i, m] for m in range(TILES)]
        w = [hist[1, i, m] for m in range(TILES)]
        vu = total(tree_sum(v[m] * un[m] for m in range(TILES)))
        wu = total(tree_sum(w[m] * un[m] for m in range(TILES)))
        vj = jnp.sum(jnp.where(lane1 == j + 1, v[0][0:1, :], 0.0), axis=1, keepdims=True)
        wj = jnp.sum(jnp.where(lane1 == j + 1, w[0][0:1, :], 0.0), axis=1, keepdims=True)
        for m in range(TILES):
            h[m] = h[m] + (wu * v[m] + vu * w[m])
            base[m] = base[m] - (wj * v[m] + vj * w[m])
    for m in range(TILES):
        h_ref[m] = h[m]
        base_ref[m] = base[m]
    keep_v.wait()
    keep_w.wait()


def last_body(own, got_ref, h_ref, u_ref, hist_ref, matrix_ref, updated_ref, whole_ref, hist, block, whole, sides, sems):
    read_hist = pltpu.make_async_copy(hist_ref, hist, sems.at[0])
    read_block = pltpu.make_async_copy(matrix_ref, block, sems.at[1])
    read_hist.start()
    read_block.start()
    u = [u_ref[m] for m in range(TILES)]
    p, kappa = image_of(got_ref, h_ref, u, u_ref[SCALE, 0:1, 0:1])
    read_hist.wait()
    per = TILES * 8
    for m in range(TILES):
        n = (PANEL_COLUMNS - 1) * per + 8 * m
        hist[0, n : n + 8, :] = u[m]
        hist[1, n : n + 8, :] = p[m] - kappa * u[m]
    for side, n in ((0, own[1]), (1, own[2])):
        z, m0 = n // 2, 6 * (n % 2)
        for t in range(6):
            for half in range(2):
                rows = pl.ds(half * 8 * per + 8 * (m0 + t) + z, 8, stride=per)
                for k in range(2):
                    at = 16 * k + 8 * half
                    sides[side, at : at + 8, LANES * t : LANES * (t + 1)] = hist[k ^ side, rows, :]

    def pieces(x):
        high = x.astype(jnp.bfloat16)
        rest = x - high.astype(jnp.float32)
        mid = rest.astype(jnp.bfloat16)
        return high, mid, (rest - mid.astype(jnp.float32)).astype(jnp.bfloat16)

    lh, lm, ll = pieces(sides[0].T)
    rh, rm, rl = pieces(sides[1])
    left = jnp.concatenate([lh, lh, lm, lm, lh, ll], axis=1)
    right = jnp.concatenate([rh, rm, rh, rm, rl, rh], axis=0)
    read_block.wait()
    writes = []
    step = 256
    for n in range(block.shape[0] // step):
        rows = slice(step * n, step * (n + 1))
        block[rows, :] = block[rows, :] - jnp.dot(left[rows, :], right, preferred_element_type=jnp.float32)
        writes.append(pltpu.make_async_copy(block.at[rows, :], updated_ref.at[rows, :], sems.at[2 + n]))
        writes[-1].start()
    for half in range(2):
        for m in range(TILES):
            for z in range(8):
                s = TILES * z + m
                rows = pl.ds(half * 8 * per + 8 * m + z, 8, stride=per)
                whole[8 * half : 8 * half + 8, LANES * s : LANES * (s + 1)] = hist[0, rows, :]
    write = pltpu.make_async_copy(whole, whole_ref, sems.at[5])
    write.start()
    for w in writes:
        w.wait()
    write.wait()


def per_device(matrix):
    f32 = jnp.float32
    r, c = lax.axis_index("row"), lax.axis_index("col")
    ways = lax.axis_size("col")
    devices = ways * lax.axis_size("row")
    tile_cols = matrix.shape[1]
    own = jnp.stack([(OWN * (r * ways + c)) & (LANES - 1), r, c])
    rows = lax.all_to_all(
        matrix.reshape(ways, OWN, tile_cols), "col", split_axis=0, concat_axis=0, tiled=True
    )

    def exchange(packed):
        return lax.all_to_all(packed, ("row", "col"), split_axis=0, concat_axis=0, tiled=True)

    def shape(*dims):
        return jax.ShapeDtypeStruct(dims, f32)

    vec, ext, packed = shape(TILES, 8, LANES), shape(TILES + 2, 8, LANES), shape(devices, LANES)
    hist = shape(2, PANEL_COLUMNS, TILES, 8, LANES)
    order = TILES * 8 * LANES
    first = pl.pallas_call(first_body, out_shape=packed, in_specs=[SMEM, VMEM], out_specs=VMEM, name="first")
    step = pl.pallas_call(
        step_body,
        out_shape=(vec, ext, packed),
        in_specs=[SMEM] * 2 + [VMEM] * 5,
        out_specs=(VMEM,) * 3,
        scratch_shapes=[pltpu.VMEM((order // LANES, LANES), f32)],
        name="step",
    )
    history = pl.pallas_call(
        history_body,
        out_shape=(vec, vec, hist),
        in_specs=[SMEM] + [VMEM] * 4 + [ANY],
        out_specs=(VMEM, VMEM, ANY),
        input_output_aliases={5: 2},
        scratch_shapes=[pltpu.VMEM(hist.shape, f32), pltpu.SemaphoreType.DMA((3,))],
        name="history",
    )
    last = pl.pallas_call(
        last_body,
        out_shape=(shape(*matrix.shape), shape(PANEL_COLUMNS, order)),
        in_specs=[SMEM] + [VMEM] * 3 + [ANY] * 2,
        out_specs=(ANY, ANY),
        scratch_shapes=[
            pltpu.VMEM((2, PANEL_COLUMNS * TILES * 8, LANES), f32),
            pltpu.VMEM(matrix.shape, f32),
            pltpu.VMEM((PANEL_COLUMNS, order), f32),
            pltpu.VMEM((2, 2 * PANEL_COLUMNS, tile_cols), f32),
            pltpu.SemaphoreType.DMA((6,)),
        ],
        name="last",
    )

    def one_column(j, state):
        got, base, h, u, kept = state
        col = jnp.reshape(j, (1,))
        w, un, out = step(col, own, got, base, h, u, rows)
        got_next = exchange(out)
        base, h, kept = history(col, got, w, u, un, kept)
        return got_next, base, h, un, kept

    def zeros(s):
        return jnp.zeros(s.shape, f32)

    u = jnp.concatenate([zeros(vec), jnp.full((1, 8, LANES), -1.0, f32), jnp.zeros((1, 8, LANES), f32)])
    state = (exchange(first(own, rows)), zeros(vec), zeros(vec), u, zeros(hist))
    got, _, h, u, kept = lax.fori_loop(0, PANEL_COLUMNS, one_column, state)
    updated, whole = last(own, got, h, u, kept.reshape(2, -1, LANES), matrix)
    return updated, whole, u[COEF, :2, :PANEL_COLUMNS]


def solution(mesh):
    return jax.shard_map(
        per_device,
        mesh=mesh,
        in_specs=(P("row", "col"),),
        out_specs=(P("row", "col"), P(), P()),
        check_vma=False,
    )
```

time: 626 us -> 409 us (0.65)
  matrix products: 118 us -> 0 us
  Pallas kernels: 0 us -> 82.6 us
  local copies, waits for them, and re-layouts: 69.4 us -> 2.22 us
  waiting for transfers between devices: 159 us -> 210 us
  other arithmetic: 48.4 us -> 0.08 us
  blocking collectives: 48.1 us -> 0 us
  loops' own time: 44.1 us -> 0.82 us
  starting transfers between devices: 134 us -> 111 us
    dot_general x113 -> x0, matrix products: 118 us -> none  [the longest x16 58.7 us: single_column(): jnp.dot(matrix, reflector_cols, precision=HIGH)]
    pallas_call x0 -> x34, Pallas kernels: none -> 82.6 us  [the longest x16 47.8 us: one_column(): base, h, kept = history(col, got, w, u, un, kept)]
    all_to_all x32 -> x18, waiting for transfers between devices: 159 us -> 210 us  [the longest x17 175 us: exchange(): lax.all_to_all(packed, ('row', 'col'), split_axis=0, concat_axis=0, tiled...]
    all_gather x2 -> x0, blocking collectives: 48.1 us -> none  [the longest x1 27.8 us: per_device(): whole_panel = lax.all_gather(panel, 'row', axis=1, tiled=True)]
    another operation x1, loops' own time: 44.1 us -> 0.82 us  [per_device(): got, _, h, u, kept = lax.fori_loop(0, PANEL_COLUMNS, one_column, state)]
    scatter x32 -> x0, local copies, waits for them, and re-layouts: 28.9 us -> none  [the longest x16 14.5 us: single_column(): reflectors = reflectors.at[step].set(reflector)]
    another operation x33 -> x1, other arithmetic: 24.4 us -> 0.08 us  [per_device(): own = jnp.stack([OWN * (r * ways + c) & LANES - 1, r, c])]
    all_to_all x32 -> x18, starting transfers between devices: 134 us -> 111 us  [the longest x17 103 us: exchange(): lax.all_to_all(packed, ('row', 'col'), split_axis=0, concat_axis=0, tiled...]
  transfers between devices with their start and end apart: 32 -> 18, of which waited for: 32 -> 18; matrix products, arithmetic and copies ran while one was open for 8% -> 0% of each run, Pallas kernels for 0% -> 12%
where the time goes in v1:
time: 409 us; the launch traced here: 407 us
  waiting for transfers between devices  210 us (51%)
  starting transfers between devices  111 us (27%)
  Pallas kernels  82.6 us (20%)
    all_to_all x17, waiting for transfers between devices, exchange(): lax.all_to_all(packed, ('row', 'col'), split_axis=0, concat_axis=0, tiled...  175 us
    all_to_all x17, starting transfers between devices, exchange(): lax.all_to_all(packed, ('row', 'col'), split_axis=0, concat_axis=0, tiled...  103 us
    pallas_call x16, Pallas kernels, one_column(): base, h, kept = history(col, got, w, u, un, kept)  47.8 us
    all_to_all x1, waiting for transfers between devices, per_device(): lax.all_to_all(matrix.reshape(ways, OWN, tile_cols), 'col', split_axis=0,...  34.8 us
    pallas_call x16, Pallas kernels, one_column(): w, un, out = step(col, own, got, base, h, u, rows)  28.7 us
  transfers between devices with their start and end apart: 18, of which 18 were waited for; matrix products, arithmetic and copies ran while one was open for 0% of the time, Pallas kernels for 12%

profile of v1, /device:TPU:1, one launch (start us, length us, event | category | flops | bytes accessed | tf_op | source)
XLA Modules:
  0.0 406.6 jit_solution(12778570755065898368)
XLA Ops:
  0.6 7.6 %all-to-all-start.1 = ((f32[16,48,768]{2,1,0:T(8,128)}), f32[16,48,768]{2,1,0:T(8,128)S(1)}, u32[]{:S(2)}, u32[]{:S(2)}) async-start(f32[16,48,768]{2,1,0:T(8,128)} %bitcast.25), calls=%async_computation.1 | async-start | bytes 4718592 | tf_op jit(solution)/shard_map/all_to_all | solution.py:209
  8.3 34.8 %all-to-all-done.1.rows_ref = f32[16,48,768]{2,1,0:T(8,128)S(1)} async-done(((f32[16,48,768]{2,1,0:T(8,128)}), f32[16,48,768]{2,1,0:T(8,128)S(1)}, u32[]{:S(2)}, u32[]{:S(2)}) %all-to-all-start.1) | async-done | bytes 2359328 | tf_op jit(solution)/shard_map/all_to_all | solution.py:209
  44.4 12.5 %all-to-all-start.2 = ((f32[256,1,128]{2,1,0:T(1,128)}), f32[256,1,128]{2,1,0:T(1,128)S(1)}, u32[]{:S(2)}, u32[]{:S(2)}) async-start(f32[256,1,128]{2,1,0:T(1,128)} %bitcast.27), calls=%async_computation.2 | async-start | bytes 262144 | tf_op jit(solution)/shard_map/all_to_all | solution.py:214
  56.9 13.0 %all-to-all-done.2 = f32[256,1,128]{2,1,0:T(1,128)S(1)} async-done(((f32[256,1,128]{2,1,0:T(1,128)}), f32[256,1,128]{2,1,0:T(1,128)S(1)}, u32[]{:S(2)}, u32[]{:S(2)}) %all-to-all-start.2) | async-done | bytes 131104 | tf_op jit(solution)/shard_map/all_to_all | solution.py:214
  71.3 330.1 %while.21 = (s32[]{:T(128)}, f32[256,128]{1,0:T(8,128)S(1)}, f32[12,8,128]{2,1,0:T(8,128)S(1)}, f32[12,8,128]{2,1,0:T(8,128)S(1)}, f32[14,8,128]{2,1,0:T(8,128)S...) while((s32[]{:T(128)}, f32[256,128]{1,0:T(8,128)S(1)}, ...), condition=%wide.region_1.0_spmd, body=%wide.region_0.0_spmd.sunk | while | flops 2 | bytes 999585 | solution.py:268
  73.0 5.7 %all-to-all-start = ((f32[256,1,128]{2,1,0:T(1,128)}), f32[256,1,128]{2,1,0:T(1,128)S(1)}, u32[]{:S(2)}, u32[]{:S(2)}) async-start(f32[256,1,128]{2,1,0:T(1,128)} %bitcast.26), calls=%async_computation | async-start | bytes 262144 | tf_op jit(solution)/shard_map/while/body/eval_jaxpr/all_to_all | solution.py:214
  81.7 10.1 %all-to-all-done = f32[256,1,128]{2,1,0:T(1,128)S(1)} async-done(((f32[256,1,128]{2,1,0:T(1,128)}), f32[256,1,128]{2,1,0:T(1,128)S(1)}, u32[]{:S(2)}, u32[]{:S(2)}) %all-to-all-start) | async-done | bytes 131104 | tf_op jit(solution)/shard_map/while/body/eval_jaxpr/all_to_all | solution.py:214
  93.7 5.7 %all-to-all-start = ((f32[256,1,128]{2,1,0:T(1,128)}), f32[256,1,128]{2,1,0:T(1,128)S(1)}, u32[]{:S(2)}, u32[]{:S(2)}) async-start(f32[256,1,128]{2,1,0:T(1,128)} %bitcast.26), calls=%async_computation | async-start | bytes 262144 | tf_op jit(solution)/shard_map/while/body/eval_jaxpr/all_to_all | solution.py:214
  102.4 10.1 %all-to-all-done = f32[256,1,128]{2,1,0:T(1,128)S(1)} async-done(((f32[256,1,128]{2,1,0:T(1,128)}), f32[256,1,128]{2,1,0:T(1,128)S(1)}, u32[]{:S(2)}, u32[]{:S(2)}) %all-to-all-start) | async-done | bytes 131104 | tf_op jit(solution)/shard_map/while/body/eval_jaxpr/all_to_all | solution.py:214
  114.3 5.7 %all-to-all-start = ((f32[256,1,128]{2,1,0:T(1,128)}), f32[256,1,128]{2,1,0:T(1,128)S(1)}, u32[]{:S(2)}, u32[]{:S(2)}) async-start(f32[256,1,128]{2,1,0:T(1,128)} %bitcast.26), calls=%async_computation | async-start | bytes 262144 | tf_op jit(solution)/shard_map/while/body/eval_jaxpr/all_to_all | solution.py:214
  123.0 10.1 %all-to-all-done = f32[256,1,128]{2,1,0:T(1,128)S(1)} async-done(((f32[256,1,128]{2,1,0:T(1,128)}), f32[256,1,128]{2,1,0:T(1,128)S(1)}, u32[]{:S(2)}, u32[]{:S(2)}) %all-to-all-start) | async-done | bytes 131104 | tf_op jit(solution)/shard_map/while/body/eval_jaxpr/all_to_all | solution.py:214
  134.9 5.7 %all-to-all-start = ((f32[256,1,128]{2,1,0:T(1,128)}), f32[256,1,128]{2,1,0:T(1,128)S(1)}, u32[]{:S(2)}, u32[]{:S(2)}) async-start(f32[256,1,128]{2,1,0:T(1,128)} %bitcast.26), calls=%async_computation | async-start | bytes 262144 | tf_op jit(solution)/shard_map/while/body/eval_jaxpr/all_to_all | solution.py:214
  143.6 10.1 %all-to-all-done = f32[256,1,128]{2,1,0:T(1,128)S(1)} async-done(((f32[256,1,128]{2,1,0:T(1,128)}), f32[256,1,128]{2,1,0:T(1,128)S(1)}, u32[]{:S(2)}, u32[]{:S(2)}) %all-to-all-start) | async-done | bytes 131104 | tf_op jit(solution)/shard_map/while/body/eval_jaxpr/all_to_all | solution.py:214
  155.6 5.7 %all-to-all-start = ((f32[256,1,128]{2,1,0:T(1,128)}), f32[256,1,128]{2,1,0:T(1,128)S(1)}, u32[]{:S(2)}, u32[]{:S(2)}) async-start(f32[256,1,128]{2,1,0:T(1,128)} %bitcast.26), calls=%async_computation | async-start | bytes 262144 | tf_op jit(solution)/shard_map/while/body/eval_jaxpr/all_to_all | solution.py:214
  164.3 10.1 %all-to-all-done = f32[256,1,128]{2,1,0:T(1,128)S(1)} async-done(((f32[256,1,128]{2,1,0:T(1,128)}), f32[256,1,128]{2,1,0:T(1,128)S(1)}, u32[]{:S(2)}, u32[]{:S(2)}) %all-to-all-start) | async-done | bytes 131104 | tf_op jit(solution)/shard_map/while/body/eval_jaxpr/all_to_all | solution.py:214
  176.2 5.7 %all-to-all-start = ((f32[256,1,128]{2,1,0:T(1,128)}), f32[256,1,128]{2,1,0:T(1,128)S(1)}, u32[]{:S(2)}, u32[]{:S(2)}) async-start(f32[256,1,128]{2,1,0:T(1,128)} %bitcast.26), calls=%async_computation | async-start | bytes 262144 | tf_op jit(solution)/shard_map/while/body/eval_jaxpr/all_to_all | solution.py:214
  184.9 10.1 %all-to-all-done = f32[256,1,128]{2,1,0:T(1,128)S(1)} async-done(((f32[256,1,128]{2,1,0:T(1,128)}), f32[256,1,128]{2,1,0:T(1,128)S(1)}, u32[]{:S(2)}, u32[]{:S(2)}) %all-to-all-start) | async-done | bytes 131104 | tf_op jit(solution)/shard_map/while/body/eval_jaxpr/all_to_all | solution.py:214
  196.8 5.7 %all-to-all-start = ((f32[256,1,128]{2,1,0:T(1,128)}), f32[256,1,128]{2,1,0:T(1,128)S(1)}, u32[]{:S(2)}, u32[]{:S(2)}) async-start(f32[256,1,128]{2,1,0:T(1,128)} %bitcast.26), calls=%async_computation | async-start | bytes 262144 | tf_op jit(solution)/shard_map/while/body/eval_jaxpr/all_to_all | solution.py:214
  205.5 10.1 %all-to-all-done = f32[256,1,128]{2,1,0:T(1,128)S(1)} async-done(((f32[256,1,128]{2,1,0:T(1,128)}), f32[256,1,128]{2,1,0:T(1,128)S(1)}, u32[]{:S(2)}, u32[]{:S(2)}) %all-to-all-start) | async-done | bytes 131104 | tf_op jit(solution)/shard_map/while/body/eval_jaxpr/all_to_all | solution.py:214
  226.2 10.1 %all-to-all-done = f32[256,1,128]{2,1,0:T(1,128)S(1)} async-done(((f32[256,1,128]{2,1,0:T(1,128)}), f32[256,1,128]{2,1,0:T(1,128)S(1)}, u32[]{:S(2)}, u32[]{:S(2)}) %all-to-all-start) | async-done | bytes 131104 | tf_op jit(solution)/shard_map/while/body/eval_jaxpr/all_to_all | solution.py:214
  238.1 5.7 %all-to-all-start = ((f32[256,1,128]{2,1,0:T(1,128)}), f32[256,1,128]{2,1,0:T(1,128)S(1)}, u32[]{:S(2)}, u32[]{:S(2)}) async-start(f32[256,1,128]{2,1,0:T(1,128)} %bitcast.26), calls=%async_computation | async-start | bytes 262144 | tf_op jit(solution)/shard_map/while/body/eval_jaxpr/all_to_all | solution.py:214
  246.8 10.1 %all-to-all-done = f32[256,1,128]{2,1,0:T(1,128)S(1)} async-done(((f32[256,1,128]{2,1,0:T(1,128)}), f32[256,1,128]{2,1,0:T(1,128)S(1)}, u32[]{:S(2)}, u32[]{:S(2)}) %all-to-all-start) | async-done | bytes 131104 | tf_op jit(solution)/shard_map/while/body/eval_jaxpr/all_to_all | solution.py:214
  258.7 5.7 %all-to-all-start = ((f32[256,1,128]{2,1,0:T(1,128)}), f32[256,1,128]{2,1,0:T(1,128)S(1)}, u32[]{:S(2)}, u32[]{:S(2)}) async-start(f32[256,1,128]{2,1,0:T(1,128)} %bitcast.26), calls=%async_computation | async-start | bytes 262144 | tf_op jit(solution)/shard_map/while/body/eval_jaxpr/all_to_all | solution.py:214
  267.4 10.1 %all-to-all-done = f32[256,1,128]{2,1,0:T(1,128)S(1)} async-done(((f32[256,1,128]{2,1,0:T(1,128)}), f32[256,1,128]{2,1,0:T(1,128)S(1)}, u32[]{:S(2)}, u32[]{:S(2)}) %all-to-all-start) | async-done | bytes 131104 | tf_op jit(solution)/shard_map/while/body/eval_jaxpr/all_to_all | solution.py:214
  288.0 10.1 %all-to-all-done = f32[256,1,128]{2,1,0:T(1,128)S(1)} async-done(((f32[256,1,128]{2,1,0:T(1,128)}), f32[256,1,128]{2,1,0:T(1,128)S(1)}, u32[]{:S(2)}, u32[]{:S(2)}) %all-to-all-start) | async-done | bytes 131104 | tf_op jit(solution)/shard_map/while/body/eval_jaxpr/all_to_all | solution.py:214
  300.0 5.7 %all-to-all-start = ((f32[256,1,128]{2,1,0:T(1,128)}), f32[256,1,128]{2,1,0:T(1,128)S(1)}, u32[]{:S(2)}, u32[]{:S(2)}) async-start(f32[256,1,128]{2,1,0:T(1,128)} %bitcast.26), calls=%async_computation | async-start | bytes 262144 | tf_op jit(solution)/shard_map/while/body/eval_jaxpr/all_to_all | solution.py:214
  308.7 10.1 %all-to-all-done = f32[256,1,128]{2,1,0:T(1,128)S(1)} async-done(((f32[256,1,128]{2,1,0:T(1,128)}), f32[256,1,128]{2,1,0:T(1,128)S(1)}, u32[]{:S(2)}, u32[]{:S(2)}) %all-to-all-start) | async-done | bytes 131104 | tf_op jit(solution)/shard_map/while/body/eval_jaxpr/all_to_all | solution.py:214
  329.3 10.1 %all-to-all-done = f32[256,1,128]{2,1,0:T(1,128)S(1)} async-done(((f32[256,1,128]{2,1,0:T(1,128)}), f32[256,1,128]{2,1,0:T(1,128)S(1)}, u32[]{:S(2)}, u32[]{:S(2)}) %all-to-all-start) | async-done | bytes 131104 | tf_op jit(solution)/shard_map/while/body/eval_jaxpr/all_to_all | solution.py:214
  349.9 10.1 %all-to-all-done = f32[256,1,128]{2,1,0:T(1,128)S(1)} async-done(((f32[256,1,128]{2,1,0:T(1,128)}), f32[256,1,128]{2,1,0:T(1,128)S(1)}, u32[]{:S(2)}, u32[]{:S(2)}) %all-to-all-start) | async-done | bytes 131104 | tf_op jit(solution)/shard_map/while/body/eval_jaxpr/all_to_all | solution.py:214
  361.9 5.7 %all-to-all-start = ((f32[256,1,128]{2,1,0:T(1,128)}), f32[256,1,128]{2,1,0:T(1,128)S(1)}, u32[]{:S(2)}, u32[]{:S(2)}) async-start(f32[256,1,128]{2,1,0:T(1,128)} %bitcast.26), calls=%async_computation | async-start | bytes 262144 | tf_op jit(solution)/shard_map/while/body/eval_jaxpr/all_to_all | solution.py:214
  370.6 10.1 %all-to-all-done = f32[256,1,128]{2,1,0:T(1,128)S(1)} async-done(((f32[256,1,128]{2,1,0:T(1,128)}), f32[256,1,128]{2,1,0:T(1,128)S(1)}, u32[]{:S(2)}, u32[]{:S(2)}) %all-to-all-start) | async-done | bytes 131104 | tf_op jit(solution)/shard_map/while/body/eval_jaxpr/all_to_all | solution.py:214
  391.2 10.1 %all-to-all-done = f32[256,1,128]{2,1,0:T(1,128)S(1)} async-done(((f32[256,1,128]{2,1,0:T(1,128)}), f32[256,1,128]{2,1,0:T(1,128)S(1)}, u32[]{:S(2)}, u32[]{:S(2)}) %all-to-all-start) | async-done | bytes 131104 | tf_op jit(solution)/shard_map/while/body/eval_jaxpr/all_to_all | solution.py:214
  (110 shorter events, 113.2 us)
Async XLA Ops:
  0.6 42.5 %all-to-all-start.1 = ((f32[16,48,768]{2,1,0:T(8,128)}), f32[16,48,768]{2,1,0:T(8,128)S(1)}, u32[]{:S(2)}, u32[]{:S(2)}) async-start(f32[16,48,768]{2,1,0:T(8,128)} %bitcast.25), calls=%async_computation.1 | async-start | bytes 4718592 | tf_op jit(solution)/shard_map/all_to_all | solution.py:209
  44.4 26.8 %copy-start = (f32[14,8,128]{2,1,0:T(8,128)S(1)}, f32[14,8,128]{2,1,0:T(8,128)}, u32[]{:S(2)}) copy-start(f32[14,8,128]{2,1,0:T(8,128)} %constant.29.clone.1) | copy-start | bytes 172036
  44.4 25.5 %all-to-all-start.2 = ((f32[256,1,128]{2,1,0:T(1,128)}), f32[256,1,128]{2,1,0:T(1,128)S(1)}, u32[]{:S(2)}, u32[]{:S(2)}) async-start(f32[256,1,128]{2,1,0:T(1,128)} %bitcast.27), calls=%async_computation.2 | async-start | bytes 262144 | tf_op jit(solution)/shard_map/all_to_all | solution.py:214
  73.0 8.7 %copy-start.1 = (f32[14,8,128]{2,1,0:T(8,128)S(1)}, f32[14,8,128]{2,1,0:T(8,128)}, u32[]{:S(2)}) copy-start(f32[14,8,128]{2,1,0:T(8,128)} %get-tuple-element.247.un_ref) | copy-start | bytes 172036 | tf_op jit(solution)/shard_map/while
  73.0 18.8 %all-to-all-start = ((f32[256,1,128]{2,1,0:T(1,128)}), f32[256,1,128]{2,1,0:T(1,128)S(1)}, u32[]{:S(2)}, u32[]{:S(2)}) async-start(f32[256,1,128]{2,1,0:T(1,128)} %bitcast.26), calls=%async_computation | async-start | bytes 262144 | tf_op jit(solution)/shard_map/while/body/eval_jaxpr/all_to_all | solution.py:214
  93.7 8.7 %copy-start.1 = (f32[14,8,128]{2,1,0:T(8,128)S(1)}, f32[14,8,128]{2,1,0:T(8,128)}, u32[]{:S(2)}) copy-start(f32[14,8,128]{2,1,0:T(8,128)} %get-tuple-element.247.un_ref) | copy-start | bytes 172036 | tf_op jit(solution)/shard_map/while
  93.7 18.8 %all-to-all-start = ((f32[256,1,128]{2,1,0:T(1,128)}), f32[256,1,128]{2,1,0:T(1,128)S(1)}, u32[]{:S(2)}, u32[]{:S(2)}) async-start(f32[256,1,128]{2,1,0:T(1,128)} %bitcast.26), calls=%async_computation | async-start | bytes 262144 | tf_op jit(solution)/shard_map/while/body/eval_jaxpr/all_to_all | solution.py:214
  114.3 18.8 %all-to-all-start = ((f32[256,1,128]{2,1,0:T(1,128)}), f32[256,1,128]{2,1,0:T(1,128)S(1)}, u32[]{:S(2)}, u32[]{:S(2)}) async-start(f32[256,1,128]{2,1,0:T(1,128)} %bitcast.26), calls=%async_computation | async-start | bytes 262144 | tf_op jit(solution)/shard_map/while/body/eval_jaxpr/all_to_all | solution.py:214
  134.9 8.7 %copy-start.1 = (f32[14,8,128]{2,1,0:T(8,128)S(1)}, f32[14,8,128]{2,1,0:T(8,128)}, u32[]{:S(2)}) copy-start(f32[14,8,128]{2,1,0:T(8,128)} %get-tuple-element.247.un_ref) | copy-start | bytes 172036 | tf_op jit(solution)/shard_map/while
  134.9 18.8 %all-to-all-start = ((f32[256,1,128]{2,1,0:T(1,128)}), f32[256,1,128]{2,1,0:T(1,128)S(1)}, u32[]{:S(2)}, u32[]{:S(2)}) async-start(f32[256,1,128]{2,1,0:T(1,128)} %bitcast.26), calls=%async_computation | async-start | bytes 262144 | tf_op jit(solution)/shard_map/while/body/eval_jaxpr/all_to_all | solution.py:214
  155.6 8.7 %copy-start.1 = (f32[14,8,128]{2,1,0:T(8,128)S(1)}, f32[14,8,128]{2,1,0:T(8,128)}, u32[]{:S(2)}) copy-start(f32[14,8,128]{2,1,0:T(8,128)} %get-tuple-element.247.un_ref) | copy-start | bytes 172036 | tf_op jit(solution)/shard_map/while
  155.6 18.8 %all-to-all-start = ((f32[256,1,128]{2,1,0:T(1,128)}), f32[256,1,128]{2,1,0:T(1,128)S(1)}, u32[]{:S(2)}, u32[]{:S(2)}) async-start(f32[256,1,128]{2,1,0:T(1,128)} %bitcast.26), calls=%async_computation | async-start | bytes 262144 | tf_op jit(solution)/shard_map/while/body/eval_jaxpr/all_to_all | solution.py:214
  176.2 8.7 %copy-start.1 = (f32[14,8,128]{2,1,0:T(8,128)S(1)}, f32[14,8,128]{2,1,0:T(8,128)}, u32[]{:S(2)}) copy-start(f32[14,8,128]{2,1,0:T(8,128)} %get-tuple-element.247.un_ref) | copy-start | bytes 172036 | tf_op jit(solution)/shard_map/while
  176.2 18.8 %all-to-all-start = ((f32[256,1,128]{2,1,0:T(1,128)}), f32[256,1,128]{2,1,0:T(1,128)S(1)}, u32[]{:S(2)}, u32[]{:S(2)}) async-start(f32[256,1,128]{2,1,0:T(1,128)} %bitcast.26), calls=%async_computation | async-start | bytes 262144 | tf_op jit(solution)/shard_map/while/body/eval_jaxpr/all_to_all | solution.py:214
  196.8 8.7 %copy-start.1 = (f32[14,8,128]{2,1,0:T(8,128)S(1)}, f32[14,8,128]{2,1,0:T(8,128)}, u32[]{:S(2)}) copy-start(f32[14,8,128]{2,1,0:T(8,128)} %get-tuple-element.247.un_ref) | copy-start | bytes 172036 | tf_op jit(solution)/shard_map/while
  196.8 18.8 %all-to-all-start = ((f32[256,1,128]{2,1,0:T(1,128)}), f32[256,1,128]{2,1,0:T(1,128)S(1)}, u32[]{:S(2)}, u32[]{:S(2)}) async-start(f32[256,1,128]{2,1,0:T(1,128)} %bitcast.26), calls=%async_computation | async-start | bytes 262144 | tf_op jit(solution)/shard_map/while/body/eval_jaxpr/all_to_all | solution.py:214
  217.5 8.7 %copy-start.1 = (f32[14,8,128]{2,1,0:T(8,128)S(1)}, f32[14,8,128]{2,1,0:T(8,128)}, u32[]{:S(2)}) copy-start(f32[14,8,128]{2,1,0:T(8,128)} %get-tuple-element.247.un_ref) | copy-start | bytes 172036 | tf_op jit(solution)/shard_map/while
  217.5 18.8 %all-to-all-start = ((f32[256,1,128]{2,1,0:T(1,128)}), f32[256,1,128]{2,1,0:T(1,128)S(1)}, u32[]{:S(2)}, u32[]{:S(2)}) async-start(f32[256,1,128]{2,1,0:T(1,128)} %bitcast.26), calls=%async_computation | async-start | bytes 262144 | tf_op jit(solution)/shard_map/while/body/eval_jaxpr/all_to_all | solution.py:214
  238.1 8.7 %copy-start.1 = (f32[14,8,128]{2,1,0:T(8,128)S(1)}, f32[14,8,128]{2,1,0:T(8,128)}, u32[]{:S(2)}) copy-start(f32[14,8,128]{2,1,0:T(8,128)} %get-tuple-element.247.un_ref) | copy-start | bytes 172036 | tf_op jit(solution)/shard_map/while
  238.1 18.8 %all-to-all-start = ((f32[256,1,128]{2,1,0:T(1,128)}), f32[256,1,128]{2,1,0:T(1,128)S(1)}, u32[]{:S(2)}, u32[]{:S(2)}) async-start(f32[256,1,128]{2,1,0:T(1,128)} %bitcast.26), calls=%async_computation | async-start | bytes 262144 | tf_op jit(solution)/shard_map/while/body/eval_jaxpr/all_to_all | solution.py:214
  258.7 8.7 %copy-start.1 = (f32[14,8,128]{2,1,0:T(8,128)S(1)}, f32[14,8,128]{2,1,0:T(8,128)}, u32[]{:S(2)}) copy-start(f32[14,8,128]{2,1,0:T(8,128)} %get-tuple-element.247.un_ref) | copy-start | bytes 172036 | tf_op jit(solution)/shard_map/while
  258.7 18.8 %all-to-all-start = ((f32[256,1,128]{2,1,0:T(1,128)}), f32[256,1,128]{2,1,0:T(1,128)S(1)}, u32[]{:S(2)}, u32[]{:S(2)}) async-start(f32[256,1,128]{2,1,0:T(1,128)} %bitcast.26), calls=%async_computation | async-start | bytes 262144 | tf_op jit(solution)/shard_map/while/body/eval_jaxpr/all_to_all | solution.py:214
  279.4 18.8 %all-to-all-start = ((f32[256,1,128]{2,1,0:T(1,128)}), f32[256,1,128]{2,1,0:T(1,128)S(1)}, u32[]{:S(2)}, u32[]{:S(2)}) async-start(f32[256,1,128]{2,1,0:T(1,128)} %bitcast.26), calls=%async_computation | async-start | bytes 262144 | tf_op jit(solution)/shard_map/while/body/eval_jaxpr/all_to_all | solution.py:214
  300.0 8.7 %copy-start.1 = (f32[14,8,128]{2,1,0:T(8,128)S(1)}, f32[14,8,128]{2,1,0:T(8,128)}, u32[]{:S(2)}) copy-start(f32[14,8,128]{2,1,0:T(8,128)} %get-tuple-element.247.un_ref) | copy-start | bytes 172036 | tf_op jit(solution)/shard_map/while
  300.0 18.8 %all-to-all-start = ((f32[256,1,128]{2,1,0:T(1,128)}), f32[256,1,128]{2,1,0:T(1,128)S(1)}, u32[]{:S(2)}, u32[]{:S(2)}) async-start(f32[256,1,128]{2,1,0:T(1,128)} %bitcast.26), calls=%async_computation | async-start | bytes 262144 | tf_op jit(solution)/shard_map/while/body/eval_jaxpr/all_to_all | solution.py:214
  320.6 8.7 %copy-start.1 = (f32[14,8,128]{2,1,0:T(8,128)S(1)}, f32[14,8,128]{2,1,0:T(8,128)}, u32[]{:S(2)}) copy-start(f32[14,8,128]{2,1,0:T(8,128)} %get-tuple-element.247.un_ref) | copy-start | bytes 172036 | tf_op jit(solution)/shard_map/while
  320.6 18.8 %all-to-all-start = ((f32[256,1,128]{2,1,0:T(1,128)}), f32[256,1,128]{2,1,0:T(1,128)S(1)}, u32[]{:S(2)}, u32[]{:S(2)}) async-start(f32[256,1,128]{2,1,0:T(1,128)} %bitcast.26), calls=%async_computation | async-start | bytes 262144 | tf_op jit(solution)/shard_map/while/body/eval_jaxpr/all_to_all | solution.py:214
  341.2 8.7 %copy-start.1 = (f32[14,8,128]{2,1,0:T(8,128)S(1)}, f32[14,8,128]{2,1,0:T(8,128)}, u32[]{:S(2)}) copy-start(f32[14,8,128]{2,1,0:T(8,128)} %get-tuple-element.247.un_ref) | copy-start | bytes 172036 | tf_op jit(solution)/shard_map/while
  341.3 18.8 %all-to-all-start = ((f32[256,1,128]{2,1,0:T(1,128)}), f32[256,1,128]{2,1,0:T(1,128)S(1)}, u32[]{:S(2)}, u32[]{:S(2)}) async-start(f32[256,1,128]{2,1,0:T(1,128)} %bitcast.26), calls=%async_computation | async-start | bytes 262144 | tf_op jit(solution)/shard_map/while/body/eval_jaxpr/all_to_all | solution.py:214
  361.9 18.8 %all-to-all-start = ((f32[256,1,128]{2,1,0:T(1,128)}), f32[256,1,128]{2,1,0:T(1,128)S(1)}, u32[]{:S(2)}, u32[]{:S(2)}) async-start(f32[256,1,128]{2,1,0:T(1,128)} %bitcast.26), calls=%async_computation | async-start | bytes 262144 | tf_op jit(solution)/shard_map/while/body/eval_jaxpr/all_to_all | solution.py:214
  382.5 8.7 %copy-start.1 = (f32[14,8,128]{2,1,0:T(8,128)S(1)}, f32[14,8,128]{2,1,0:T(8,128)}, u32[]{:S(2)}) copy-start(f32[14,8,128]{2,1,0:T(8,128)} %get-tuple-element.247.un_ref) | copy-start | bytes 172036 | tf_op jit(solution)/shard_map/while
  382.5 18.8 %all-to-all-start = ((f32[256,1,128]{2,1,0:T(1,128)}), f32[256,1,128]{2,1,0:T(1,128)S(1)}, u32[]{:S(2)}, u32[]{:S(2)}) async-start(f32[256,1,128]{2,1,0:T(1,128)} %bitcast.26), calls=%async_computation | async-start | bytes 262144 | tf_op jit(solution)/shard_map/while/body/eval_jaxpr/all_to_all | solution.py:214
  (3 other events, 26.0 us)

commit v2 on v1

--- a/solution.py
+++ b/solution.py
@@ -46,12 +46,8 @@
     return (iota((8, LANES), 0) * TILES + m) * LANES + iota((8, LANES), 1)
 
 
-def message(first, second, offset):
-    row, lane = iota((OWN, LANES), 0), iota((OWN, LANES), 1)
-    here = (row + offset) & (LANES - 1)
-    there = (row + offset + OWN) & (LANES - 1)
-    picked = jnp.where(lane == here, first, 0.0) + jnp.where(lane == there, second, 0.0)
-    return jnp.sum(picked, axis=0, keepdims=True)
+def message(first, second, slots_ref):
+    return jnp.sum(slots_ref[0] * first + slots_ref[1] * second, axis=0, keepdims=True)
 
 
 def own_column(rows_ref, k):
@@ -59,10 +55,23 @@
     return jnp.sum(jnp.where(iota((OWN, LANES), 1) == k, head, 0.0), axis=1, keepdims=True)
 
 
-def first_body(own, rows_ref, out_ref):
-    out_ref[...] = jnp.broadcast_to(
-        message(own_column(rows_ref, 0), own_column(rows_ref, 1), own[0]), out_ref.shape
-    )
+def begin_body(top_ref, out_ref, tmp):
+    lane = iota((8, LANES), 1)
+    for t in range(6):
+        tmp[32 * t : 32 * (t + 1), :] = top_ref[:, LANES * t : LANES * (t + 1)]
+
+    def tile(k, m):
+        half, t = divmod(m, 6)
+        return tmp[pl.ds(32 * t + 2 * half + k, 8, stride=4), :]
+
+    for gm in range(4):
+        rows = []
+        for k in range(2):
+            t = [tile(k, 3 * gm + n) for n in range(3)]
+            rows.append([t[0], t[0], jnp.where(lane < 96, t[1], t[0]), t[1], t[1], jnp.where(lane < 112, t[2], t[1]), t[2], t[2]])
+        for q in range(8):
+            mine = ((lane - OWN * q) & (LANES - 1)) < OWN
+            out_ref[pl.ds(8 * gm + q, 8, stride=32), :] = jnp.where(mine, rows[0][q], pltpu.roll(rows[1][q], OWN, 1))
 
 
 def image_of(got_ref, h_ref, u, scale):
@@ -72,7 +81,7 @@
     return p, kappa
 
 
-def step_body(col, own, got_ref, base_ref, h_ref, u_ref, rows_ref, w_ref, un_ref, out_ref, flat_ref):
+def step_body(col, slots_ref, got_ref, base_ref, h_ref, u_ref, rows_ref, w_ref, un_ref, out_ref, flat_ref):
     j = col[0]
     u = [u_ref[m] for m in range(TILES)]
     scale = u_ref[SCALE, 0:1, 0:1]
@@ -101,7 +110,7 @@
         acc[s % 2] = acc[s % 2] + rows_ref[k, :, LANES * t : LANES * (t + 1)] * flat_ref[s : s + 1, :]
     product = jnp.sum(acc[0] + acc[1], axis=1, keepdims=True) * inverse + own_column(rows_ref, j + 1)
     out_ref[...] = jnp.broadcast_to(
-        message(product, own_column(rows_ref, j + 2), own[0]), out_ref.shape
+        message(product, own_column(rows_ref, j + 2), slots_ref), out_ref.shape
     )
     for m in range(TILES):
         w_ref[m] = p[m] - kappa * u[m]
@@ -159,7 +168,7 @@
         n = (PANEL_COLUMNS - 1) * per + 8 * m
         hist[0, n : n + 8, :] = u[m]
         hist[1, n : n + 8, :] = p[m] - kappa * u[m]
-    for side, n in ((0, own[1]), (1, own[2])):
+    for side, n in ((0, own[0]), (1, own[1])):
         z, m0 = n // 2, 6 * (n % 2)
         for t in range(6):
             for half in range(2):
@@ -205,10 +214,19 @@
     ways = lax.axis_size("col")
     devices = ways * lax.axis_size("row")
     tile_cols = matrix.shape[1]
-    own = jnp.stack([(OWN * (r * ways + c)) & (LANES - 1), r, c])
+    own = jnp.stack([r, c])
     rows = lax.all_to_all(
         matrix.reshape(ways, OWN, tile_cols), "col", split_axis=0, concat_axis=0, tiled=True
     )
+    top = jnp.where(r == 0, matrix[:2], 0.0)
+    for far in (8, 4, 2, 1):
+        top = top + lax.ppermute(top, "row", [(n, n + far) for n in range(0, 16, 2 * far)])
+    for bit in (1, 2, 4, 8):
+        other = lax.ppermute(top, "col", [(n, n ^ bit) for n in range(ways)])
+        low = (c & bit) == 0
+        top = jnp.concatenate([jnp.where(low, top, other), jnp.where(low, other, top)])
+    place = iota((2, OWN, LANES), 2) - iota((2, OWN, LANES), 1) - OWN * (r * ways + c + iota((2, OWN, LANES), 0))
+    slots = jnp.where((place & (LANES - 1)) == 0, 1.0, 0.0).astype(f32)
 
     def exchange(packed):
         return lax.all_to_all(packed, ("row", "col"), split_axis=0, concat_axis=0, tiled=True)
@@ -219,11 +237,11 @@
     vec, ext, packed = shape(TILES, 8, LANES), shape(TILES + 2, 8, LANES), shape(devices, LANES)
     hist = shape(2, PANEL_COLUMNS, TILES, 8, LANES)
     order = TILES * 8 * LANES
-    first = pl.pallas_call(first_body, out_shape=packed, in_specs=[SMEM, VMEM], out_specs=VMEM, name="first")
+    begin = pl.pallas_call(begin_body, out_shape=packed, in_specs=[VMEM], out_specs=VMEM, scratch_shapes=[pltpu.VMEM((192, LANES), f32)], name="begin")
     step = pl.pallas_call(
         step_body,
         out_shape=(vec, ext, packed),
-        in_specs=[SMEM] * 2 + [VMEM] * 5,
+        in_specs=[SMEM] + [VMEM] * 6,
         out_specs=(VMEM,) * 3,
         scratch_shapes=[pltpu.VMEM((order // LANES, LANES), f32)],
         name="step",
@@ -255,7 +273,7 @@
     def one_column(j, state):
         got, base, h, u, kept = state
         col = jnp.reshape(j, (1,))
-        w, un, out = step(col, own, got, base, h, u, rows)
+        w, un, out = step(col, slots, got, base, h, u, rows)
         got_next = exchange(out)
         base, h, kept = history(col, got, w, u, un, kept)
         return got_next, base, h, un, kept
@@ -264,7 +282,7 @@
         return jnp.zeros(s.shape, f32)
 
     u = jnp.concatenate([zeros(vec), jnp.full((1, 8, LANES), -1.0, f32), jnp.zeros((1, 8, LANES), f32)])
-    state = (exchange(first(own, rows)), zeros(vec), zeros(vec), u, zeros(hist))
+    state = (begin(top), zeros(vec), zeros(vec), u, zeros(hist))
     got, _, h, u, kept = lax.fori_loop(0, PANEL_COLUMNS, one_column, state)
     updated, whole = last(own, got, h, u, kept.reshape(2, -1, LANES), matrix)
     return updated, whole, u[COEF, :2, :PANEL_COLUMNS]

time: 409 us -> 420 us (1.027)
  waiting for transfers between devices: 210 us -> 182 us
  other arithmetic: 0.08 us -> 14 us
  local copies, waits for them, and re-layouts: 2.22 us -> 15.2 us
  starting transfers between devices: 111 us -> 117 us
    all_to_all x1, waiting for transfers between devices: 34.8 us -> 0.01 us  [per_device(): lax.all_to_all(matrix.reshape(ways, OWN, tile_cols), 'col', split_axis=0,...]
    ppermute x0 -> x8, waiting for transfers between devices: none -> 32.9 us  [the longest x4 17.7 us: per_device(): other = lax.ppermute(top, 'col', [(n, n ^ bit) for n in range(ways)])]
    all_to_all x17 -> x16, waiting for transfers between devices: 175 us -> 149 us  [exchange(): lax.all_to_all(packed, ('row', 'col'), split_axis=0, concat_axis=0, tiled...]
    while x64 -> x32, local copies, waits for them, and re-layouts: 0.3 us -> 13.3 us
    select_n x0 -> x21, other arithmetic: none -> 11.9 us  [the longest x16 11.1 us: per_device(): slots = jnp.where(place & LANES - 1 == 0, 1.0, 0.0).astype(f32)]
    ppermute x0 -> x8, starting transfers between devices: none -> 8.75 us  [the longest x4 5.5 us: per_device(): other = lax.ppermute(top, 'col', [(n, n ^ bit) for n in range(ways)])]
    all_to_all x17 -> x16, starting transfers between devices: 103 us -> 101 us  [exchange(): lax.all_to_all(packed, ('row', 'col'), split_axis=0, concat_axis=0, tiled...]
  transfers between devices with their start and end apart: 18 -> 25, of which waited for: 18 -> 21; matrix products, arithmetic and copies ran while one was open for 0% -> 4% of each run, Pallas kernels for 12% -> 12%
where the time goes in v2:
time: 420 us; the launch traced here: 416 us
  waiting for transfers between devices  182 us (43%)
  starting transfers between devices  117 us (28%)
  Pallas kernels  86.6 us (21%)
  local copies, waits for them, and re-layouts  15.2 us (4%)
  other arithmetic  14 us (3%)
    all_to_all x16, waiting for transfers between devices, exchange(): lax.all_to_all(packed, ('row', 'col'), split_axis=0, concat_axis=0, tiled...  149 us
    all_to_all x16, starting transfers between devices, exchange(): lax.all_to_all(packed, ('row', 'col'), split_axis=0, concat_axis=0, tiled...  101 us
    pallas_call x16, Pallas kernels, one_column(): base, h, kept = history(col, got, w, u, un, kept)  47.8 us
    pallas_call x16, Pallas kernels, one_column(): w, un, out = step(col, slots, got, base, h, u, rows)  32.9 us
    ppermute x4, waiting for transfers between devices, per_device(): other = lax.ppermute(top, 'col', [(n, n ^ bit) for n in range(ways)])  17.7 us
    ppermute x4, waiting for transfers between devices, per_device(): lax.ppermute(top, 'row', [(n, n + far) for n in range(0, 16, 2 * far)])  15.2 us
    while x32, local copies, waits for them, and re-layouts  13.3 us
    select_n x16, other arithmetic, per_device(): slots = jnp.where(place & LANES - 1 == 0, 1.0, 0.0).astype(f32)  11.1 us
  transfers between devices with their start and end apart: 25, of which 21 were waited for; matrix products, arithmetic and copies ran while one was open for 4% of the time, Pallas kernels for 12%

profile of v2, /device:TPU:1, one launch (start us, length us, event | category | flops | bytes accessed | tf_op | source)
XLA Modules:
  0.0 416.3 jit_solution(10484552448272441343)
XLA Ops:
  0.6 7.6 %all-to-all-start.1 = ((f32[16,48,768]{2,1,0:T(8,128)}), f32[16,48,768]{2,1,0:T(8,128)S(1)}, u32[]{:S(2)}, u32[]{:S(2)}) async-start(f32[16,48,768]{2,1,0:T(8,128)} %bitcast.19), calls=%async_computation.1 | async-start | bytes 4718592 | tf_op jit(solution)/shard_map/all_to_all | solution.py:218
  13.1 15.2 %collective-permute-done.3 = f32[2,768]{1,0:T(2,128)S(1)} collective-permute-done((f32[2,768]{1,0:T(2,128)S(1)}, f32[2,768]{1,0:T(2,128)S(1)}, u32[]{:S(2)}, u32[]{:S(2)}) %collective-permute-start.3) | collective-permute-done | bytes 6176 | tf_op jit(solution)/shard_map/ppermute | solution.py:223
  29.9 10.4 %collective-permute-done.4 = f32[2,768]{1,0:T(2,128)S(1)} collective-permute-done((f32[2,768]{1,0:T(2,128)S(1)}, f32[2,768]{1,0:T(2,128)S(1)}, u32[]{:S(2)}, u32[]{:S(2)}) %collective-permute-start.4) | collective-permute-done | bytes 6176 | tf_op jit(solution)/shard_map/ppermute | solution.py:225
  55.3 355.6 %while.22 = (s32[]{:T(128)}, f32[256,128]{1,0:T(8,128)S(1)}, f32[12,8,128]{2,1,0:T(8,128)S(1)}, f32[12,8,128]{2,1,0:T(8,128)S(1)}, f32[14,8,128]{2,1,0:T(8,128)S...) while((s32[]{:T(128)}, f32[256,128]{1,0:T(8,128)S(1)}, ...), condition=%wide.region_1.2_spmd.clone, body=%wide.region_0.1_spmd.clone.sunk | while | flops 61442 | bytes 819341 | solution.py:286
  58.0 18.0 %all-to-all-start = ((f32[256,1,128]{2,1,0:T(1,128)}), f32[256,1,128]{2,1,0:T(1,128)S(1)}, u32[]{:S(2)}, u32[]{:S(2)}) async-start(f32[256,1,128]{2,1,0:T(1,128)} %bitcast.20), calls=%async_computation | async-start | bytes 262144 | tf_op jit(solution)/shard_map/while/body/eval_jaxpr/all_to_all | solution.py:232
  79.9 9.2 %all-to-all-done = f32[256,1,128]{2,1,0:T(1,128)S(1)} async-done(((f32[256,1,128]{2,1,0:T(1,128)}), f32[256,1,128]{2,1,0:T(1,128)S(1)}, u32[]{:S(2)}, u32[]{:S(2)}) %all-to-all-start) | async-done | bytes 131104 | tf_op jit(solution)/shard_map/while/body/eval_jaxpr/all_to_all | solution.py:232
  91.9 5.5 %all-to-all-start = ((f32[256,1,128]{2,1,0:T(1,128)}), f32[256,1,128]{2,1,0:T(1,128)S(1)}, u32[]{:S(2)}, u32[]{:S(2)}) async-start(f32[256,1,128]{2,1,0:T(1,128)} %bitcast.20), calls=%async_computation | async-start | bytes 262144 | tf_op jit(solution)/shard_map/while/body/eval_jaxpr/all_to_all | solution.py:232
  101.2 9.3 %all-to-all-done = f32[256,1,128]{2,1,0:T(1,128)S(1)} async-done(((f32[256,1,128]{2,1,0:T(1,128)}), f32[256,1,128]{2,1,0:T(1,128)S(1)}, u32[]{:S(2)}, u32[]{:S(2)}) %all-to-all-start) | async-done | bytes 131104 | tf_op jit(solution)/shard_map/while/body/eval_jaxpr/all_to_all | solution.py:232
  113.3 5.5 %all-to-all-start = ((f32[256,1,128]{2,1,0:T(1,128)}), f32[256,1,128]{2,1,0:T(1,128)S(1)}, u32[]{:S(2)}, u32[]{:S(2)}) async-start(f32[256,1,128]{2,1,0:T(1,128)} %bitcast.20), calls=%async_computation | async-start | bytes 262144 | tf_op jit(solution)/shard_map/while/body/eval_jaxpr/all_to_all | solution.py:232
  122.7 9.3 %all-to-all-done = f32[256,1,128]{2,1,0:T(1,128)S(1)} async-done(((f32[256,1,128]{2,1,0:T(1,128)}), f32[256,1,128]{2,1,0:T(1,128)S(1)}, u32[]{:S(2)}, u32[]{:S(2)}) %all-to-all-start) | async-done | bytes 131104 | tf_op jit(solution)/shard_map/while/body/eval_jaxpr/all_to_all | solution.py:232
  134.8 5.5 %all-to-all-start = ((f32[256,1,128]{2,1,0:T(1,128)}), f32[256,1,128]{2,1,0:T(1,128)S(1)}, u32[]{:S(2)}, u32[]{:S(2)}) async-start(f32[256,1,128]{2,1,0:T(1,128)} %bitcast.20), calls=%async_computation | async-start | bytes 262144 | tf_op jit(solution)/shard_map/while/body/eval_jaxpr/all_to_all | solution.py:232
  144.1 9.3 %all-to-all-done = f32[256,1,128]{2,1,0:T(1,128)S(1)} async-done(((f32[256,1,128]{2,1,0:T(1,128)}), f32[256,1,128]{2,1,0:T(1,128)S(1)}, u32[]{:S(2)}, u32[]{:S(2)}) %all-to-all-start) | async-done | bytes 131104 | tf_op jit(solution)/shard_map/while/body/eval_jaxpr/all_to_all | solution.py:232
  156.2 5.5 %all-to-all-start = ((f32[256,1,128]{2,1,0:T(1,128)}), f32[256,1,128]{2,1,0:T(1,128)S(1)}, u32[]{:S(2)}, u32[]{:S(2)}) async-start(f32[256,1,128]{2,1,0:T(1,128)} %bitcast.20), calls=%async_computation | async-start | bytes 262144 | tf_op jit(solution)/shard_map/while/body/eval_jaxpr/all_to_all | solution.py:232
  165.6 9.3 %all-to-all-done = f32[256,1,128]{2,1,0:T(1,128)S(1)} async-done(((f32[256,1,128]{2,1,0:T(1,128)}), f32[256,1,128]{2,1,0:T(1,128)S(1)}, u32[]{:S(2)}, u32[]{:S(2)}) %all-to-all-start) | async-done | bytes 131104 | tf_op jit(solution)/shard_map/while/body/eval_jaxpr/all_to_all | solution.py:232
  177.7 5.5 %all-to-all-start = ((f32[256,1,128]{2,1,0:T(1,128)}), f32[256,1,128]{2,1,0:T(1,128)S(1)}, u32[]{:S(2)}, u32[]{:S(2)}) async-start(f32[256,1,128]{2,1,0:T(1,128)} %bitcast.20), calls=%async_computation | async-start | bytes 262144 | tf_op jit(solution)/shard_map/while/body/eval_jaxpr/all_to_all | solution.py:232
  187.0 9.3 %all-to-all-done = f32[256,1,128]{2,1,0:T(1,128)S(1)} async-done(((f32[256,1,128]{2,1,0:T(1,128)}), f32[256,1,128]{2,1,0:T(1,128)S(1)}, u32[]{:S(2)}, u32[]{:S(2)}) %all-to-all-start) | async-done | bytes 131104 | tf_op jit(solution)/shard_map/while/body/eval_jaxpr/all_to_all | solution.py:232
  199.1 5.5 %all-to-all-start = ((f32[256,1,128]{2,1,0:T(1,128)}), f32[256,1,128]{2,1,0:T(1,128)S(1)}, u32[]{:S(2)}, u32[]{:S(2)}) async-start(f32[256,1,128]{2,1,0:T(1,128)} %bitcast.20), calls=%async_computation | async-start | bytes 262144 | tf_op jit(solution)/shard_map/while/body/eval_jaxpr/all_to_all | solution.py:232
  208.5 9.3 %all-to-all-done = f32[256,1,128]{2,1,0:T(1,128)S(1)} async-done(((f32[256,1,128]{2,1,0:T(1,128)}), f32[256,1,128]{2,1,0:T(1,128)S(1)}, u32[]{:S(2)}, u32[]{:S(2)}) %all-to-all-start) | async-done | bytes 131104 | tf_op jit(solution)/shard_map/while/body/eval_jaxpr/all_to_all | solution.py:232
  220.6 5.5 %all-to-all-start = ((f32[256,1,128]{2,1,0:T(1,128)}), f32[256,1,128]{2,1,0:T(1,128)S(1)}, u32[]{:S(2)}, u32[]{:S(2)}) async-start(f32[256,1,128]{2,1,0:T(1,128)} %bitcast.20), calls=%async_computation | async-start | bytes 262144 | tf_op jit(solution)/shard_map/while/body/eval_jaxpr/all_to_all | solution.py:232
  229.9 9.3 %all-to-all-done = f32[256,1,128]{2,1,0:T(1,128)S(1)} async-done(((f32[256,1,128]{2,1,0:T(1,128)}), f32[256,1,128]{2,1,0:T(1,128)S(1)}, u32[]{:S(2)}, u32[]{:S(2)}) %all-to-all-start) | async-done | bytes 131104 | tf_op jit(solution)/shard_map/while/body/eval_jaxpr/all_to_all | solution.py:232
  242.0 5.5 %all-to-all-start = ((f32[256,1,128]{2,1,0:T(1,128)}), f32[256,1,128]{2,1,0:T(1,128)S(1)}, u32[]{:S(2)}, u32[]{:S(2)}) async-start(f32[256,1,128]{2,1,0:T(1,128)} %bitcast.20), calls=%async_computation | async-start | bytes 262144 | tf_op jit(solution)/shard_map/while/body/eval_jaxpr/all_to_all | solution.py:232
  251.4 9.3 %all-to-all-done = f32[256,1,128]{2,1,0:T(1,128)S(1)} async-done(((f32[256,1,128]{2,1,0:T(1,128)}), f32[256,1,128]{2,1,0:T(1,128)S(1)}, u32[]{:S(2)}, u32[]{:S(2)}) %all-to-all-start) | async-done | bytes 131104 | tf_op jit(solution)/shard_map/while/body/eval_jaxpr/all_to_all | solution.py:232
  263.5 5.5 %all-to-all-start = ((f32[256,1,128]{2,1,0:T(1,128)}), f32[256,1,128]{2,1,0:T(1,128)S(1)}, u32[]{:S(2)}, u32[]{:S(2)}) async-start(f32[256,1,128]{2,1,0:T(1,128)} %bitcast.20), calls=%async_computation | async-start | bytes 262144 | tf_op jit(solution)/shard_map/while/body/eval_jaxpr/all_to_all | solution.py:232
  272.8 9.3 %all-to-all-done = f32[256,1,128]{2,1,0:T(1,128)S(1)} async-done(((f32[256,1,128]{2,1,0:T(1,128)}), f32[256,1,128]{2,1,0:T(1,128)S(1)}, u32[]{:S(2)}, u32[]{:S(2)}) %all-to-all-start) | async-done | bytes 131104 | tf_op jit(solution)/shard_map/while/body/eval_jaxpr/all_to_all | solution.py:232
  284.9 5.5 %all-to-all-start = ((f32[256,1,128]{2,1,0:T(1,128)}), f32[256,1,128]{2,1,0:T(1,128)S(1)}, u32[]{:S(2)}, u32[]{:S(2)}) async-start(f32[256,1,128]{2,1,0:T(1,128)} %bitcast.20), calls=%async_computation | async-start | bytes 262144 | tf_op jit(solution)/shard_map/while/body/eval_jaxpr/all_to_all | solution.py:232
  294.3 9.3 %all-to-all-done = f32[256,1,128]{2,1,0:T(1,128)S(1)} async-done(((f32[256,1,128]{2,1,0:T(1,128)}), f32[256,1,128]{2,1,0:T(1,128)S(1)}, u32[]{:S(2)}, u32[]{:S(2)}) %all-to-all-start) | async-done | bytes 131104 | tf_op jit(solution)/shard_map/while/body/eval_jaxpr/all_to_all | solution.py:232
  315.7 9.3 %all-to-all-done = f32[256,1,128]{2,1,0:T(1,128)S(1)} async-done(((f32[256,1,128]{2,1,0:T(1,128)}), f32[256,1,128]{2,1,0:T(1,128)S(1)}, u32[]{:S(2)}, u32[]{:S(2)}) %all-to-all-start) | async-done | bytes 131104 | tf_op jit(solution)/shard_map/while/body/eval_jaxpr/all_to_all | solution.py:232
  337.2 9.3 %all-to-all-done = f32[256,1,128]{2,1,0:T(1,128)S(1)} async-done(((f32[256,1,128]{2,1,0:T(1,128)}), f32[256,1,128]{2,1,0:T(1,128)S(1)}, u32[]{:S(2)}, u32[]{:S(2)}) %all-to-all-start) | async-done | bytes 131104 | tf_op jit(solution)/shard_map/while/body/eval_jaxpr/all_to_all | solution.py:232
  349.3 5.5 %all-to-all-start = ((f32[256,1,128]{2,1,0:T(1,128)}), f32[256,1,128]{2,1,0:T(1,128)S(1)}, u32[]{:S(2)}, u32[]{:S(2)}) async-start(f32[256,1,128]{2,1,0:T(1,128)} %bitcast.20), calls=%async_computation | async-start | bytes 262144 | tf_op jit(solution)/shard_map/while/body/eval_jaxpr/all_to_all | solution.py:232
  358.7 9.3 %all-to-all-done = f32[256,1,128]{2,1,0:T(1,128)S(1)} async-done(((f32[256,1,128]{2,1,0:T(1,128)}), f32[256,1,128]{2,1,0:T(1,128)S(1)}, u32[]{:S(2)}, u32[]{:S(2)}) %all-to-all-start) | async-done | bytes 131104 | tf_op jit(solution)/shard_map/while/body/eval_jaxpr/all_to_all | solution.py:232
  380.1 9.3 %all-to-all-done = f32[256,1,128]{2,1,0:T(1,128)S(1)} async-done(((f32[256,1,128]{2,1,0:T(1,128)}), f32[256,1,128]{2,1,0:T(1,128)S(1)}, u32[]{:S(2)}, u32[]{:S(2)}) %all-to-all-start) | async-done | bytes 131104 | tf_op jit(solution)/shard_map/while/body/eval_jaxpr/all_to_all | solution.py:232
  401.5 9.3 %all-to-all-done = f32[256,1,128]{2,1,0:T(1,128)S(1)} async-done(((f32[256,1,128]{2,1,0:T(1,128)}), f32[256,1,128]{2,1,0:T(1,128)S(1)}, u32[]{:S(2)}, u32[]{:S(2)}) %all-to-all-start) | async-done | bytes 131104 | tf_op jit(solution)/shard_map/while/body/eval_jaxpr/all_to_all | solution.py:232
  (122 shorter events, 154.0 us)
Async XLA Ops:
  0.6 53.3 %all-to-all-start.1 = ((f32[16,48,768]{2,1,0:T(8,128)}), f32[16,48,768]{2,1,0:T(8,128)S(1)}, u32[]{:S(2)}, u32[]{:S(2)}) async-start(f32[16,48,768]{2,1,0:T(8,128)} %bitcast.19), calls=%async_computation.1 | async-start | bytes 4718592 | tf_op jit(solution)/shard_map/all_to_all | solution.py:218
  8.2 47.1 %copy-start = (f32[14,8,128]{2,1,0:T(8,128)S(1)}, f32[14,8,128]{2,1,0:T(8,128)}, u32[]{:S(2)}) copy-start(f32[14,8,128]{2,1,0:T(8,128)} %constant.37.clone.1) | copy-start | bytes 172036
  9.0 0.7 collective-permute-start
  10.4 0.7 collective-permute-start.1
  11.1 0.7 collective-permute-start.2
  11.8 16.5 %collective-permute-start.3 = (f32[2,768]{1,0:T(2,128)S(1)}, f32[2,768]{1,0:T(2,128)S(1)}, u32[]{:S(2)}, u32[]{:S(2)}) collective-permute-start(f32[2,768]{1,0:T(2,128)S(1)} %add.40), channel_id=1, source_target_pairs={{0,16},{32,48},{64,80},{96,112},{128,144},{160,176},{192,208},{224... | collective-permute-start | bytes 18440 | tf_op jit(solution)/shard_map/ppermute | solution.py:223
  28.3 12.1 %collective-permute-start.4 = (f32[2,768]{1,0:T(2,128)S(1)}, f32[2,768]{1,0:T(2,128)S(1)}, u32[]{:S(2)}, u32[]{:S(2)}) collective-permute-start(f32[2,768]{1,0:T(2,128)S(1)} %add.41), channel_id=1, source_target_pairs={{0,1},{1,0},{2,3},{3,2},{4,5},{5,4},{6,7},{7,6},{8,9},{9,8},{10,11... | collective-permute-start | bytes 18440 | tf_op jit(solution)/shard_map/ppermute | solution.py:225
  40.4 4.2 %collective-permute-start.5 = (f32[4,768]{1,0:T(4,128)S(1)}, f32[4,768]{1,0:T(4,128)S(1)}, u32[]{:S(2)}, u32[]{:S(2)}) collective-permute-start(f32[4,768]{1,0:T(4,128)S(1)} %pad_maximum_fusion.3), channel_id=1, source_target_pairs={{0,2},{1,3},{2,0},{3,1},{4,6},{5,7},{6,4},{7,5},{8,10},{9,11},{10,... | collective-permute-start | bytes 36872 | tf_op jit(solution)/shard_map/ppermute | solution.py:225
  44.6 2.8 collective-permute-start.6
  47.4 4.8 %collective-permute-start.7 = (f32[16,768]{1,0:T(8,128)S(1)}, f32[16,768]{1,0:T(8,128)S(1)}, u32[]{:S(2)}, u32[]{:S(2)}) collective-permute-start(f32[16,768]{1,0:T(8,128)S(1)} %pad_maximum_fusion.1), channel_id=1, source_target_pairs={{0,8},{1,9},{2,10},{3,11},{4,12},{5,13},{6,14},{7,15},{8,0},{9,1},... | collective-permute-start | bytes 147464 | tf_op jit(solution)/shard_map/ppermute | solution.py:225
  58.0 31.0 %all-to-all-start = ((f32[256,1,128]{2,1,0:T(1,128)}), f32[256,1,128]{2,1,0:T(1,128)S(1)}, u32[]{:S(2)}, u32[]{:S(2)}) async-start(f32[256,1,128]{2,1,0:T(1,128)} %bitcast.20), calls=%async_computation | async-start | bytes 262144 | tf_op jit(solution)/shard_map/while/body/eval_jaxpr/all_to_all | solution.py:232
  91.9 18.7 %all-to-all-start = ((f32[256,1,128]{2,1,0:T(1,128)}), f32[256,1,128]{2,1,0:T(1,128)S(1)}, u32[]{:S(2)}, u32[]{:S(2)}) async-start(f32[256,1,128]{2,1,0:T(1,128)} %bitcast.20), calls=%async_computation | async-start | bytes 262144 | tf_op jit(solution)/shard_map/while/body/eval_jaxpr/all_to_all | solution.py:232
  113.3 18.7 %all-to-all-start = ((f32[256,1,128]{2,1,0:T(1,128)}), f32[256,1,128]{2,1,0:T(1,128)S(1)}, u32[]{:S(2)}, u32[]{:S(2)}) async-start(f32[256,1,128]{2,1,0:T(1,128)} %bitcast.20), calls=%async_computation | async-start | bytes 262144 | tf_op jit(solution)/shard_map/while/body/eval_jaxpr/all_to_all | solution.py:232
  134.8 18.7 %all-to-all-start = ((f32[256,1,128]{2,1,0:T(1,128)}), f32[256,1,128]{2,1,0:T(1,128)S(1)}, u32[]{:S(2)}, u32[]{:S(2)}) async-start(f32[256,1,128]{2,1,0:T(1,128)} %bitcast.20), calls=%async_computation | async-start | bytes 262144 | tf_op jit(solution)/shard_map/while/body/eval_jaxpr/all_to_all | solution.py:232
  156.2 18.7 %all-to-all-start = ((f32[256,1,128]{2,1,0:T(1,128)}), f32[256,1,128]{2,1,0:T(1,128)S(1)}, u32[]{:S(2)}, u32[]{:S(2)}) async-start(f32[256,1,128]{2,1,0:T(1,128)} %bitcast.20), calls=%async_computation | async-start | bytes 262144 | tf_op jit(solution)/shard_map/while/body/eval_jaxpr/all_to_all | solution.py:232
  177.7 18.7 %all-to-all-start = ((f32[256,1,128]{2,1,0:T(1,128)}), f32[256,1,128]{2,1,0:T(1,128)S(1)}, u32[]{:S(2)}, u32[]{:S(2)}) async-start(f32[256,1,128]{2,1,0:T(1,128)} %bitcast.20), calls=%async_computation | async-start | bytes 262144 | tf_op jit(solution)/shard_map/while/body/eval_jaxpr/all_to_all | solution.py:232
  199.1 18.7 %all-to-all-start = ((f32[256,1,128]{2,1,0:T(1,128)}), f32[256,1,128]{2,1,0:T(1,128)S(1)}, u32[]{:S(2)}, u32[]{:S(2)}) async-start(f32[256,1,128]{2,1,0:T(1,128)} %bitcast.20), calls=%async_computation | async-start | bytes 262144 | tf_op jit(solution)/shard_map/while/body/eval_jaxpr/all_to_all | solution.py:232
  220.6 18.7 %all-to-all-start = ((f32[256,1,128]{2,1,0:T(1,128)}), f32[256,1,128]{2,1,0:T(1,128)S(1)}, u32[]{:S(2)}, u32[]{:S(2)}) async-start(f32[256,1,128]{2,1,0:T(1,128)} %bitcast.20), calls=%async_computation | async-start | bytes 262144 | tf_op jit(solution)/shard_map/while/body/eval_jaxpr/all_to_all | solution.py:232
  242.0 18.7 %all-to-all-start = ((f32[256,1,128]{2,1,0:T(1,128)}), f32[256,1,128]{2,1,0:T(1,128)S(1)}, u32[]{:S(2)}, u32[]{:S(2)}) async-start(f32[256,1,128]{2,1,0:T(1,128)} %bitcast.20), calls=%async_computation | async-start | bytes 262144 | tf_op jit(solution)/shard_map/while/body/eval_jaxpr/all_to_all | solution.py:232
  263.5 18.7 %all-to-all-start = ((f32[256,1,128]{2,1,0:T(1,128)}), f32[256,1,128]{2,1,0:T(1,128)S(1)}, u32[]{:S(2)}, u32[]{:S(2)}) async-start(f32[256,1,128]{2,1,0:T(1,128)} %bitcast.20), calls=%async_computation | async-start | bytes 262144 | tf_op jit(solution)/shard_map/while/body/eval_jaxpr/all_to_all | solution.py:232
  284.9 18.7 %all-to-all-start = ((f32[256,1,128]{2,1,0:T(1,128)}), f32[256,1,128]{2,1,0:T(1,128)S(1)}, u32[]{:S(2)}, u32[]{:S(2)}) async-start(f32[256,1,128]{2,1,0:T(1,128)} %bitcast.20), calls=%async_computation | async-start | bytes 262144 | tf_op jit(solution)/shard_map/while/body/eval_jaxpr/all_to_all | solution.py:232
  306.4 18.7 %all-to-all-start = ((f32[256,1,128]{2,1,0:T(1,128)}), f32[256,1,128]{2,1,0:T(1,128)S(1)}, u32[]{:S(2)}, u32[]{:S(2)}) async-start(f32[256,1,128]{2,1,0:T(1,128)} %bitcast.20), calls=%async_computation | async-start | bytes 262144 | tf_op jit(solution)/shard_map/while/body/eval_jaxpr/all_to_all | solution.py:232
  327.8 18.7 %all-to-all-start = ((f32[256,1,128]{2,1,0:T(1,128)}), f32[256,1,128]{2,1,0:T(1,128)S(1)}, u32[]{:S(2)}, u32[]{:S(2)}) async-start(f32[256,1,128]{2,1,0:T(1,128)} %bitcast.20), calls=%async_computation | async-start | bytes 262144 | tf_op jit(solution)/shard_map/while/body/eval_jaxpr/all_to_all | solution.py:232
  349.3 18.7 %all-to-all-start = ((f32[256,1,128]{2,1,0:T(1,128)}), f32[256,1,128]{2,1,0:T(1,128)S(1)}, u32[]{:S(2)}, u32[]{:S(2)}) async-start(f32[256,1,128]{2,1,0:T(1,128)} %bitcast.20), calls=%async_computation | async-start | bytes 262144 | tf_op jit(solution)/shard_map/while/body/eval_jaxpr/all_to_all | solution.py:232
  370.7 18.7 %all-to-all-start = ((f32[256,1,128]{2,1,0:T(1,128)}), f32[256,1,128]{2,1,0:T(1,128)S(1)}, u32[]{:S(2)}, u32[]{:S(2)}) async-start(f32[256,1,128]{2,1,0:T(1,128)} %bitcast.20), calls=%async_computation | async-start | bytes 262144 | tf_op jit(solution)/shard_map/while/body/eval_jaxpr/all_to_all | solution.py:232
  392.2 18.7 %all-to-all-start = ((f32[256,1,128]{2,1,0:T(1,128)}), f32[256,1,128]{2,1,0:T(1,128)S(1)}, u32[]{:S(2)}, u32[]{:S(2)}) async-start(f32[256,1,128]{2,1,0:T(1,128)} %bitcast.20), calls=%async_computation | async-start | bytes 262144 | tf_op jit(solution)/shard_map/while/body/eval_jaxpr/all_to_all | solution.py:232

commit v3 on v2

--- a/solution.py
+++ b/solution.py
@@ -46,8 +46,11 @@
     return (iota((8, LANES), 0) * TILES + m) * LANES + iota((8, LANES), 1)
 
 
-def message(first, second, slots_ref):
-    return jnp.sum(slots_ref[0] * first + slots_ref[1] * second, axis=0, keepdims=True)
+def message(first, second):
+    device = lax.axis_index("row") * lax.axis_size("col") + lax.axis_index("col")
+    place = iota((OWN, LANES), 1) - iota((OWN, LANES), 0) - OWN * device
+    picked = jnp.where((place & (LANES - 1)) == 0, first, 0.0) + jnp.where((place & (LANES - 1)) == OWN, second, 0.0)
+    return jnp.sum(picked, axis=0, keepdims=True)
 
 
 def own_column(rows_ref, k):
@@ -55,7 +58,11 @@
     return jnp.sum(jnp.where(iota((OWN, LANES), 1) == k, head, 0.0), axis=1, keepdims=True)
 
 
-def begin_body(top_ref, out_ref, tmp):
+def begin_body(top_ref, out_ref, hist_ref, tmp, zero, sem):
+    zero[...] = jnp.zeros(zero.shape, jnp.float32)
+    clear = [pltpu.make_async_copy(zero, hist_ref.at[n], sem.at[n]) for n in range(2)]
+    for copy in clear:
+        copy.start()
     lane = iota((8, LANES), 1)
     for t in range(6):
         tmp[32 * t : 32 * (t + 1), :] = top_ref[:, LANES * t : LANES * (t + 1)]
@@ -72,6 +79,8 @@
         for q in range(8):
             mine = ((lane - OWN * q) & (LANES - 1)) < OWN
             out_ref[pl.ds(8 * gm + q, 8, stride=32), :] = jnp.where(mine, rows[0][q], pltpu.roll(rows[1][q], OWN, 1))
+    for copy in clear:
+        copy.wait()
 
 
 def image_of(got_ref, h_ref, u, scale):
@@ -81,7 +90,7 @@
     return p, kappa
 
 
-def step_body(col, slots_ref, got_ref, base_ref, h_ref, u_ref, rows_ref, w_ref, un_ref, out_ref, flat_ref):
+def step_body(col, got_ref, base_ref, h_ref, u_ref, rows_ref, w_ref, un_ref, out_ref, flat_ref):
     j = col[0]
     u = [u_ref[m] for m in range(TILES)]
     scale = u_ref[SCALE, 0:1, 0:1]
@@ -110,7 +119,7 @@
         acc[s % 2] = acc[s % 2] + rows_ref[k, :, LANES * t : LANES * (t + 1)] * flat_ref[s : s + 1, :]
     product = jnp.sum(acc[0] + acc[1], axis=1, keepdims=True) * inverse + own_column(rows_ref, j + 1)
     out_ref[...] = jnp.broadcast_to(
-        message(product, own_column(rows_ref, j + 2), slots_ref), out_ref.shape
+        message(product, own_column(rows_ref, j + 2)), out_ref.shape
     )
     for m in range(TILES):
         w_ref[m] = p[m] - kappa * u[m]
@@ -215,18 +224,16 @@
     devices = ways * lax.axis_size("row")
     tile_cols = matrix.shape[1]
     own = jnp.stack([r, c])
-    rows = lax.all_to_all(
-        matrix.reshape(ways, OWN, tile_cols), "col", split_axis=0, concat_axis=0, tiled=True
-    )
-    top = jnp.where(r == 0, matrix[:2], 0.0)
+    top = lax.all_to_all(
+        jnp.broadcast_to(matrix[:2], (ways, 2, tile_cols)), "col", split_axis=0, concat_axis=0, tiled=True
+    ).reshape(2 * ways, tile_cols)
+    top, matrix_after = lax.optimization_barrier((top, matrix))
+    top = jnp.where(r == 0, top, 0.0)
     for far in (8, 4, 2, 1):
         top = top + lax.ppermute(top, "row", [(n, n + far) for n in range(0, 16, 2 * far)])
-    for bit in (1, 2, 4, 8):
-        other = lax.ppermute(top, "col", [(n, n ^ bit) for n in range(ways)])
-        low = (c & bit) == 0
-        top = jnp.concatenate([jnp.where(low, top, other), jnp.where(low, other, top)])
-    place = iota((2, OWN, LANES), 2) - iota((2, OWN, LANES), 1) - OWN * (r * ways + c + iota((2, OWN, LANES), 0))
-    slots = jnp.where((place & (LANES - 1)) == 0, 1.0, 0.0).astype(f32)
+    rows = lax.all_to_all(
+        matrix_after.reshape(ways, OWN, tile_cols), "col", split_axis=0, concat_axis=0, tiled=True
+    )
 
     def exchange(packed):
         return lax.all_to_all(packed, ("row", "col"), split_axis=0, concat_axis=0, tiled=True)
@@ -237,11 +244,22 @@
     vec, ext, packed = shape(TILES, 8, LANES), shape(TILES + 2, 8, LANES), shape(devices, LANES)
     hist = shape(2, PANEL_COLUMNS, TILES, 8, LANES)
     order = TILES * 8 * LANES
-    begin = pl.pallas_call(begin_body, out_shape=packed, in_specs=[VMEM], out_specs=VMEM, scratch_shapes=[pltpu.VMEM((192, LANES), f32)], name="begin")
+    begin = pl.pallas_call(
+        begin_body,
+        out_shape=(packed, hist),
+        in_specs=[VMEM],
+        out_specs=(VMEM, ANY),
+        scratch_shapes=[
+            pltpu.VMEM((192, LANES), f32),
+            pltpu.VMEM(hist.shape[1:], f32),
+            pltpu.SemaphoreType.DMA((2,)),
+        ],
+        name="begin",
+    )
     step = pl.pallas_call(
         step_body,
         out_shape=(vec, ext, packed),
-        in_specs=[SMEM] + [VMEM] * 6,
+        in_specs=[SMEM] + [VMEM] * 5,
         out_specs=(VMEM,) * 3,
         scratch_shapes=[pltpu.VMEM((order // LANES, LANES), f32)],
         name="step",
@@ -273,7 +291,7 @@
     def one_column(j, state):
         got, base, h, u, kept = state
         col = jnp.reshape(j, (1,))
-        w, un, out = step(col, slots, got, base, h, u, rows)
+        w, un, out = step(col, got, base, h, u, rows)
         got_next = exchange(out)
         base, h, kept = history(col, got, w, u, un, kept)
         return got_next, base, h, un, kept
@@ -282,7 +300,8 @@
         return jnp.zeros(s.shape, f32)
 
     u = jnp.concatenate([zeros(vec), jnp.full((1, 8, LANES), -1.0, f32), jnp.zeros((1, 8, LANES), f32)])
-    state = (begin(top), zeros(vec), zeros(vec), u, zeros(hist))
+    got, kept = begin(top)
+    state = (got, zeros(vec), zeros(vec), u, kept)
     got, _, h, u, kept = lax.fori_loop(0, PANEL_COLUMNS, one_column, state)
     updated, whole = last(own, got, h, u, kept.reshape(2, -1, LANES), matrix)
     return updated, whole, u[COEF, :2, :PANEL_COLUMNS]

time: 420 us -> 388 us (0.924)
  blocking collectives: 0 us -> 14.1 us
  local copies, waits for them, and re-layouts: 15.2 us -> 1.72 us
  other arithmetic: 14 us -> 1.38 us
  Pallas kernels: 86.6 us -> 74.9 us
  starting transfers between devices: 117 us -> 106 us
    ppermute x4 -> x0, waiting for transfers between devices: 17.7 us -> none  [per_device(): other = lax.ppermute(top, 'col', [(n, n ^ bit) for n in range(ways)])]
    all_to_all x0 -> x1, blocking collectives: none -> 14.1 us  [per_device(): lax.all_to_all(jnp.broadcast_to(matrix[:2], (ways, 2, tile_cols)), 'col',...]
    while x32 -> x64, local copies, waits for them, and re-layouts: 13.3 us -> 0.3 us
    all_to_all x16, waiting for transfers between devices: 149 us -> 162 us  [exchange(): lax.all_to_all(packed, ('row', 'col'), split_axis=0, concat_axis=0, tiled...]
    select_n x21 -> x1, other arithmetic: 11.9 us -> 0.01 us  [per_device(): top = jnp.where(r == 0, top, 0.0)]
    pallas_call x17, Pallas kernels: 33.9 us -> 22.2 us  [the longest x16 20.1 us: one_column(): w, un, out = step(col, got, base, h, u, rows)]
    all_to_all x1, waiting for transfers between devices: 0.01 us -> 6.02 us  [per_device(): lax.all_to_all(matrix_after.reshape(ways, OWN, tile_cols), 'col', split_a...]
    ppermute x4 -> x0, starting transfers between devices: 5.5 us -> none  [per_device(): other = lax.ppermute(top, 'col', [(n, n ^ bit) for n in range(ways)])]
  transfers between devices with their start and end apart: 25 -> 21, of which waited for: 21 -> 18; matrix products, arithmetic and copies ran while one was open for 4% -> 0% of each run, Pallas kernels for 12% -> 13%
where the time goes in v3:
time: 388 us; the launch traced here: 385 us
  waiting for transfers between devices  186 us (48%)
  starting transfers between devices  106 us (27%)
  Pallas kernels  74.9 us (19%)
  blocking collectives  14.1 us (4%)
    all_to_all x16, waiting for transfers between devices, exchange(): lax.all_to_all(packed, ('row', 'col'), split_axis=0, concat_axis=0, tiled...  162 us
    all_to_all x16, starting transfers between devices, exchange(): lax.all_to_all(packed, ('row', 'col'), split_axis=0, concat_axis=0, tiled...  98.6 us
    pallas_call x16, Pallas kernels, one_column(): base, h, kept = history(col, got, w, u, un, kept)  47.8 us
    pallas_call x16, Pallas kernels, one_column(): w, un, out = step(col, got, base, h, u, rows)  20.1 us
    ppermute x4, waiting for transfers between devices, per_device(): lax.ppermute(top, 'row', [(n, n + far) for n in range(0, 16, 2 * far)])  18.4 us
    all_to_all x1, blocking collectives, per_device(): lax.all_to_all(jnp.broadcast_to(matrix[:2], (ways, 2, tile_cols)), 'col',...  14.1 us
  transfers between devices with their start and end apart: 21, of which 18 were waited for; matrix products, arithmetic and copies ran while one was open for 0% of the time, Pallas kernels for 13%

profile of v3, /device:TPU:1, one launch (start us, length us, event | category | flops | bytes accessed | tf_op | source)
XLA Modules:
  0.0 385.5 jit_solution(2242672977196322931)
XLA Ops:
  1.4 14.1 %all_to_all.25 = f32[16,2,768]{2,1,0:T(2,128)S(1)} all-to-all(f32[16,2,768]{2,1,0:T(2,128)S(1)} %broadcast_in_dim.7), channel_id=1, replica_groups=mesh['row'=16,'col'=16] {'col'}, dimensions={0} | all-to-all | bytes 196608 | tf_op jit(solution)/shard_map/all_to_all | solution.py:227
  23.4 18.4 %collective-permute-done.3 = f32[32,768]{1,0:T(8,128)S(1)} collective-permute-done((f32[32,768]{1,0:T(8,128)S(1)}, f32[32,768]{1,0:T(8,128)S(1)}, u32[]{:S(2)}, u32[]{:S(2)}) %collective-permute-start.3) | collective-permute-done | bytes 98336 | tf_op jit(solution)/shard_map/ppermute | solution.py:233
  44.6 6.0 %all-to-all-done.2 = f32[16,48,768]{2,1,0:T(8,128)S(1)} async-done(((f32[16,48,768]{2,1,0:T(8,128)}), f32[16,48,768]{2,1,0:T(8,128)S(1)}, u32[]{:S(2)}, u32[]{:S(2)}) %all-to-all-start.2) | async-done | bytes 2359328 | tf_op jit(solution)/shard_map/all_to_all | solution.py:234
  50.7 329.4 %while.21 = (s32[]{:T(128)}, f32[256,128]{1,0:T(8,128)S(1)}, f32[12,8,128]{2,1,0:T(8,128)S(1)}, f32[12,8,128]{2,1,0:T(8,128)S(1)}, f32[14,8,128]{2,1,0:T(8,128)S...) while((s32[]{:T(128)}, f32[256,128]{1,0:T(8,128)S(1)}, ...), condition=%wide.region_1.2_spmd, body=%wide.region_0.1_spmd.sunk | while | flops 2 | bytes 999577 | solution.py:305
  51.9 13.8 %all-to-all-start = ((f32[256,1,128]{2,1,0:T(1,128)}), f32[256,1,128]{2,1,0:T(1,128)S(1)}, u32[]{:S(2)}, u32[]{:S(2)}) async-start(f32[256,1,128]{2,1,0:T(1,128)} %bitcast.20), calls=%async_computation | async-start | bytes 262144 | tf_op jit(solution)/shard_map/while/body/eval_jaxpr/all_to_all | solution.py:239
  68.7 10.0 %all-to-all-done = f32[256,1,128]{2,1,0:T(1,128)S(1)} async-done(((f32[256,1,128]{2,1,0:T(1,128)}), f32[256,1,128]{2,1,0:T(1,128)S(1)}, u32[]{:S(2)}, u32[]{:S(2)}) %all-to-all-start) | async-done | bytes 131104 | tf_op jit(solution)/shard_map/while/body/eval_jaxpr/all_to_all | solution.py:239
  80.0 5.7 %all-to-all-start = ((f32[256,1,128]{2,1,0:T(1,128)}), f32[256,1,128]{2,1,0:T(1,128)S(1)}, u32[]{:S(2)}, u32[]{:S(2)}) async-start(f32[256,1,128]{2,1,0:T(1,128)} %bitcast.20), calls=%async_computation | async-start | bytes 262144 | tf_op jit(solution)/shard_map/while/body/eval_jaxpr/all_to_all | solution.py:239
  88.7 10.1 %all-to-all-done = f32[256,1,128]{2,1,0:T(1,128)S(1)} async-done(((f32[256,1,128]{2,1,0:T(1,128)}), f32[256,1,128]{2,1,0:T(1,128)S(1)}, u32[]{:S(2)}, u32[]{:S(2)}) %all-to-all-start) | async-done | bytes 131104 | tf_op jit(solution)/shard_map/while/body/eval_jaxpr/all_to_all | solution.py:239
  100.1 5.7 %all-to-all-start = ((f32[256,1,128]{2,1,0:T(1,128)}), f32[256,1,128]{2,1,0:T(1,128)S(1)}, u32[]{:S(2)}, u32[]{:S(2)}) async-start(f32[256,1,128]{2,1,0:T(1,128)} %bitcast.20), calls=%async_computation | async-start | bytes 262144 | tf_op jit(solution)/shard_map/while/body/eval_jaxpr/all_to_all | solution.py:239
  108.8 10.1 %all-to-all-done = f32[256,1,128]{2,1,0:T(1,128)S(1)} async-done(((f32[256,1,128]{2,1,0:T(1,128)}), f32[256,1,128]{2,1,0:T(1,128)S(1)}, u32[]{:S(2)}, u32[]{:S(2)}) %all-to-all-start) | async-done | bytes 131104 | tf_op jit(solution)/shard_map/while/body/eval_jaxpr/all_to_all | solution.py:239
  120.2 5.7 %all-to-all-start = ((f32[256,1,128]{2,1,0:T(1,128)}), f32[256,1,128]{2,1,0:T(1,128)S(1)}, u32[]{:S(2)}, u32[]{:S(2)}) async-start(f32[256,1,128]{2,1,0:T(1,128)} %bitcast.20), calls=%async_computation | async-start | bytes 262144 | tf_op jit(solution)/shard_map/while/body/eval_jaxpr/all_to_all | solution.py:239
  128.8 10.1 %all-to-all-done = f32[256,1,128]{2,1,0:T(1,128)S(1)} async-done(((f32[256,1,128]{2,1,0:T(1,128)}), f32[256,1,128]{2,1,0:T(1,128)S(1)}, u32[]{:S(2)}, u32[]{:S(2)}) %all-to-all-start) | async-done | bytes 131104 | tf_op jit(solution)/shard_map/while/body/eval_jaxpr/all_to_all | solution.py:239
  140.3 5.7 %all-to-all-start = ((f32[256,1,128]{2,1,0:T(1,128)}), f32[256,1,128]{2,1,0:T(1,128)S(1)}, u32[]{:S(2)}, u32[]{:S(2)}) async-start(f32[256,1,128]{2,1,0:T(1,128)} %bitcast.20), calls=%async_computation | async-start | bytes 262144 | tf_op jit(solution)/shard_map/while/body/eval_jaxpr/all_to_all | solution.py:239
  148.9 10.1 %all-to-all-done = f32[256,1,128]{2,1,0:T(1,128)S(1)} async-done(((f32[256,1,128]{2,1,0:T(1,128)}), f32[256,1,128]{2,1,0:T(1,128)S(1)}, u32[]{:S(2)}, u32[]{:S(2)}) %all-to-all-start) | async-done | bytes 131104 | tf_op jit(solution)/shard_map/while/body/eval_jaxpr/all_to_all | solution.py:239
  160.3 5.7 %all-to-all-start = ((f32[256,1,128]{2,1,0:T(1,128)}), f32[256,1,128]{2,1,0:T(1,128)S(1)}, u32[]{:S(2)}, u32[]{:S(2)}) async-start(f32[256,1,128]{2,1,0:T(1,128)} %bitcast.20), calls=%async_computation | async-start | bytes 262144 | tf_op jit(solution)/shard_map/while/body/eval_jaxpr/all_to_all | solution.py:239
  169.0 10.1 %all-to-all-done = f32[256,1,128]{2,1,0:T(1,128)S(1)} async-done(((f32[256,1,128]{2,1,0:T(1,128)}), f32[256,1,128]{2,1,0:T(1,128)S(1)}, u32[]{:S(2)}, u32[]{:S(2)}) %all-to-all-start) | async-done | bytes 131104 | tf_op jit(solution)/shard_map/while/body/eval_jaxpr/all_to_all | solution.py:239
  180.4 5.7 %all-to-all-start = ((f32[256,1,128]{2,1,0:T(1,128)}), f32[256,1,128]{2,1,0:T(1,128)S(1)}, u32[]{:S(2)}, u32[]{:S(2)}) async-start(f32[256,1,128]{2,1,0:T(1,128)} %bitcast.20), calls=%async_computation | async-start | bytes 262144 | tf_op jit(solution)/shard_map/while/body/eval_jaxpr/all_to_all | solution.py:239
  189.1 10.1 %all-to-all-done = f32[256,1,128]{2,1,0:T(1,128)S(1)} async-done(((f32[256,1,128]{2,1,0:T(1,128)}), f32[256,1,128]{2,1,0:T(1,128)S(1)}, u32[]{:S(2)}, u32[]{:S(2)}) %all-to-all-start) | async-done | bytes 131104 | tf_op jit(solution)/shard_map/while/body/eval_jaxpr/all_to_all | solution.py:239
  200.5 5.7 %all-to-all-start = ((f32[256,1,128]{2,1,0:T(1,128)}), f32[256,1,128]{2,1,0:T(1,128)S(1)}, u32[]{:S(2)}, u32[]{:S(2)}) async-start(f32[256,1,128]{2,1,0:T(1,128)} %bitcast.20), calls=%async_computation | async-start | bytes 262144 | tf_op jit(solution)/shard_map/while/body/eval_jaxpr/all_to_all | solution.py:239
  209.2 10.1 %all-to-all-done = f32[256,1,128]{2,1,0:T(1,128)S(1)} async-done(((f32[256,1,128]{2,1,0:T(1,128)}), f32[256,1,128]{2,1,0:T(1,128)S(1)}, u32[]{:S(2)}, u32[]{:S(2)}) %all-to-all-start) | async-done | bytes 131104 | tf_op jit(solution)/shard_map/while/body/eval_jaxpr/all_to_all | solution.py:239
  220.6 5.7 %all-to-all-start = ((f32[256,1,128]{2,1,0:T(1,128)}), f32[256,1,128]{2,1,0:T(1,128)S(1)}, u32[]{:S(2)}, u32[]{:S(2)}) async-start(f32[256,1,128]{2,1,0:T(1,128)} %bitcast.20), calls=%async_computation | async-start | bytes 262144 | tf_op jit(solution)/shard_map/while/body/eval_jaxpr/all_to_all | solution.py:239
  229.3 10.1 %all-to-all-done = f32[256,1,128]{2,1,0:T(1,128)S(1)} async-done(((f32[256,1,128]{2,1,0:T(1,128)}), f32[256,1,128]{2,1,0:T(1,128)S(1)}, u32[]{:S(2)}, u32[]{:S(2)}) %all-to-all-start) | async-done | bytes 131104 | tf_op jit(solution)/shard_map/while/body/eval_jaxpr/all_to_all | solution.py:239
  249.4 10.1 %all-to-all-done = f32[256,1,128]{2,1,0:T(1,128)S(1)} async-done(((f32[256,1,128]{2,1,0:T(1,128)}), f32[256,1,128]{2,1,0:T(1,128)S(1)}, u32[]{:S(2)}, u32[]{:S(2)}) %all-to-all-start) | async-done | bytes 131104 | tf_op jit(solution)/shard_map/while/body/eval_jaxpr/all_to_all | solution.py:239
  260.8 5.7 %all-to-all-start = ((f32[256,1,128]{2,1,0:T(1,128)}), f32[256,1,128]{2,1,0:T(1,128)S(1)}, u32[]{:S(2)}, u32[]{:S(2)}) async-start(f32[256,1,128]{2,1,0:T(1,128)} %bitcast.20), calls=%async_computation | async-start | bytes 262144 | tf_op jit(solution)/shard_map/while/body/eval_jaxpr/all_to_all | solution.py:239
  269.5 10.1 %all-to-all-done = f32[256,1,128]{2,1,0:T(1,128)S(1)} async-done(((f32[256,1,128]{2,1,0:T(1,128)}), f32[256,1,128]{2,1,0:T(1,128)S(1)}, u32[]{:S(2)}, u32[]{:S(2)}) %all-to-all-start) | async-done | bytes 131104 | tf_op jit(solution)/shard_map/while/body/eval_jaxpr/all_to_all | solution.py:239
  289.6 10.1 %all-to-all-done = f32[256,1,128]{2,1,0:T(1,128)S(1)} async-done(((f32[256,1,128]{2,1,0:T(1,128)}), f32[256,1,128]{2,1,0:T(1,128)S(1)}, u32[]{:S(2)}, u32[]{:S(2)}) %all-to-all-start) | async-done | bytes 131104 | tf_op jit(solution)/shard_map/while/body/eval_jaxpr/all_to_all | solution.py:239
  309.7 10.1 %all-to-all-done = f32[256,1,128]{2,1,0:T(1,128)S(1)} async-done(((f32[256,1,128]{2,1,0:T(1,128)}), f32[256,1,128]{2,1,0:T(1,128)S(1)}, u32[]{:S(2)}, u32[]{:S(2)}) %all-to-all-start) | async-done | bytes 131104 | tf_op jit(solution)/shard_map/while/body/eval_jaxpr/all_to_all | solution.py:239
  321.1 5.7 %all-to-all-start = ((f32[256,1,128]{2,1,0:T(1,128)}), f32[256,1,128]{2,1,0:T(1,128)S(1)}, u32[]{:S(2)}, u32[]{:S(2)}) async-start(f32[256,1,128]{2,1,0:T(1,128)} %bitcast.20), calls=%async_computation | async-start | bytes 262144 | tf_op jit(solution)/shard_map/while/body/eval_jaxpr/all_to_all | solution.py:239
  329.7 10.1 %all-to-all-done = f32[256,1,128]{2,1,0:T(1,128)S(1)} async-done(((f32[256,1,128]{2,1,0:T(1,128)}), f32[256,1,128]{2,1,0:T(1,128)S(1)}, u32[]{:S(2)}, u32[]{:S(2)}) %all-to-all-start) | async-done | bytes 131104 | tf_op jit(solution)/shard_map/while/body/eval_jaxpr/all_to_all | solution.py:239
  341.2 5.7 %all-to-all-start = ((f32[256,1,128]{2,1,0:T(1,128)}), f32[256,1,128]{2,1,0:T(1,128)S(1)}, u32[]{:S(2)}, u32[]{:S(2)}) async-start(f32[256,1,128]{2,1,0:T(1,128)} %bitcast.20), calls=%async_computation | async-start | bytes 262144 | tf_op jit(solution)/shard_map/while/body/eval_jaxpr/all_to_all | solution.py:239
  349.8 10.1 %all-to-all-done = f32[256,1,128]{2,1,0:T(1,128)S(1)} async-done(((f32[256,1,128]{2,1,0:T(1,128)}), f32[256,1,128]{2,1,0:T(1,128)S(1)}, u32[]{:S(2)}, u32[]{:S(2)}) %all-to-all-start) | async-done | bytes 131104 | tf_op jit(solution)/shard_map/while/body/eval_jaxpr/all_to_all | solution.py:239
  369.9 10.1 %all-to-all-done = f32[256,1,128]{2,1,0:T(1,128)S(1)} async-done(((f32[256,1,128]{2,1,0:T(1,128)}), f32[256,1,128]{2,1,0:T(1,128)S(1)}, u32[]{:S(2)}, u32[]{:S(2)}) %all-to-all-start) | async-done | bytes 131104 | tf_op jit(solution)/shard_map/while/body/eval_jaxpr/all_to_all | solution.py:239
  (124 shorter events, 107.7 us)
Async XLA Ops:
  15.6 35.1 %all-to-all-start.2 = ((f32[16,48,768]{2,1,0:T(8,128)}), f32[16,48,768]{2,1,0:T(8,128)S(1)}, u32[]{:S(2)}, u32[]{:S(2)}) async-start(f32[16,48,768]{2,1,0:T(8,128)} %bitcast.19), calls=%async_computation.2 | async-start | bytes 4718592 | tf_op jit(solution)/shard_map/all_to_all | solution.py:234
  19.3 31.3 %copy-start = (f32[14,8,128]{2,1,0:T(8,128)S(1)}, f32[14,8,128]{2,1,0:T(8,128)}, u32[]{:S(2)}) copy-start(f32[14,8,128]{2,1,0:T(8,128)} %constant.23.clone.1) | copy-start | bytes 172036
  19.4 0.7 collective-permute-start
  20.1 0.7 collective-permute-start.1
  20.8 0.7 collective-permute-start.2
  21.5 20.3 %collective-permute-start.3 = (f32[32,768]{1,0:T(8,128)S(1)}, f32[32,768]{1,0:T(8,128)S(1)}, u32[]{:S(2)}, u32[]{:S(2)}) collective-permute-start(f32[32,768]{1,0:T(8,128)S(1)} %add.30), channel_id=1, source_target_pairs={{0,16},{32,48},{64,80},{96,112},{128,144},{160,176},{192,208},{224... | collective-permute-start | bytes 294920 | tf_op jit(solution)/shard_map/ppermute | solution.py:233
  51.9 16.8 %copy-start.1 = (f32[14,8,128]{2,1,0:T(8,128)S(1)}, f32[14,8,128]{2,1,0:T(8,128)}, u32[]{:S(2)}) copy-start(f32[14,8,128]{2,1,0:T(8,128)} %get-tuple-element.232.un_ref) | copy-start | bytes 172036 | tf_op jit(solution)/shard_map/while
  51.9 26.8 %all-to-all-start = ((f32[256,1,128]{2,1,0:T(1,128)}), f32[256,1,128]{2,1,0:T(1,128)S(1)}, u32[]{:S(2)}, u32[]{:S(2)}) async-start(f32[256,1,128]{2,1,0:T(1,128)} %bitcast.20), calls=%async_computation | async-start | bytes 262144 | tf_op jit(solution)/shard_map/while/body/eval_jaxpr/all_to_all | solution.py:239
  80.0 18.8 %all-to-all-start = ((f32[256,1,128]{2,1,0:T(1,128)}), f32[256,1,128]{2,1,0:T(1,128)S(1)}, u32[]{:S(2)}, u32[]{:S(2)}) async-start(f32[256,1,128]{2,1,0:T(1,128)} %bitcast.20), calls=%async_computation | async-start | bytes 262144 | tf_op jit(solution)/shard_map/while/body/eval_jaxpr/all_to_all | solution.py:239
  100.1 8.7 %copy-start.1 = (f32[14,8,128]{2,1,0:T(8,128)S(1)}, f32[14,8,128]{2,1,0:T(8,128)}, u32[]{:S(2)}) copy-start(f32[14,8,128]{2,1,0:T(8,128)} %get-tuple-element.232.un_ref) | copy-start | bytes 172036 | tf_op jit(solution)/shard_map/while
  100.1 18.8 %all-to-all-start = ((f32[256,1,128]{2,1,0:T(1,128)}), f32[256,1,128]{2,1,0:T(1,128)S(1)}, u32[]{:S(2)}, u32[]{:S(2)}) async-start(f32[256,1,128]{2,1,0:T(1,128)} %bitcast.20), calls=%async_computation | async-start | bytes 262144 | tf_op jit(solution)/shard_map/while/body/eval_jaxpr/all_to_all | solution.py:239
  120.2 8.7 %copy-start.1 = (f32[14,8,128]{2,1,0:T(8,128)S(1)}, f32[14,8,128]{2,1,0:T(8,128)}, u32[]{:S(2)}) copy-start(f32[14,8,128]{2,1,0:T(8,128)} %get-tuple-element.232.un_ref) | copy-start | bytes 172036 | tf_op jit(solution)/shard_map/while
  120.2 18.8 %all-to-all-start = ((f32[256,1,128]{2,1,0:T(1,128)}), f32[256,1,128]{2,1,0:T(1,128)S(1)}, u32[]{:S(2)}, u32[]{:S(2)}) async-start(f32[256,1,128]{2,1,0:T(1,128)} %bitcast.20), calls=%async_computation | async-start | bytes 262144 | tf_op jit(solution)/shard_map/while/body/eval_jaxpr/all_to_all | solution.py:239
  140.2 8.7 %copy-start.1 = (f32[14,8,128]{2,1,0:T(8,128)S(1)}, f32[14,8,128]{2,1,0:T(8,128)}, u32[]{:S(2)}) copy-start(f32[14,8,128]{2,1,0:T(8,128)} %get-tuple-element.232.un_ref) | copy-start | bytes 172036 | tf_op jit(solution)/shard_map/while
  140.3 18.8 %all-to-all-start = ((f32[256,1,128]{2,1,0:T(1,128)}), f32[256,1,128]{2,1,0:T(1,128)S(1)}, u32[]{:S(2)}, u32[]{:S(2)}) async-start(f32[256,1,128]{2,1,0:T(1,128)} %bitcast.20), calls=%async_computation | async-start | bytes 262144 | tf_op jit(solution)/shard_map/while/body/eval_jaxpr/all_to_all | solution.py:239
  160.3 8.7 %copy-start.1 = (f32[14,8,128]{2,1,0:T(8,128)S(1)}, f32[14,8,128]{2,1,0:T(8,128)}, u32[]{:S(2)}) copy-start(f32[14,8,128]{2,1,0:T(8,128)} %get-tuple-element.232.un_ref) | copy-start | bytes 172036 | tf_op jit(solution)/shard_map/while
  160.3 18.8 %all-to-all-start = ((f32[256,1,128]{2,1,0:T(1,128)}), f32[256,1,128]{2,1,0:T(1,128)S(1)}, u32[]{:S(2)}, u32[]{:S(2)}) async-start(f32[256,1,128]{2,1,0:T(1,128)} %bitcast.20), calls=%async_computation | async-start | bytes 262144 | tf_op jit(solution)/shard_map/while/body/eval_jaxpr/all_to_all | solution.py:239
  180.4 8.7 %copy-start.1 = (f32[14,8,128]{2,1,0:T(8,128)S(1)}, f32[14,8,128]{2,1,0:T(8,128)}, u32[]{:S(2)}) copy-start(f32[14,8,128]{2,1,0:T(8,128)} %get-tuple-element.232.un_ref) | copy-start | bytes 172036 | tf_op jit(solution)/shard_map/while
  180.4 18.8 %all-to-all-start = ((f32[256,1,128]{2,1,0:T(1,128)}), f32[256,1,128]{2,1,0:T(1,128)S(1)}, u32[]{:S(2)}, u32[]{:S(2)}) async-start(f32[256,1,128]{2,1,0:T(1,128)} %bitcast.20), calls=%async_computation | async-start | bytes 262144 | tf_op jit(solution)/shard_map/while/body/eval_jaxpr/all_to_all | solution.py:239
  200.5 18.8 %all-to-all-start = ((f32[256,1,128]{2,1,0:T(1,128)}), f32[256,1,128]{2,1,0:T(1,128)S(1)}, u32[]{:S(2)}, u32[]{:S(2)}) async-start(f32[256,1,128]{2,1,0:T(1,128)} %bitcast.20), calls=%async_computation | async-start | bytes 262144 | tf_op jit(solution)/shard_map/while/body/eval_jaxpr/all_to_all | solution.py:239
  220.6 8.7 %copy-start.1 = (f32[14,8,128]{2,1,0:T(8,128)S(1)}, f32[14,8,128]{2,1,0:T(8,128)}, u32[]{:S(2)}) copy-start(f32[14,8,128]{2,1,0:T(8,128)} %get-tuple-element.232.un_ref) | copy-start | bytes 172036 | tf_op jit(solution)/shard_map/while
  220.6 18.8 %all-to-all-start = ((f32[256,1,128]{2,1,0:T(1,128)}), f32[256,1,128]{2,1,0:T(1,128)S(1)}, u32[]{:S(2)}, u32[]{:S(2)}) async-start(f32[256,1,128]{2,1,0:T(1,128)} %bitcast.20), calls=%async_computation | async-start | bytes 262144 | tf_op jit(solution)/shard_map/while/body/eval_jaxpr/all_to_all | solution.py:239
  240.7 18.8 %all-to-all-start = ((f32[256,1,128]{2,1,0:T(1,128)}), f32[256,1,128]{2,1,0:T(1,128)S(1)}, u32[]{:S(2)}, u32[]{:S(2)}) async-start(f32[256,1,128]{2,1,0:T(1,128)} %bitcast.20), calls=%async_computation | async-start | bytes 262144 | tf_op jit(solution)/shard_map/while/body/eval_jaxpr/all_to_all | solution.py:239
  260.8 8.7 %copy-start.1 = (f32[14,8,128]{2,1,0:T(8,128)S(1)}, f32[14,8,128]{2,1,0:T(8,128)}, u32[]{:S(2)}) copy-start(f32[14,8,128]{2,1,0:T(8,128)} %get-tuple-element.232.un_ref) | copy-start | bytes 172036 | tf_op jit(solution)/shard_map/while
  260.8 18.8 %all-to-all-start = ((f32[256,1,128]{2,1,0:T(1,128)}), f32[256,1,128]{2,1,0:T(1,128)S(1)}, u32[]{:S(2)}, u32[]{:S(2)}) async-start(f32[256,1,128]{2,1,0:T(1,128)} %bitcast.20), calls=%async_computation | async-start | bytes 262144 | tf_op jit(solution)/shard_map/while/body/eval_jaxpr/all_to_all | solution.py:239
  280.9 18.8 %all-to-all-start = ((f32[256,1,128]{2,1,0:T(1,128)}), f32[256,1,128]{2,1,0:T(1,128)S(1)}, u32[]{:S(2)}, u32[]{:S(2)}) async-start(f32[256,1,128]{2,1,0:T(1,128)} %bitcast.20), calls=%async_computation | async-start | bytes 262144 | tf_op jit(solution)/shard_map/while/body/eval_jaxpr/all_to_all | solution.py:239
  301.0 18.8 %all-to-all-start = ((f32[256,1,128]{2,1,0:T(1,128)}), f32[256,1,128]{2,1,0:T(1,128)S(1)}, u32[]{:S(2)}, u32[]{:S(2)}) async-start(f32[256,1,128]{2,1,0:T(1,128)} %bitcast.20), calls=%async_computation | async-start | bytes 262144 | tf_op jit(solution)/shard_map/while/body/eval_jaxpr/all_to_all | solution.py:239
  321.1 18.8 %all-to-all-start = ((f32[256,1,128]{2,1,0:T(1,128)}), f32[256,1,128]{2,1,0:T(1,128)S(1)}, u32[]{:S(2)}, u32[]{:S(2)}) async-start(f32[256,1,128]{2,1,0:T(1,128)} %bitcast.20), calls=%async_computation | async-start | bytes 262144 | tf_op jit(solution)/shard_map/while/body/eval_jaxpr/all_to_all | solution.py:239
  341.2 8.7 %copy-start.1 = (f32[14,8,128]{2,1,0:T(8,128)S(1)}, f32[14,8,128]{2,1,0:T(8,128)}, u32[]{:S(2)}) copy-start(f32[14,8,128]{2,1,0:T(8,128)} %get-tuple-element.232.un_ref) | copy-start | bytes 172036 | tf_op jit(solution)/shard_map/while
  341.2 18.8 %all-to-all-start = ((f32[256,1,128]{2,1,0:T(1,128)}), f32[256,1,128]{2,1,0:T(1,128)S(1)}, u32[]{:S(2)}, u32[]{:S(2)}) async-start(f32[256,1,128]{2,1,0:T(1,128)} %bitcast.20), calls=%async_computation | async-start | bytes 262144 | tf_op jit(solution)/shard_map/while/body/eval_jaxpr/all_to_all | solution.py:239
  361.2 8.7 %copy-start.1 = (f32[14,8,128]{2,1,0:T(8,128)S(1)}, f32[14,8,128]{2,1,0:T(8,128)}, u32[]{:S(2)}) copy-start(f32[14,8,128]{2,1,0:T(8,128)} %get-tuple-element.232.un_ref) | copy-start | bytes 172036 | tf_op jit(solution)/shard_map/while
  361.2 18.8 %all-to-all-start = ((f32[256,1,128]{2,1,0:T(1,128)}), f32[256,1,128]{2,1,0:T(1,128)S(1)}, u32[]{:S(2)}, u32[]{:S(2)}) async-start(f32[256,1,128]{2,1,0:T(1,128)} %bitcast.20), calls=%async_computation | async-start | bytes 262144 | tf_op jit(solution)/shard_map/while/body/eval_jaxpr/all_to_all | solution.py:239
  (6 other events, 52.0 us)

commit v4 on v3

--- a/solution.py
+++ b/solution.py
@@ -58,11 +58,8 @@
     return jnp.sum(jnp.where(iota((OWN, LANES), 1) == k, head, 0.0), axis=1, keepdims=True)
 
 
-def begin_body(top_ref, out_ref, hist_ref, tmp, zero, sem):
-    zero[...] = jnp.zeros(zero.shape, jnp.float32)
-    clear = [pltpu.make_async_copy(zero, hist_ref.at[n], sem.at[n]) for n in range(2)]
-    for copy in clear:
-        copy.start()
+def begin_body(top_ref, out_ref, hist_ref, tmp):
+    del hist_ref
     lane = iota((8, LANES), 1)
     for t in range(6):
         tmp[32 * t : 32 * (t + 1), :] = top_ref[:, LANES * t : LANES * (t + 1)]
@@ -79,9 +76,6 @@
         for q in range(8):
             mine = ((lane - OWN * q) & (LANES - 1)) < OWN
             out_ref[pl.ds(8 * gm + q, 8, stride=32), :] = jnp.where(mine, rows[0][q], pltpu.roll(rows[1][q], OWN, 1))
-    for copy in clear:
-        copy.wait()
-
 
 def image_of(got_ref, h_ref, u, scale):
     y = unpack(lambda first: got_ref[pl.ds(first, 8, stride=32), :])
@@ -148,8 +142,9 @@
         hist[0, row, m] = u_ref[m]
         hist[1, row, m] = w_ref[m]
     for i in range(PANEL_COLUMNS):
-        v = [hist[0, i, m] for m in range(TILES)]
-        w = [hist[1, i, m] for m in range(TILES)]
+        kept = i < j
+        v = [jnp.where(kept, hist[0, i, m], 0.0) for m in range(TILES)]
+        w = [jnp.where(kept, hist[1, i, m], 0.0) for m in range(TILES)]
         vu = total(tree_sum(v[m] * un[m] for m in range(TILES)))
         wu = total(tree_sum(w[m] * un[m] for m in range(TILES)))
         vj = jnp.sum(jnp.where(lane1 == j + 1, v[0][0:1, :], 0.0), axis=1, keepdims=True)
@@ -164,11 +159,12 @@
     keep_w.wait()
 
 
-def last_body(own, got_ref, h_ref, u_ref, hist_ref, matrix_ref, updated_ref, whole_ref, hist, block, whole, sides, sems):
+def last_body(own, got_ref, h_ref, u_ref, hist_ref, matrix_ref, updated_ref, whole_ref, coef_ref, hist, block, whole, sides, sems):
     read_hist = pltpu.make_async_copy(hist_ref, hist, sems.at[0])
     read_block = pltpu.make_async_copy(matrix_ref, block, sems.at[1])
     read_hist.start()
     read_block.start()
+    coef_ref[...] = u_ref[COEF, 0:2, 0:PANEL_COLUMNS]
     u = [u_ref[m] for m in range(TILES)]
     p, kappa = image_of(got_ref, h_ref, u, u_ref[SCALE, 0:1, 0:1])
     read_hist.wait()
@@ -224,16 +220,14 @@
     devices = ways * lax.axis_size("row")
     tile_cols = matrix.shape[1]
     own = jnp.stack([r, c])
-    top = lax.all_to_all(
-        jnp.broadcast_to(matrix[:2], (ways, 2, tile_cols)), "col", split_axis=0, concat_axis=0, tiled=True
-    ).reshape(2 * ways, tile_cols)
-    top, matrix_after = lax.optimization_barrier((top, matrix))
-    top = jnp.where(r == 0, top, 0.0)
+    rows = lax.all_to_all(
+        matrix.reshape(ways, OWN, tile_cols), "col", split_axis=0, concat_axis=0, tiled=True
+    )
+    top = jnp.where(r == 0, matrix[:2], 0.0)
     for far in (8, 4, 2, 1):
         top = top + lax.ppermute(top, "row", [(n, n + far) for n in range(0, 16, 2 * far)])
-    rows = lax.all_to_all(
-        matrix_after.reshape(ways, OWN, tile_cols), "col", split_axis=0, concat_axis=0, tiled=True
-    )
+    rows, top = lax.optimization_barrier((rows, jnp.broadcast_to(top, (ways, 2, tile_cols))))
+    top = lax.all_to_all(top, "col", split_axis=0, concat_axis=0, tiled=True).reshape(2 * ways, tile_cols)
 
     def exchange(packed):
         return lax.all_to_all(packed, ("row", "col"), split_axis=0, concat_axis=0, tiled=True)
@@ -251,8 +245,6 @@
         out_specs=(VMEM, ANY),
         scratch_shapes=[
             pltpu.VMEM((192, LANES), f32),
-            pltpu.VMEM(hist.shape[1:], f32),
-            pltpu.SemaphoreType.DMA((2,)),
         ],
         name="begin",
     )
@@ -275,9 +267,9 @@
     )
     last = pl.pallas_call(
         last_body,
-        out_shape=(shape(*matrix.shape), shape(PANEL_COLUMNS, order)),
+        out_shape=(shape(*matrix.shape), shape(PANEL_COLUMNS, order), shape(2, PANEL_COLUMNS)),
         in_specs=[SMEM] + [VMEM] * 3 + [ANY] * 2,
-        out_specs=(ANY, ANY),
+        out_specs=(ANY, ANY, VMEM),
         scratch_shapes=[
             pltpu.VMEM((2, PANEL_COLUMNS * TILES * 8, LANES), f32),
             pltpu.VMEM(matrix.shape, f32),
@@ -303,8 +295,7 @@
     got, kept = begin(top)
     state = (got, zeros(vec), zeros(vec), u, kept)
     got, _, h, u, kept = lax.fori_loop(0, PANEL_COLUMNS, one_column, state)
-    updated, whole = last(own, got, h, u, kept.reshape(2, -1, LANES), matrix)
-    return updated, whole, u[COEF, :2, :PANEL_COLUMNS]
+    return last(own, got, h, u, kept.reshape(2, -1, LANES), matrix)
 
 
 def solution(mesh):

time: 388 us -> 392 us (1.010)
  blocking collectives: 14.1 us -> 0 us
  local copies, waits for them, and re-layouts: 1.72 us -> 14.7 us
  starting transfers between devices: 106 us -> 111 us
  waiting for transfers between devices: 186 us -> 181 us
    all_to_all x16, waiting for transfers between devices: 162 us -> 145 us  [exchange(): lax.all_to_all(packed, ('row', 'col'), split_axis=0, concat_axis=0, tiled...]
    all_to_all x1 -> x2, waiting for transfers between devices: 6.02 us -> 20.8 us  [the longest x1 14.9 us: per_device(): lax.all_to_all(matrix.reshape(ways, OWN, tile_cols), 'col', split_axis=0,...]
    all_to_all x1 -> x0, blocking collectives: 14.1 us -> none  [per_device(): lax.all_to_all(jnp.broadcast_to(matrix[:2], (ways, 2, tile_cols)), 'col',...]
    while x64 -> x32, local copies, waits for them, and re-layouts: 0.3 us -> 13.3 us
    all_to_all x1 -> x2, starting transfers between devices: 3.74 us -> 11.2 us  [the longest x1 7.72 us: per_device(): lax.all_to_all(matrix.reshape(ways, OWN, tile_cols), 'col', split_axis=0,...]
  transfers between devices with their start and end apart: 21 -> 22, of which waited for: 18 -> 19; matrix products, arithmetic and copies ran while one was open for 0% -> 4% of each run, Pallas kernels for 13% -> 13%
where the time goes in v4:
time: 392 us; the launch traced here: 388 us
  waiting for transfers between devices  181 us (46%)
  starting transfers between devices  111 us (28%)
  Pallas kernels  78.3 us (20%)
  local copies, waits for them, and re-layouts  14.7 us (4%)
    all_to_all x16, waiting for transfers between devices, exchange(): lax.all_to_all(packed, ('row', 'col'), split_axis=0, concat_axis=0, tiled...  145 us
    all_to_all x16, starting transfers between devices, exchange(): lax.all_to_all(packed, ('row', 'col'), split_axis=0, concat_axis=0, tiled...  96.3 us
    pallas_call x16, Pallas kernels, one_column(): base, h, kept = history(col, got, w, u, un, kept)  51.7 us
    pallas_call x16, Pallas kernels, one_column(): w, un, out = step(col, got, base, h, u, rows)  20.1 us
    ppermute x4, waiting for transfers between devices, per_device(): lax.ppermute(top, 'row', [(n, n + far) for n in range(0, 16, 2 * far)])  15.2 us
    all_to_all x1, waiting for transfers between devices, per_device(): lax.all_to_all(matrix.reshape(ways, OWN, tile_cols), 'col', split_axis=0,...  14.9 us
    while x32, local copies, waits for them, and re-layouts  13.3 us
  transfers between devices with their start and end apart: 22, of which 19 were waited for; matrix products, arithmetic and copies ran while one was open for 4% of the time, Pallas kernels for 13%

profile of v4, /device:TPU:1, one launch (start us, length us, event | category | flops | bytes accessed | tf_op | source)
XLA Modules:
  0.0 388.4 jit_solution(16521498570089182543)
XLA Ops:
  0.6 7.7 %all-to-all-start.1 = ((f32[16,48,768]{2,1,0:T(8,128)}), f32[16,48,768]{2,1,0:T(8,128)S(1)}, u32[]{:S(2)}, u32[]{:S(2)}) async-start(f32[16,48,768]{2,1,0:T(8,128)} %bitcast.17), calls=%async_computation.1 | async-start | bytes 4718592 | tf_op jit(solution)/shard_map/all_to_all | solution.py:223
  13.2 15.2 %collective-permute-done.3 = f32[2,768]{1,0:T(2,128)S(1)} collective-permute-done((f32[2,768]{1,0:T(2,128)S(1)}, f32[2,768]{1,0:T(2,128)S(1)}, u32[]{:S(2)}, u32[]{:S(2)}) %collective-permute-start.3) | collective-permute-done | bytes 6176 | tf_op jit(solution)/shard_map/ppermute | solution.py:228
  28.4 14.9 %all-to-all-done.1 = f32[16,48,768]{2,1,0:T(8,128)S(1)} async-done(((f32[16,48,768]{2,1,0:T(8,128)}), f32[16,48,768]{2,1,0:T(8,128)S(1)}, u32[]{:S(2)}, u32[]{:S(2)}) %all-to-all-start.1) | async-done | bytes 2359328 | tf_op jit(solution)/shard_map/all_to_all | solution.py:223
  48.1 6.0 %all-to-all-done.2 = f32[16,2,768]{2,1,0:T(2,128)S(1)} async-done(((f32[16,2,768]{2,1,0:T(2,128)}), f32[16,2,768]{2,1,0:T(2,128)S(1)}, u32[]{:S(2)}, u32[]{:S(2)}) %all-to-all-start.2) | async-done | bytes 98336 | tf_op jit(solution)/shard_map/all_to_all | solution.py:230
  55.9 327.1 %while.21 = (s32[]{:T(128)}, f32[256,128]{1,0:T(8,128)S(1)}, f32[12,8,128]{2,1,0:T(8,128)S(1)}, f32[12,8,128]{2,1,0:T(8,128)S(1)}, f32[14,8,128]{2,1,0:T(8,128)S...) while((s32[]{:T(128)}, f32[256,128]{1,0:T(8,128)S(1)}, ...), condition=%wide.region_1.2_spmd, body=%wide.region_0.1_spmd.sunk | while | flops 2 | bytes 770173 | solution.py:297
  57.1 13.5 %all-to-all-start = ((f32[256,1,128]{2,1,0:T(1,128)}), f32[256,1,128]{2,1,0:T(1,128)S(1)}, u32[]{:S(2)}, u32[]{:S(2)}) async-start(f32[256,1,128]{2,1,0:T(1,128)} %bitcast.18), calls=%async_computation | async-start | bytes 262144 | tf_op jit(solution)/shard_map/while/body/eval_jaxpr/all_to_all | solution.py:233
  74.7 8.9 %all-to-all-done = f32[256,1,128]{2,1,0:T(1,128)S(1)} async-done(((f32[256,1,128]{2,1,0:T(1,128)}), f32[256,1,128]{2,1,0:T(1,128)S(1)}, u32[]{:S(2)}, u32[]{:S(2)}) %all-to-all-start) | async-done | bytes 131104 | tf_op jit(solution)/shard_map/while/body/eval_jaxpr/all_to_all | solution.py:233
  84.9 5.5 %all-to-all-start = ((f32[256,1,128]{2,1,0:T(1,128)}), f32[256,1,128]{2,1,0:T(1,128)S(1)}, u32[]{:S(2)}, u32[]{:S(2)}) async-start(f32[256,1,128]{2,1,0:T(1,128)} %bitcast.18), calls=%async_computation | async-start | bytes 262144 | tf_op jit(solution)/shard_map/while/body/eval_jaxpr/all_to_all | solution.py:233
  94.5 9.1 %all-to-all-done = f32[256,1,128]{2,1,0:T(1,128)S(1)} async-done(((f32[256,1,128]{2,1,0:T(1,128)}), f32[256,1,128]{2,1,0:T(1,128)S(1)}, u32[]{:S(2)}, u32[]{:S(2)}) %all-to-all-start) | async-done | bytes 131104 | tf_op jit(solution)/shard_map/while/body/eval_jaxpr/all_to_all | solution.py:233
  104.8 5.5 %all-to-all-start = ((f32[256,1,128]{2,1,0:T(1,128)}), f32[256,1,128]{2,1,0:T(1,128)S(1)}, u32[]{:S(2)}, u32[]{:S(2)}) async-start(f32[256,1,128]{2,1,0:T(1,128)} %bitcast.18), calls=%async_computation | async-start | bytes 262144 | tf_op jit(solution)/shard_map/while/body/eval_jaxpr/all_to_all | solution.py:233
  114.5 9.1 %all-to-all-done = f32[256,1,128]{2,1,0:T(1,128)S(1)} async-done(((f32[256,1,128]{2,1,0:T(1,128)}), f32[256,1,128]{2,1,0:T(1,128)S(1)}, u32[]{:S(2)}, u32[]{:S(2)}) %all-to-all-start) | async-done | bytes 131104 | tf_op jit(solution)/shard_map/while/body/eval_jaxpr/all_to_all | solution.py:233
  124.8 5.5 %all-to-all-start = ((f32[256,1,128]{2,1,0:T(1,128)}), f32[256,1,128]{2,1,0:T(1,128)S(1)}, u32[]{:S(2)}, u32[]{:S(2)}) async-start(f32[256,1,128]{2,1,0:T(1,128)} %bitcast.18), calls=%async_computation | async-start | bytes 262144 | tf_op jit(solution)/shard_map/while/body/eval_jaxpr/all_to_all | solution.py:233
  134.4 9.1 %all-to-all-done = f32[256,1,128]{2,1,0:T(1,128)S(1)} async-done(((f32[256,1,128]{2,1,0:T(1,128)}), f32[256,1,128]{2,1,0:T(1,128)S(1)}, u32[]{:S(2)}, u32[]{:S(2)}) %all-to-all-start) | async-done | bytes 131104 | tf_op jit(solution)/shard_map/while/body/eval_jaxpr/all_to_all | solution.py:233
  144.8 5.5 %all-to-all-start = ((f32[256,1,128]{2,1,0:T(1,128)}), f32[256,1,128]{2,1,0:T(1,128)S(1)}, u32[]{:S(2)}, u32[]{:S(2)}) async-start(f32[256,1,128]{2,1,0:T(1,128)} %bitcast.18), calls=%async_computation | async-start | bytes 262144 | tf_op jit(solution)/shard_map/while/body/eval_jaxpr/all_to_all | solution.py:233
  154.4 9.1 %all-to-all-done = f32[256,1,128]{2,1,0:T(1,128)S(1)} async-done(((f32[256,1,128]{2,1,0:T(1,128)}), f32[256,1,128]{2,1,0:T(1,128)S(1)}, u32[]{:S(2)}, u32[]{:S(2)}) %all-to-all-start) | async-done | bytes 131104 | tf_op jit(solution)/shard_map/while/body/eval_jaxpr/all_to_all | solution.py:233
  164.7 5.5 %all-to-all-start = ((f32[256,1,128]{2,1,0:T(1,128)}), f32[256,1,128]{2,1,0:T(1,128)S(1)}, u32[]{:S(2)}, u32[]{:S(2)}) async-start(f32[256,1,128]{2,1,0:T(1,128)} %bitcast.18), calls=%async_computation | async-start | bytes 262144 | tf_op jit(solution)/shard_map/while/body/eval_jaxpr/all_to_all | solution.py:233
  174.3 9.1 %all-to-all-done = f32[256,1,128]{2,1,0:T(1,128)S(1)} async-done(((f32[256,1,128]{2,1,0:T(1,128)}), f32[256,1,128]{2,1,0:T(1,128)S(1)}, u32[]{:S(2)}, u32[]{:S(2)}) %all-to-all-start) | async-done | bytes 131104 | tf_op jit(solution)/shard_map/while/body/eval_jaxpr/all_to_all | solution.py:233
  184.7 5.5 %all-to-all-start = ((f32[256,1,128]{2,1,0:T(1,128)}), f32[256,1,128]{2,1,0:T(1,128)S(1)}, u32[]{:S(2)}, u32[]{:S(2)}) async-start(f32[256,1,128]{2,1,0:T(1,128)} %bitcast.18), calls=%async_computation | async-start | bytes 262144 | tf_op jit(solution)/shard_map/while/body/eval_jaxpr/all_to_all | solution.py:233
  194.3 9.1 %all-to-all-done = f32[256,1,128]{2,1,0:T(1,128)S(1)} async-done(((f32[256,1,128]{2,1,0:T(1,128)}), f32[256,1,128]{2,1,0:T(1,128)S(1)}, u32[]{:S(2)}, u32[]{:S(2)}) %all-to-all-start) | async-done | bytes 131104 | tf_op jit(solution)/shard_map/while/body/eval_jaxpr/all_to_all | solution.py:233
  214.2 9.1 %all-to-all-done = f32[256,1,128]{2,1,0:T(1,128)S(1)} async-done(((f32[256,1,128]{2,1,0:T(1,128)}), f32[256,1,128]{2,1,0:T(1,128)S(1)}, u32[]{:S(2)}, u32[]{:S(2)}) %all-to-all-start) | async-done | bytes 131104 | tf_op jit(solution)/shard_map/while/body/eval_jaxpr/all_to_all | solution.py:233
  224.6 5.5 %all-to-all-start = ((f32[256,1,128]{2,1,0:T(1,128)}), f32[256,1,128]{2,1,0:T(1,128)S(1)}, u32[]{:S(2)}, u32[]{:S(2)}) async-start(f32[256,1,128]{2,1,0:T(1,128)} %bitcast.18), calls=%async_computation | async-start | bytes 262144 | tf_op jit(solution)/shard_map/while/body/eval_jaxpr/all_to_all | solution.py:233
  234.2 9.1 %all-to-all-done = f32[256,1,128]{2,1,0:T(1,128)S(1)} async-done(((f32[256,1,128]{2,1,0:T(1,128)}), f32[256,1,128]{2,1,0:T(1,128)S(1)}, u32[]{:S(2)}, u32[]{:S(2)}) %all-to-all-start) | async-done | bytes 131104 | tf_op jit(solution)/shard_map/while/body/eval_jaxpr/all_to_all | solution.py:233
  254.2 9.1 %all-to-all-done = f32[256,1,128]{2,1,0:T(1,128)S(1)} async-done(((f32[256,1,128]{2,1,0:T(1,128)}), f32[256,1,128]{2,1,0:T(1,128)S(1)}, u32[]{:S(2)}, u32[]{:S(2)}) %all-to-all-start) | async-done | bytes 131104 | tf_op jit(solution)/shard_map/while/body/eval_jaxpr/all_to_all | solution.py:233
  264.5 5.5 %all-to-all-start = ((f32[256,1,128]{2,1,0:T(1,128)}), f32[256,1,128]{2,1,0:T(1,128)S(1)}, u32[]{:S(2)}, u32[]{:S(2)}) async-start(f32[256,1,128]{2,1,0:T(1,128)} %bitcast.18), calls=%async_computation | async-start | bytes 262144 | tf_op jit(solution)/shard_map/while/body/eval_jaxpr/all_to_all | solution.py:233
  274.1 9.1 %all-to-all-done = f32[256,1,128]{2,1,0:T(1,128)S(1)} async-done(((f32[256,1,128]{2,1,0:T(1,128)}), f32[256,1,128]{2,1,0:T(1,128)S(1)}, u32[]{:S(2)}, u32[]{:S(2)}) %all-to-all-start) | async-done | bytes 131104 | tf_op jit(solution)/shard_map/while/body/eval_jaxpr/all_to_all | solution.py:233
  284.5 5.5 %all-to-all-start = ((f32[256,1,128]{2,1,0:T(1,128)}), f32[256,1,128]{2,1,0:T(1,128)S(1)}, u32[]{:S(2)}, u32[]{:S(2)}) async-start(f32[256,1,128]{2,1,0:T(1,128)} %bitcast.18), calls=%async_computation | async-start | bytes 262144 | tf_op jit(solution)/shard_map/while/body/eval_jaxpr/all_to_all | solution.py:233
  294.1 9.1 %all-to-all-done = f32[256,1,128]{2,1,0:T(1,128)S(1)} async-done(((f32[256,1,128]{2,1,0:T(1,128)}), f32[256,1,128]{2,1,0:T(1,128)S(1)}, u32[]{:S(2)}, u32[]{:S(2)}) %all-to-all-start) | async-done | bytes 131104 | tf_op jit(solution)/shard_map/while/body/eval_jaxpr/all_to_all | solution.py:233
  314.0 9.1 %all-to-all-done = f32[256,1,128]{2,1,0:T(1,128)S(1)} async-done(((f32[256,1,128]{2,1,0:T(1,128)}), f32[256,1,128]{2,1,0:T(1,128)S(1)}, u32[]{:S(2)}, u32[]{:S(2)}) %all-to-all-start) | async-done | bytes 131104 | tf_op jit(solution)/shard_map/while/body/eval_jaxpr/all_to_all | solution.py:233
  324.4 5.5 %all-to-all-start = ((f32[256,1,128]{2,1,0:T(1,128)}), f32[256,1,128]{2,1,0:T(1,128)S(1)}, u32[]{:S(2)}, u32[]{:S(2)}) async-start(f32[256,1,128]{2,1,0:T(1,128)} %bitcast.18), calls=%async_computation | async-start | bytes 262144 | tf_op jit(solution)/shard_map/while/body/eval_jaxpr/all_to_all | solution.py:233
  334.0 9.1 %all-to-all-done = f32[256,1,128]{2,1,0:T(1,128)S(1)} async-done(((f32[256,1,128]{2,1,0:T(1,128)}), f32[256,1,128]{2,1,0:T(1,128)S(1)}, u32[]{:S(2)}, u32[]{:S(2)}) %all-to-all-start) | async-done | bytes 131104 | tf_op jit(solution)/shard_map/while/body/eval_jaxpr/all_to_all | solution.py:233
  354.0 9.1 %all-to-all-done = f32[256,1,128]{2,1,0:T(1,128)S(1)} async-done(((f32[256,1,128]{2,1,0:T(1,128)}), f32[256,1,128]{2,1,0:T(1,128)S(1)}, u32[]{:S(2)}, u32[]{:S(2)}) %all-to-all-start) | async-done | bytes 131104 | tf_op jit(solution)/shard_map/while/body/eval_jaxpr/all_to_all | solution.py:233
  373.9 9.1 %all-to-all-done = f32[256,1,128]{2,1,0:T(1,128)S(1)} async-done(((f32[256,1,128]{2,1,0:T(1,128)}), f32[256,1,128]{2,1,0:T(1,128)S(1)}, u32[]{:S(2)}, u32[]{:S(2)}) %all-to-all-start) | async-done | bytes 131104 | tf_op jit(solution)/shard_map/while/body/eval_jaxpr/all_to_all | solution.py:233
  (91 shorter events, 129.5 us)
Async XLA Ops:
  0.6 55.2 %copy-start = (f32[14,8,128]{2,1,0:T(8,128)S(1)}, f32[14,8,128]{2,1,0:T(8,128)}, u32[]{:S(2)}) copy-start(f32[14,8,128]{2,1,0:T(8,128)} %constant.23.clone.1) | copy-start | bytes 172036
  0.6 42.6 %all-to-all-start.1 = ((f32[16,48,768]{2,1,0:T(8,128)}), f32[16,48,768]{2,1,0:T(8,128)S(1)}, u32[]{:S(2)}, u32[]{:S(2)}) async-start(f32[16,48,768]{2,1,0:T(8,128)} %bitcast.17), calls=%async_computation.1 | async-start | bytes 4718592 | tf_op jit(solution)/shard_map/all_to_all | solution.py:223
  9.1 0.7 collective-permute-start
  10.5 0.7 collective-permute-start.1
  11.2 0.7 collective-permute-start.2
  11.9 16.5 %collective-permute-start.3 = (f32[2,768]{1,0:T(2,128)S(1)}, f32[2,768]{1,0:T(2,128)S(1)}, u32[]{:S(2)}, u32[]{:S(2)}) collective-permute-start(f32[2,768]{1,0:T(2,128)S(1)} %add.30), channel_id=1, source_target_pairs={{0,16},{32,48},{64,80},{96,112},{128,144},{160,176},{192,208},{224... | collective-permute-start | bytes 18440 | tf_op jit(solution)/shard_map/ppermute | solution.py:228
  43.9 10.1 %all-to-all-start.2 = ((f32[16,2,768]{2,1,0:T(2,128)}), f32[16,2,768]{2,1,0:T(2,128)S(1)}, u32[]{:S(2)}, u32[]{:S(2)}) async-start(f32[16,2,768]{2,1,0:T(2,128)} %broadcast_in_dim.8), calls=%async_computation.2 | async-start | bytes 196608 | tf_op jit(solution)/shard_map/all_to_all | solution.py:230
  57.1 26.5 %all-to-all-start = ((f32[256,1,128]{2,1,0:T(1,128)}), f32[256,1,128]{2,1,0:T(1,128)S(1)}, u32[]{:S(2)}, u32[]{:S(2)}) async-start(f32[256,1,128]{2,1,0:T(1,128)} %bitcast.18), calls=%async_computation | async-start | bytes 262144 | tf_op jit(solution)/shard_map/while/body/eval_jaxpr/all_to_all | solution.py:233
  84.9 18.7 %all-to-all-start = ((f32[256,1,128]{2,1,0:T(1,128)}), f32[256,1,128]{2,1,0:T(1,128)S(1)}, u32[]{:S(2)}, u32[]{:S(2)}) async-start(f32[256,1,128]{2,1,0:T(1,128)} %bitcast.18), calls=%async_computation | async-start | bytes 262144 | tf_op jit(solution)/shard_map/while/body/eval_jaxpr/all_to_all | solution.py:233
  104.8 18.7 %all-to-all-start = ((f32[256,1,128]{2,1,0:T(1,128)}), f32[256,1,128]{2,1,0:T(1,128)S(1)}, u32[]{:S(2)}, u32[]{:S(2)}) async-start(f32[256,1,128]{2,1,0:T(1,128)} %bitcast.18), calls=%async_computation | async-start | bytes 262144 | tf_op jit(solution)/shard_map/while/body/eval_jaxpr/all_to_all | solution.py:233
  124.8 18.7 %all-to-all-start = ((f32[256,1,128]{2,1,0:T(1,128)}), f32[256,1,128]{2,1,0:T(1,128)S(1)}, u32[]{:S(2)}, u32[]{:S(2)}) async-start(f32[256,1,128]{2,1,0:T(1,128)} %bitcast.18), calls=%async_computation | async-start | bytes 262144 | tf_op jit(solution)/shard_map/while/body/eval_jaxpr/all_to_all | solution.py:233
  144.8 18.7 %all-to-all-start = ((f32[256,1,128]{2,1,0:T(1,128)}), f32[256,1,128]{2,1,0:T(1,128)S(1)}, u32[]{:S(2)}, u32[]{:S(2)}) async-start(f32[256,1,128]{2,1,0:T(1,128)} %bitcast.18), calls=%async_computation | async-start | bytes 262144 | tf_op jit(solution)/shard_map/while/body/eval_jaxpr/all_to_all | solution.py:233
  164.7 18.7 %all-to-all-start = ((f32[256,1,128]{2,1,0:T(1,128)}), f32[256,1,128]{2,1,0:T(1,128)S(1)}, u32[]{:S(2)}, u32[]{:S(2)}) async-start(f32[256,1,128]{2,1,0:T(1,128)} %bitcast.18), calls=%async_computation | async-start | bytes 262144 | tf_op jit(solution)/shard_map/while/body/eval_jaxpr/all_to_all | solution.py:233
  184.7 18.7 %all-to-all-start = ((f32[256,1,128]{2,1,0:T(1,128)}), f32[256,1,128]{2,1,0:T(1,128)S(1)}, u32[]{:S(2)}, u32[]{:S(2)}) async-start(f32[256,1,128]{2,1,0:T(1,128)} %bitcast.18), calls=%async_computation | async-start | bytes 262144 | tf_op jit(solution)/shard_map/while/body/eval_jaxpr/all_to_all | solution.py:233
  204.6 18.7 %all-to-all-start = ((f32[256,1,128]{2,1,0:T(1,128)}), f32[256,1,128]{2,1,0:T(1,128)S(1)}, u32[]{:S(2)}, u32[]{:S(2)}) async-start(f32[256,1,128]{2,1,0:T(1,128)} %bitcast.18), calls=%async_computation | async-start | bytes 262144 | tf_op jit(solution)/shard_map/while/body/eval_jaxpr/all_to_all | solution.py:233
  224.6 18.7 %all-to-all-start = ((f32[256,1,128]{2,1,0:T(1,128)}), f32[256,1,128]{2,1,0:T(1,128)S(1)}, u32[]{:S(2)}, u32[]{:S(2)}) async-start(f32[256,1,128]{2,1,0:T(1,128)} %bitcast.18), calls=%async_computation | async-start | bytes 262144 | tf_op jit(solution)/shard_map/while/body/eval_jaxpr/all_to_all | solution.py:233
  244.6 18.7 %all-to-all-start = ((f32[256,1,128]{2,1,0:T(1,128)}), f32[256,1,128]{2,1,0:T(1,128)S(1)}, u32[]{:S(2)}, u32[]{:S(2)}) async-start(f32[256,1,128]{2,1,0:T(1,128)} %bitcast.18), calls=%async_computation | async-start | bytes 262144 | tf_op jit(solution)/shard_map/while/body/eval_jaxpr/all_to_all | solution.py:233
  264.5 18.7 %all-to-all-start = ((f32[256,1,128]{2,1,0:T(1,128)}), f32[256,1,128]{2,1,0:T(1,128)S(1)}, u32[]{:S(2)}, u32[]{:S(2)}) async-start(f32[256,1,128]{2,1,0:T(1,128)} %bitcast.18), calls=%async_computation | async-start | bytes 262144 | tf_op jit(solution)/shard_map/while/body/eval_jaxpr/all_to_all | solution.py:233
  284.5 18.7 %all-to-all-start = ((f32[256,1,128]{2,1,0:T(1,128)}), f32[256,1,128]{2,1,0:T(1,128)S(1)}, u32[]{:S(2)}, u32[]{:S(2)}) async-start(f32[256,1,128]{2,1,0:T(1,128)} %bitcast.18), calls=%async_computation | async-start | bytes 262144 | tf_op jit(solution)/shard_map/while/body/eval_jaxpr/all_to_all | solution.py:233
  304.4 18.7 %all-to-all-start = ((f32[256,1,128]{2,1,0:T(1,128)}), f32[256,1,128]{2,1,0:T(1,128)S(1)}, u32[]{:S(2)}, u32[]{:S(2)}) async-start(f32[256,1,128]{2,1,0:T(1,128)} %bitcast.18), calls=%async_computation | async-start | bytes 262144 | tf_op jit(solution)/shard_map/while/body/eval_jaxpr/all_to_all | solution.py:233
  324.4 18.7 %all-to-all-start = ((f32[256,1,128]{2,1,0:T(1,128)}), f32[256,1,128]{2,1,0:T(1,128)S(1)}, u32[]{:S(2)}, u32[]{:S(2)}) async-start(f32[256,1,128]{2,1,0:T(1,128)} %bitcast.18), calls=%async_computation | async-start | bytes 262144 | tf_op jit(solution)/shard_map/while/body/eval_jaxpr/all_to_all | solution.py:233
  344.4 18.7 %all-to-all-start = ((f32[256,1,128]{2,1,0:T(1,128)}), f32[256,1,128]{2,1,0:T(1,128)S(1)}, u32[]{:S(2)}, u32[]{:S(2)}) async-start(f32[256,1,128]{2,1,0:T(1,128)} %bitcast.18), calls=%async_computation | async-start | bytes 262144 | tf_op jit(solution)/shard_map/while/body/eval_jaxpr/all_to_all | solution.py:233
  364.3 18.7 %all-to-all-start = ((f32[256,1,128]{2,1,0:T(1,128)}), f32[256,1,128]{2,1,0:T(1,128)S(1)}, u32[]{:S(2)}, u32[]{:S(2)}) async-start(f32[256,1,128]{2,1,0:T(1,128)} %bitcast.18), calls=%async_computation | async-start | bytes 262144 | tf_op jit(solution)/shard_map/while/body/eval_jaxpr/all_to_all | solution.py:233

commit v5 on v3

v5 whole, which is shorter than its diff:
```python
import functools

import jax
import jax.numpy as jnp
from jax import lax
from jax.experimental import pallas as pl
from jax.experimental.pallas import tpu as pltpu
from jax.sharding import PartitionSpec as P

PANEL_COLUMNS = 16
LANES = 128
TILES = 12
SCALE, COEF = TILES, TILES + 1
OWN = 48

VMEM = pl.BlockSpec(memory_space=pltpu.VMEM)
SMEM = pl.BlockSpec(memory_space=pltpu.SMEM)
HBM = pl.BlockSpec(memory_space=pltpu.HBM)


def total(x):
    return jnp.sum(jnp.sum(x, axis=0, keepdims=True), axis=1, keepdims=True)


def iota(shape, dim):
    return lax.broadcasted_iota(jnp.int32, shape, dim)


def unpack(load):
    lane = iota((8, LANES), 1)
    tiles = []
    for gm in range(4):
        q = [load(8 * gm + k) for k in range(8)]
        tiles.append(jnp.where(lane < 48, q[0], jnp.where(lane < 96, q[1], q[2])))
        tiles.append(jnp.where(lane < 16, q[2], jnp.where(lane < 64, q[3], jnp.where(lane < 112, q[4], q[5]))))
        tiles.append(jnp.where(lane < 32, q[5], jnp.where(lane < 80, q[6], q[7])))
    return tiles


def tree_sum(xs):
    xs = list(xs)
    while len(xs) > 1:
        xs = [xs[i] + xs[i + 1] if i + 1 < len(xs) else xs[i] for i in range(0, len(xs), 2)]
    return xs[0]


def position(m):
    return (iota((8, LANES), 0) * TILES + m) * LANES + iota((8, LANES), 1)


def message(first, second):
    device = lax.axis_index("row") * lax.axis_size("col") + lax.axis_index("col")
    place = iota((OWN, LANES), 1) - iota((OWN, LANES), 0) - OWN * device
    picked = jnp.where((place & (LANES - 1)) == 0, first, 0.0) + jnp.where((place & (LANES - 1)) == OWN, second, 0.0)
    return jnp.sum(picked, axis=0, keepdims=True)


def own_column(rows_ref, k):
    head = rows_ref[0, :, 0:LANES]
    return jnp.sum(jnp.where(iota((OWN, LANES), 1) == k, head, 0.0), axis=1, keepdims=True)


def begin_body(top_ref, out_ref, tmp):
    lane = iota((8, LANES), 1)
    for t in range(6):
        tmp[32 * t : 32 * (t + 1), :] = top_ref[:, LANES * t : LANES * (t + 1)]

    def tile(k, m):
        half, t = divmod(m, 6)
        return tmp[pl.ds(32 * t + 2 * half + k, 8, stride=4), :]

    for gm in range(4):
        rows = []
        for k in range(2):
            t = [tile(k, 3 * gm + n) for n in range(3)]
            rows.append([t[0], t[0], jnp.where(lane < 96, t[1], t[0]), t[1], t[1], jnp.where(lane < 112, t[2], t[1]), t[2], t[2]])
        for q in range(8):
            mine = ((lane - OWN * q) & (LANES - 1)) < OWN
            out_ref[pl.ds(8 * gm + q, 8, stride=32), :] = jnp.where(mine, rows[0][q], pltpu.roll(rows[1][q], OWN, 1))

def image_of(got_ref, h, u, scale):
    y = unpack(lambda first: got_ref[pl.ds(first, 8, stride=32), :])
    p = [scale * (y[m] - h[m]) for m in range(TILES)]
    kappa = 0.5 * scale * total(tree_sum(p[m] * u[m] for m in range(TILES)))
    return p, kappa


def at(x, k):
    return x[0:1, k : k + 1]


def tiles(ref):
    return [ref[m] for m in range(TILES)]


def older_terms(pairs, u, j):
    h = [jnp.zeros((8, LANES), jnp.float32) for _ in range(TILES)]
    base = [jnp.zeros((8, LANES), jnp.float32) for _ in range(TILES)]
    for v_ref, w_ref in pairs:
        v, w = tiles(v_ref), tiles(w_ref)
        vu = total(tree_sum(v[m] * u[m] for m in range(TILES)))
        wu = total(tree_sum(w[m] * u[m] for m in range(TILES)))
        vj, wj = at(v[0], j), at(w[0], j)
        for m in range(TILES):
            h[m] = h[m] + (wu * v[m] + vu * w[m])
            base[m] = base[m] - (wj * v[m] + vj * w[m])
    return h, base


def step_body(j, *refs):
    got_ref, rows_ref = refs[:2]
    un_ref, coming_out, out_ref = refs[-4:-1] if j == 0 else refs[-5:-2]
    flat_ref = refs[-1]
    if j == 0:
        column = unpack(lambda first: got_ref[pl.ds(first, 8, stride=32), :])
        leading = at(column[0], 1)
    else:
        u_ref, coming_ref = refs[2:4]
        w_ref = refs[-2]
        pairs = [(refs[4 + 2 * i], refs[5 + 2 * i]) for i in range(j - 1)]
        u = tiles(u_ref)
        h, base = older_terms(pairs, u, j)
        p, kappa = image_of(got_ref, h, u, u_ref[SCALE, 0:1, 0:1])
        for m in range(TILES):
            base[m] = base[m] + coming_ref[m]
            w_ref[m] = p[m] - kappa * u[m]
        factor = at(p[0], j) - kappa * at(u[0], j) - kappa
        leading = at(base[0], j + 1) - at(p[0], j + 1) - factor * at(u[0], j + 1)
        column = [base[m] - p[m] - factor * u[m] for m in range(TILES)]
    column[0] = jnp.where(position(0) > j, column[0], 0.0)
    for m in range(TILES):
        rest = jnp.where(position(0) == j + 1, 0.0, column[0]) if m == 0 else column[m]
        flat_ref[pl.ds(m, 8, stride=TILES), :] = rest
    norm = jnp.sqrt(total(tree_sum(x * x for x in column)))
    inverse = 1.0 / (leading + norm)
    scale_now = 1.0 + leading / norm

    def four_blocks(n, acc):
        acc = list(acc)
        for s in range(24):
            k, t = divmod(s, 6)
            part = rows_ref[4 * n + k, :, LANES * t : LANES * (t + 1)] * flat_ref[pl.ds(24 * n + s, 1), :]
            acc[s % 2] = acc[s % 2] + part
        return tuple(acc)

    acc = lax.fori_loop(0, 4, four_blocks, (jnp.zeros((OWN, LANES), jnp.float32),) * 2)
    product = jnp.sum(acc[0] + acc[1], axis=1, keepdims=True) * inverse + rows_ref[0, :, j + 1 : j + 2]
    out_ref[...] = jnp.broadcast_to(message(product, rows_ref[0, :, j + 2 : j + 3]), out_ref.shape)
    after = unpack(lambda first: pltpu.roll(got_ref[pl.ds(first, 8, stride=32), :], LANES - OWN, 1))
    for m in range(TILES):
        r = column[m] * inverse
        un_ref[m] = jnp.where(position(0) == j + 1, 1.0, r) if m == 0 else r
        coming_out[m] = after[m]
    un_ref[SCALE] = jnp.broadcast_to(scale_now, (8, LANES))
    lane, row = iota((8, LANES), 1), iota((8, LANES), 0)
    before = jnp.zeros((8, LANES), jnp.float32) if j == 0 else u_ref[COEF]
    un_ref[COEF] = jnp.where(lane == j, jnp.where(row == 0, scale_now, -norm), before)


def last_body(own, got_ref, *refs):
    count = PANEL_COLUMNS - 1
    pairs = [(refs[2 * i], refs[2 * i + 1]) for i in range(count)]
    u_ref, matrix_ref, updated_ref, whole_ref, coef_ref, hist, block, whole, sides, sems = refs[2 * count :]
    read_block = pltpu.make_async_copy(matrix_ref, block, sems.at[0])
    read_block.start()
    coef_ref[...] = u_ref[COEF, 0:2, 0:PANEL_COLUMNS]
    u = tiles(u_ref)
    h, _ = older_terms(pairs, u, 0)
    p, kappa = image_of(got_ref, h, u, u_ref[SCALE, 0:1, 0:1])
    per = TILES * 8
    for i in range(PANEL_COLUMNS):
        for m in range(TILES):
            n = i * per + 8 * m
            hist[0, n : n + 8, :] = pairs[i][0][m] if i < count else u[m]
            hist[1, n : n + 8, :] = pairs[i][1][m] if i < count else p[m] - kappa * u[m]
    for side, n in ((0, own[0]), (1, own[1])):
        z, m0 = n // 2, 6 * (n % 2)
        for t in range(6):
            for half in range(2):
                rows = pl.ds(half * 8 * per + 8 * (m0 + t) + z, 8, stride=per)
                for k in range(2):
                    at = 16 * k + 8 * half
                    sides[side, at : at + 8, LANES * t : LANES * (t + 1)] = hist[k ^ side, rows, :]

    def pieces(x):
        high = x.astype(jnp.bfloat16)
        rest = x - high.astype(jnp.float32)
        mid = rest.astype(jnp.bfloat16)
        return high, mid, (rest - mid.astype(jnp.float32)).astype(jnp.bfloat16)

    lh, lm, ll = pieces(sides[0].T)
    rh, rm, rl = pieces(sides[1])
    left = jnp.concatenate([lh, lh, lm, lm, lh, ll], axis=1)
    right = jnp.concatenate([rh, rm, rh, rm, rl, rh], axis=0)
    read_block.wait()
    writes = []
    step = 256
    for n in range(block.shape[0] // step):
        rows = slice(step * n, step * (n + 1))
        block[rows, :] = block[rows, :] - jnp.dot(left[rows, :], right, preferred_element_type=jnp.float32)
        writes.append(pltpu.make_async_copy(block.at[rows, :], updated_ref.at[rows, :], sems.at[1 + n]))
        writes[-1].start()
    for half in range(2):
        for m in range(TILES):
            for z in range(8):
                s = TILES * z + m
                rows = pl.ds(half * 8 * per + 8 * m + z, 8, stride=per)
                whole[8 * half : 8 * half + 8, LANES * s : LANES * (s + 1)] = hist[0, rows, :]
    write = pltpu.make_async_copy(whole, whole_ref, sems.at[4])
    write.start()
    for w in writes:
        w.wait()
    write.wait()


def per_device(matrix):
    f32 = jnp.float32
    r, c = lax.axis_index("row"), lax.axis_index("col")
    ways = lax.axis_size("col")
    devices = ways * lax.axis_size("row")
    tile_cols = matrix.shape[1]
    own = jnp.stack([r, c])
    top = lax.all_to_all(
        jnp.broadcast_to(matrix[:2], (ways, 2, tile_cols)), "col", split_axis=0, concat_axis=0, tiled=True
    ).reshape(2 * ways, tile_cols)
    top, matrix_after = lax.optimization_barrier((top, matrix))
    top = jnp.where(r == 0, top, 0.0)
    for far in (8, 4, 2, 1):
        top = top + lax.ppermute(top, "row", [(n, n + far) for n in range(0, 16, 2 * far)])
    rows = lax.all_to_all(
        matrix_after.reshape(ways, OWN, tile_cols), "col", split_axis=0, concat_axis=0, tiled=True
    )

    def exchange(packed):
        return lax.all_to_all(packed, ("row", "col"), split_axis=0, concat_axis=0, tiled=True)

    def shape(*dims):
        return jax.ShapeDtypeStruct(dims, f32)

    vec, ext, packed = shape(TILES, 8, LANES), shape(TILES + 2, 8, LANES), shape(devices, LANES)
    order = TILES * 8 * LANES
    begin = pl.pallas_call(
        begin_body,
        out_shape=packed,
        in_specs=[VMEM],
        out_specs=VMEM,
        scratch_shapes=[pltpu.VMEM((192, LANES), f32)],
        compiler_params=pltpu.CompilerParams(vmem_limit_bytes=4 << 20),
        name="begin",
    )

    def step(j, *args):
        out = (ext, vec, packed) + ((vec,) if j else ())
        return pl.pallas_call(
            functools.partial(step_body, j),
            out_shape=out,
            in_specs=[VMEM] * len(args),
            out_specs=(VMEM,) * len(out),
            scratch_shapes=[pltpu.VMEM((order // LANES, LANES), f32)],
            compiler_params=pltpu.CompilerParams(vmem_limit_bytes=8 << 20),
            name=f"step{j}",
        )(*args)

    got, kept, tail = begin(top), [], []
    for j in range(PANEL_COLUMNS):
        u, coming, out, *w = step(j, got, rows, *tail, *kept)
        if j:
            kept += [tail[0], w[0]]
        got, tail = exchange(out), [u, coming]
    last = pl.pallas_call(
        last_body,
        out_shape=(shape(*matrix.shape), shape(PANEL_COLUMNS, order), shape(2, PANEL_COLUMNS)),
        in_specs=[SMEM] + [VMEM] * (len(kept) + 2) + [HBM],
        out_specs=(HBM, HBM, VMEM),
        scratch_shapes=[
            pltpu.VMEM((2, PANEL_COLUMNS * TILES * 8, LANES), f32),
            pltpu.VMEM(matrix.shape, f32),
            pltpu.VMEM((PANEL_COLUMNS, order), f32),
            pltpu.VMEM((2, 2 * PANEL_COLUMNS, tile_cols), f32),
            pltpu.SemaphoreType.DMA((5,)),
        ],
        compiler_params=pltpu.CompilerParams(vmem_limit_bytes=16 << 20),
        name="last",
    )
    return last(own, got, *kept, tail[0], matrix)


def solution(mesh):
    return jax.shard_map(
        per_device,
        mesh=mesh,
        in_specs=(P("row", "col"),),
        out_specs=(P("row", "col"), P(), P()),
        check_vma=False,
    )
```

time: 388 us -> 387 us (level)
  blocking collectives: 14.1 us -> 299 us
  waiting for transfers between devices: 186 us -> 40.8 us
  starting transfers between devices: 106 us -> 12.6 us
  Pallas kernels: 74.9 us -> 20.2 us
  local copies, waits for them, and re-layouts: 1.72 us -> 11.7 us
    all_to_all x0 -> x15, blocking collectives: none -> 285 us  [exchange(): lax.all_to_all(packed, ('row', 'col'), split_axis=0, concat_axis=0, tiled...]
    all_to_all x16 -> x1, waiting for transfers between devices: 162 us -> 13.1 us  [exchange(): lax.all_to_all(packed, ('row', 'col'), split_axis=0, concat_axis=0, tiled...]
    all_to_all x16 -> x1, starting transfers between devices: 98.6 us -> 5.53 us  [exchange(): lax.all_to_all(packed, ('row', 'col'), split_axis=0, concat_axis=0, tiled...]
    pallas_call x34 -> x18, Pallas kernels: 74.9 us -> 20.2 us  [the longest x16 16 us: step(): pl.pallas_call(functools.partial(step_body, j), out_shape=out, in_specs=[...]
    unnamed x2 -> x40, local copies, waits for them, and re-layouts: 0.01 us -> 10.8 us
  transfers between devices with their start and end apart: 21 -> 6, of which waited for: 18 -> 3; matrix products, arithmetic and copies ran while one was open for 0% -> 0% of each run, Pallas kernels for 13% -> 0%
where the time goes in v5:
time: 387 us; the launch traced here: 386 us
  blocking collectives  299 us (77%)
  waiting for transfers between devices  40.8 us (11%)
  Pallas kernels  20.2 us (5%)
  starting transfers between devices  12.6 us (3%)
  local copies, waits for them, and re-layouts  11.7 us (3%)
    all_to_all x15, blocking collectives, exchange(): lax.all_to_all(packed, ('row', 'col'), split_axis=0, concat_axis=0, tiled...  285 us
    ppermute x4, waiting for transfers between devices, per_device(): lax.ppermute(top, 'row', [(n, n + far) for n in range(0, 16, 2 * far)])  19 us
    pallas_call x16, Pallas kernels, step(): pl.pallas_call(functools.partial(step_body, j), out_shape=out, in_specs=[...  16 us
    all_to_all x1, blocking collectives, per_device(): lax.all_to_all(jnp.broadcast_to(matrix[:2], (ways, 2, tile_cols)), 'col',...  14.1 us
    all_to_all x1, waiting for transfers between devices, exchange(): lax.all_to_all(packed, ('row', 'col'), split_axis=0, concat_axis=0, tiled...  13.1 us
    unnamed x40, local copies, waits for them, and re-layouts  10.8 us
    all_to_all x1, waiting for transfers between devices, per_device(): lax.all_to_all(matrix_after.reshape(ways, OWN, tile_cols), 'col', split_a...  8.67 us
  transfers between devices with their start and end apart: 6, of which 3 were waited for; matrix products, arithmetic and copies ran while one was open for 0% of the time, Pallas kernels for 0%

profile of v5, /device:TPU:1, one launch (start us, length us, event | category | flops | bytes accessed | tf_op | source)
XLA Modules:
  0.0 385.7 jit_solution(10667609519316527999)
XLA Ops:
  1.4 14.1 %all_to_all.186 = f32[16,2,768]{2,1,0:T(2,128)S(1)} all-to-all(f32[16,2,768]{2,1,0:T(2,128)S(1)} %broadcast_in_dim.7), channel_id=1, replica_groups=mesh['row'=16,'col'=16] {'col'}, dimensions={0} | all-to-all | bytes 196608 | tf_op jit(solution)/shard_map/all_to_all | solution.py:223
  15.6 3.7 all-to-all-start.1
  21.5 1.3 collective-permute-start.3
  22.8 19.0 %collective-permute-done.3 = f32[32,768]{1,0:T(8,128)S(1)} collective-permute-done((f32[32,768]{1,0:T(8,128)S(1)}, f32[32,768]{1,0:T(8,128)S(1)}, u32[]{:S(2)}, u32[]{:S(2)}) %collective-permute-start.3) | collective-permute-done | bytes 98336 | tf_op jit(solution)/shard_map/ppermute | solution.py:229
  42.0 8.7 %all-to-all-done.1.refs_1_ = f32[16,48,768]{2,1,0:T(8,128)S(1)} async-done(((f32[16,48,768]{2,1,0:T(8,128)}), f32[16,48,768]{2,1,0:T(8,128)S(1)}, u32[]{:S(2)}, u32[]{:S(2)}) %all-to-all-start.1) | async-done | bytes 2359328 | tf_op jit(solution)/shard_map/all_to_all | solution.py:230
  51.2 26.6 %all_to_all.187 = f32[256,1,128]{2,1,0:T(1,128)S(1)} all-to-all(f32[256,1,128]{2,1,0:T(1,128)S(1)} %bitcast.99), channel_id=1, replica_groups=mesh['row'=16,'col'=16] {'row','col'}, dimensions={0} | all-to-all | bytes 262144 | tf_op jit(solution)/shard_map/all_to_all | solution.py:235
  78.7 18.4 %all_to_all.188 = f32[256,1,128]{2,1,0:T(1,128)S(1)} all-to-all(f32[256,1,128]{2,1,0:T(1,128)S(1)} %bitcast.85), channel_id=1, replica_groups=mesh['row'=16,'col'=16] {'row','col'}, dimensions={0} | all-to-all | bytes 262144 | tf_op jit(solution)/shard_map/all_to_all | solution.py:235
  98.0 18.4 %all_to_all.189 = f32[256,1,128]{2,1,0:T(1,128)S(1)} all-to-all(f32[256,1,128]{2,1,0:T(1,128)S(1)} %bitcast.86), channel_id=1, replica_groups=mesh['row'=16,'col'=16] {'row','col'}, dimensions={0} | all-to-all | bytes 262144 | tf_op jit(solution)/shard_map/all_to_all | solution.py:235
  117.3 18.4 %all_to_all.190 = f32[256,1,128]{2,1,0:T(1,128)S(1)} all-to-all(f32[256,1,128]{2,1,0:T(1,128)S(1)} %bitcast.87), channel_id=1, replica_groups=mesh['row'=16,'col'=16] {'row','col'}, dimensions={0} | all-to-all | bytes 262144 | tf_op jit(solution)/shard_map/all_to_all | solution.py:235
  136.7 18.4 %all_to_all.191 = f32[256,1,128]{2,1,0:T(1,128)S(1)} all-to-all(f32[256,1,128]{2,1,0:T(1,128)S(1)} %bitcast.88), channel_id=1, replica_groups=mesh['row'=16,'col'=16] {'row','col'}, dimensions={0} | all-to-all | bytes 262144 | tf_op jit(solution)/shard_map/all_to_all | solution.py:235
  156.1 18.4 %all_to_all.192 = f32[256,1,128]{2,1,0:T(1,128)S(1)} all-to-all(f32[256,1,128]{2,1,0:T(1,128)S(1)} %bitcast.89), channel_id=1, replica_groups=mesh['row'=16,'col'=16] {'row','col'}, dimensions={0} | all-to-all | bytes 262144 | tf_op jit(solution)/shard_map/all_to_all | solution.py:235
  175.4 18.6 %all_to_all.193 = f32[256,1,128]{2,1,0:T(1,128)S(1)} all-to-all(f32[256,1,128]{2,1,0:T(1,128)S(1)} %bitcast.90), channel_id=1, replica_groups=mesh['row'=16,'col'=16] {'row','col'}, dimensions={0} | all-to-all | bytes 262144 | tf_op jit(solution)/shard_map/all_to_all | solution.py:235
  195.0 18.4 %all_to_all.194 = f32[256,1,128]{2,1,0:T(1,128)S(1)} all-to-all(f32[256,1,128]{2,1,0:T(1,128)S(1)} %bitcast.91), channel_id=1, replica_groups=mesh['row'=16,'col'=16] {'row','col'}, dimensions={0} | all-to-all | bytes 262144 | tf_op jit(solution)/shard_map/all_to_all | solution.py:235
  213.4 1.0 step8.1
  214.4 18.4 %all_to_all.195 = f32[256,1,128]{2,1,0:T(1,128)S(1)} all-to-all(f32[256,1,128]{2,1,0:T(1,128)S(1)} %bitcast.92), channel_id=1, replica_groups=mesh['row'=16,'col'=16] {'row','col'}, dimensions={0} | all-to-all | bytes 262144 | tf_op jit(solution)/shard_map/all_to_all | solution.py:235
  232.9 1.0 step9.1
  233.9 18.4 %all_to_all.196 = f32[256,1,128]{2,1,0:T(1,128)S(1)} all-to-all(f32[256,1,128]{2,1,0:T(1,128)S(1)} %bitcast.93), channel_id=1, replica_groups=mesh['row'=16,'col'=16] {'row','col'}, dimensions={0} | all-to-all | bytes 262144 | tf_op jit(solution)/shard_map/all_to_all | solution.py:235
  252.3 1.0 step10.1
  253.3 18.4 %all_to_all.197 = f32[256,1,128]{2,1,0:T(1,128)S(1)} all-to-all(f32[256,1,128]{2,1,0:T(1,128)S(1)} %bitcast.94), channel_id=1, replica_groups=mesh['row'=16,'col'=16] {'row','col'}, dimensions={0} | all-to-all | bytes 262144 | tf_op jit(solution)/shard_map/all_to_all | solution.py:235
  271.8 1.0 step11.1
  272.9 18.4 %all_to_all.198 = f32[256,1,128]{2,1,0:T(1,128)S(1)} all-to-all(f32[256,1,128]{2,1,0:T(1,128)S(1)} %bitcast.95), channel_id=1, replica_groups=mesh['row'=16,'col'=16] {'row','col'}, dimensions={0} | all-to-all | bytes 262144 | tf_op jit(solution)/shard_map/all_to_all | solution.py:235
  291.3 1.1 step12.1
  292.4 18.7 %all_to_all.199 = f32[256,1,128]{2,1,0:T(1,128)S(1)} all-to-all(f32[256,1,128]{2,1,0:T(1,128)S(1)} %bitcast.96), channel_id=1, replica_groups=mesh['row'=16,'col'=16] {'row','col'}, dimensions={0} | all-to-all | bytes 262144 | tf_op jit(solution)/shard_map/all_to_all | solution.py:235
  311.0 1.1 step13.1
  312.2 18.4 %all_to_all.200 = f32[256,1,128]{2,1,0:T(1,128)S(1)} all-to-all(f32[256,1,128]{2,1,0:T(1,128)S(1)} %bitcast.97), channel_id=1, replica_groups=mesh['row'=16,'col'=16] {'row','col'}, dimensions={0} | all-to-all | bytes 262144 | tf_op jit(solution)/shard_map/all_to_all | solution.py:235
  330.6 1.1 step14.1
  331.7 18.4 %all_to_all.201 = f32[256,1,128]{2,1,0:T(1,128)S(1)} all-to-all(f32[256,1,128]{2,1,0:T(1,128)S(1)} %bitcast.98), channel_id=1, replica_groups=mesh['row'=16,'col'=16] {'row','col'}, dimensions={0} | all-to-all | bytes 262144 | tf_op jit(solution)/shard_map/all_to_all | solution.py:235
  350.2 1.8 step15.1
  353.9 5.5 %all-to-all-start.17 = ((f32[256,1,128]{2,1,0:T(1,128)}), f32[256,1,128]{2,1,0:T(1,128)S(1)}, u32[]{:S(2)}, u32[]{:S(2)}) async-start(f32[256,1,128]{2,1,0:T(1,128)} %bitcast.84), calls=%async_computation.17 | async-start | bytes 262144 | tf_op jit(solution)/shard_map/all_to_all | solution.py:235
  359.5 13.1 %all-to-all-done.17 = f32[256,1,128]{2,1,0:T(1,128)S(1)} async-done(((f32[256,1,128]{2,1,0:T(1,128)}), f32[256,1,128]{2,1,0:T(1,128)S(1)}, u32[]{:S(2)}, u32[]{:S(2)}) %all-to-all-start.17) | async-done | bytes 131104 | tf_op jit(solution)/shard_map/all_to_all | solution.py:235
  372.6 1.7 copy-done
  381.5 4.1 %last.1 = (f32[768,768]{1,0:T(8,128)}, f32[16,12288]{1,0:T(8,128)}, f32[2,16]{1,0:T(2,128)}) custom-call(s32[2]{0:T(128)S(1)} %pad_add_fusion.own, f32[256,128]{1,0:T(8,128)S(1)} %bitcast.69, f32[14,8,128]{2,1,0:T(8,128)S(1)} %get-tuple-element.70.refs_2_.refs_4_.refs_0_, f32[12,8,128]{2,1,0:T(8,128)S(1)} %get-tuple-element.75.refs_5_.refs_1_, ...), custom_call_target="tpu_custom_call" | custom-call | tf_op jit(solution)/shard_map/last/pallas_call | solution.py:285
  (63 shorter events, 19.2 us)
Async XLA Ops:
  15.6 35.1 %all-to-all-start.1 = ((f32[16,48,768]{2,1,0:T(8,128)}), f32[16,48,768]{2,1,0:T(8,128)S(1)}, u32[]{:S(2)}, u32[]{:S(2)}) async-start(f32[16,48,768]{2,1,0:T(8,128)} %bitcast.67), calls=%async_computation.1 | async-start | bytes 4718592 | tf_op jit(solution)/shard_map/all_to_all | solution.py:230
  19.3 0.7 collective-permute-start
  20.1 0.7 collective-permute-start.1
  20.8 0.7 collective-permute-start.2
  21.5 20.3 %collective-permute-start.3 = (f32[32,768]{1,0:T(8,128)S(1)}, f32[32,768]{1,0:T(8,128)S(1)}, u32[]{:S(2)}, u32[]{:S(2)}) collective-permute-start(f32[32,768]{1,0:T(8,128)S(1)} %add.14), channel_id=1, source_target_pairs={{0,16},{32,48},{64,80},{96,112},{128,144},{160,176},{192,208},{224... | collective-permute-start | bytes 294920 | tf_op jit(solution)/shard_map/ppermute | solution.py:229
  272.8 77.3 %copy-start.1 = (f32[12,8,128]{2,1,0:T(8,128)}, f32[12,8,128]{2,1,0:T(8,128)S(1)}, u32[]{:S(2)}) copy-start(f32[12,8,128]{2,1,0:T(8,128)S(1)} %get-tuple-element.115.refs_25_.refs_21_) | copy-start | bytes 147460
  292.4 57.8 %copy-start.3 = (f32[14,8,128]{2,1,0:T(8,128)}, f32[14,8,128]{2,1,0:T(8,128)S(1)}, u32[]{:S(2)}) copy-start(f32[14,8,128]{2,1,0:T(8,128)S(1)} %get-tuple-element.117.refs_2_.refs_28_.refs_24_) | copy-start | bytes 172036
  292.4 57.8 %copy-start.5 = (f32[12,8,128]{2,1,0:T(8,128)}, f32[12,8,128]{2,1,0:T(8,128)S(1)}, u32[]{:S(2)}) copy-start(f32[12,8,128]{2,1,0:T(8,128)S(1)} %get-tuple-element.119.refs_27_.refs_23_) | copy-start | bytes 147460
  312.1 39.9 %copy-start.7 = (f32[14,8,128]{2,1,0:T(8,128)}, f32[14,8,128]{2,1,0:T(8,128)S(1)}, u32[]{:S(2)}) copy-start(f32[14,8,128]{2,1,0:T(8,128)S(1)} %get-tuple-element.121.refs_2_.refs_30_.refs_26_) | copy-start | bytes 172036
  312.1 39.8 %copy-start.9 = (f32[12,8,128]{2,1,0:T(8,128)}, f32[12,8,128]{2,1,0:T(8,128)S(1)}, u32[]{:S(2)}) copy-start(f32[12,8,128]{2,1,0:T(8,128)S(1)} %get-tuple-element.123.refs_29_.refs_25_) | copy-start | bytes 147460
  331.7 22.2 %copy-start.11 = (f32[14,8,128]{2,1,0:T(8,128)}, f32[14,8,128]{2,1,0:T(8,128)S(1)}, u32[]{:S(2)}) copy-start(f32[14,8,128]{2,1,0:T(8,128)S(1)} %get-tuple-element.125.refs_2_.refs_28_) | copy-start | bytes 172036
  331.7 22.2 %copy-start.13 = (f32[12,8,128]{2,1,0:T(8,128)}, f32[12,8,128]{2,1,0:T(8,128)S(1)}, u32[]{:S(2)}) copy-start(f32[12,8,128]{2,1,0:T(8,128)S(1)} %get-tuple-element.127.refs_31_.refs_27_) | copy-start | bytes 147460
  352.0 0.7 copy-start.15
  352.6 0.6 copy-start.16
  353.3 0.6 copy-start.18
  353.9 18.7 %all-to-all-start.17 = ((f32[256,1,128]{2,1,0:T(1,128)}), f32[256,1,128]{2,1,0:T(1,128)S(1)}, u32[]{:S(2)}, u32[]{:S(2)}) async-start(f32[256,1,128]{2,1,0:T(1,128)} %bitcast.84), calls=%async_computation.17 | async-start | bytes 262144 | tf_op jit(solution)/shard_map/all_to_all | solution.py:235
  372.6 1.7 copy-start
  374.2 0.8 copy-start.2
  375.0 0.8 copy-start.4
  375.8 0.8 copy-start.6
  376.6 0.8 copy-start.8
  377.5 0.8 copy-start.10
  378.3 0.8 copy-start.12
  379.1 0.8 copy-start.14
  379.9 0.8 copy-start.17
  380.7 0.8 copy-start.19

commit v6 on v5

--- a/solution.py
+++ b/solution.py
@@ -14,7 +14,6 @@
 OWN = 48
 
 VMEM = pl.BlockSpec(memory_space=pltpu.VMEM)
-SMEM = pl.BlockSpec(memory_space=pltpu.SMEM)
 HBM = pl.BlockSpec(memory_space=pltpu.HBM)
 
 
@@ -109,14 +108,14 @@
 
 def step_body(j, *refs):
     got_ref, rows_ref = refs[:2]
-    un_ref, coming_out, out_ref = refs[-4:-1] if j == 0 else refs[-5:-2]
-    flat_ref = refs[-1]
+    *outs, flat_ref = refs[-5 if 0 < j < PANEL_COLUMNS - 1 else -4 :]
+    un_ref, out_ref = outs[:2]
     if j == 0:
         column = unpack(lambda first: got_ref[pl.ds(first, 8, stride=32), :])
         leading = at(column[0], 1)
     else:
         u_ref, coming_ref = refs[2:4]
-        w_ref = refs[-2]
+        w_ref = outs[-1]
         pairs = [(refs[4 + 2 * i], refs[5 + 2 * i]) for i in range(j - 1)]
         u = tiles(u_ref)
         h, base = older_terms(pairs, u, j)
@@ -146,23 +145,23 @@
     acc = lax.fori_loop(0, 4, four_blocks, (jnp.zeros((OWN, LANES), jnp.float32),) * 2)
     product = jnp.sum(acc[0] + acc[1], axis=1, keepdims=True) * inverse + rows_ref[0, :, j + 1 : j + 2]
     out_ref[...] = jnp.broadcast_to(message(product, rows_ref[0, :, j + 2 : j + 3]), out_ref.shape)
-    after = unpack(lambda first: pltpu.roll(got_ref[pl.ds(first, 8, stride=32), :], LANES - OWN, 1))
     for m in range(TILES):
         r = column[m] * inverse
         un_ref[m] = jnp.where(position(0) == j + 1, 1.0, r) if m == 0 else r
-        coming_out[m] = after[m]
+    if j < PANEL_COLUMNS - 1:
+        after = unpack(lambda first: pltpu.roll(got_ref[pl.ds(first, 8, stride=32), :], LANES - OWN, 1))
+        for m in range(TILES):
+            outs[2][m] = after[m]
     un_ref[SCALE] = jnp.broadcast_to(scale_now, (8, LANES))
     lane, row = iota((8, LANES), 1), iota((8, LANES), 0)
     before = jnp.zeros((8, LANES), jnp.float32) if j == 0 else u_ref[COEF]
     un_ref[COEF] = jnp.where(lane == j, jnp.where(row == 0, scale_now, -norm), before)
 
 
-def last_body(own, got_ref, *refs):
+def last_body(got_ref, *refs):
     count = PANEL_COLUMNS - 1
     pairs = [(refs[2 * i], refs[2 * i + 1]) for i in range(count)]
     u_ref, matrix_ref, updated_ref, whole_ref, coef_ref, hist, block, whole, sides, sems = refs[2 * count :]
-    read_block = pltpu.make_async_copy(matrix_ref, block, sems.at[0])
-    read_block.start()
     coef_ref[...] = u_ref[COEF, 0:2, 0:PANEL_COLUMNS]
     u = tiles(u_ref)
     h, _ = older_terms(pairs, u, 0)
@@ -173,7 +172,7 @@
             n = i * per + 8 * m
             hist[0, n : n + 8, :] = pairs[i][0][m] if i < count else u[m]
             hist[1, n : n + 8, :] = pairs[i][1][m] if i < count else p[m] - kappa * u[m]
-    for side, n in ((0, own[0]), (1, own[1])):
+    for side, n in ((0, lax.axis_index("row")), (1, lax.axis_index("col"))):
         z, m0 = n // 2, 6 * (n % 2)
         for t in range(6):
             for half in range(2):
@@ -192,13 +191,12 @@
     rh, rm, rl = pieces(sides[1])
     left = jnp.concatenate([lh, lh, lm, lm, lh, ll], axis=1)
     right = jnp.concatenate([rh, rm, rh, rm, rl, rh], axis=0)
-    read_block.wait()
     writes = []
     step = 256
     for n in range(block.shape[0] // step):
         rows = slice(step * n, step * (n + 1))
-        block[rows, :] = block[rows, :] - jnp.dot(left[rows, :], right, preferred_element_type=jnp.float32)
-        writes.append(pltpu.make_async_copy(block.at[rows, :], updated_ref.at[rows, :], sems.at[1 + n]))
+        block[rows, :] = matrix_ref[rows, :] - jnp.dot(left[rows, :], right, preferred_element_type=jnp.float32)
+        writes.append(pltpu.make_async_copy(block.at[rows, :], updated_ref.at[rows, :], sems.at[n]))
         writes[-1].start()
     for half in range(2):
         for m in range(TILES):
@@ -206,7 +204,7 @@
                 s = TILES * z + m
                 rows = pl.ds(half * 8 * per + 8 * m + z, 8, stride=per)
                 whole[8 * half : 8 * half + 8, LANES * s : LANES * (s + 1)] = hist[0, rows, :]
-    write = pltpu.make_async_copy(whole, whole_ref, sems.at[4])
+    write = pltpu.make_async_copy(whole, whole_ref, sems.at[3])
     write.start()
     for w in writes:
         w.wait()
@@ -215,11 +213,10 @@
 
 def per_device(matrix):
     f32 = jnp.float32
-    r, c = lax.axis_index("row"), lax.axis_index("col")
+    r = lax.axis_index("row")
     ways = lax.axis_size("col")
     devices = ways * lax.axis_size("row")
     tile_cols = matrix.shape[1]
-    own = jnp.stack([r, c])
     top = lax.all_to_all(
         jnp.broadcast_to(matrix[:2], (ways, 2, tile_cols)), "col", split_axis=0, concat_axis=0, tiled=True
     ).reshape(2 * ways, tile_cols)
@@ -250,7 +247,7 @@
     )
 
     def step(j, *args):
-        out = (ext, vec, packed) + ((vec,) if j else ())
+        out = (ext, packed) + (vec,) * ((j < PANEL_COLUMNS - 1) + (j > 0))
         return pl.pallas_call(
             functools.partial(step_body, j),
             out_shape=out,
@@ -263,26 +260,26 @@
 
     got, kept, tail = begin(top), [], []
     for j in range(PANEL_COLUMNS):
-        u, coming, out, *w = step(j, got, rows, *tail, *kept)
+        u, out, *vectors = step(j, got, rows, *tail, *kept)
         if j:
-            kept += [tail[0], w[0]]
-        got, tail = exchange(out), [u, coming]
+            kept += [tail[0], vectors[-1]]
+        got, tail = exchange(out), [u, vectors[0]]
     last = pl.pallas_call(
         last_body,
         out_shape=(shape(*matrix.shape), shape(PANEL_COLUMNS, order), shape(2, PANEL_COLUMNS)),
-        in_specs=[SMEM] + [VMEM] * (len(kept) + 2) + [HBM],
+        in_specs=[VMEM] * (len(kept) + 3),
         out_specs=(HBM, HBM, VMEM),
         scratch_shapes=[
             pltpu.VMEM((2, PANEL_COLUMNS * TILES * 8, LANES), f32),
             pltpu.VMEM(matrix.shape, f32),
             pltpu.VMEM((PANEL_COLUMNS, order), f32),
             pltpu.VMEM((2, 2 * PANEL_COLUMNS, tile_cols), f32),
-            pltpu.SemaphoreType.DMA((5,)),
+            pltpu.SemaphoreType.DMA((4,)),
         ],
         compiler_params=pltpu.CompilerParams(vmem_limit_bytes=16 << 20),
         name="last",
     )
-    return last(own, got, *kept, tail[0], matrix)
+    return last(got, *kept, tail[0], matrix)
 
 
 def solution(mesh):

time: 387 us -> 374 us (0.966)
  blocking collectives: 299 us -> 318 us
  waiting for transfers between devices: 40.8 us -> 27.7 us
  local copies, waits for them, and re-layouts: 11.7 us -> 0.85 us
  starting transfers between devices: 12.6 us -> 7.03 us
    all_to_all x15 -> x16, blocking collectives: 285 us -> 304 us  [exchange(): lax.all_to_all(packed, ('row', 'col'), split_axis=0, concat_axis=0, tiled...]
    all_to_all x1 -> x0, waiting for transfers between devices: 13.1 us -> none  [exchange(): lax.all_to_all(packed, ('row', 'col'), split_axis=0, concat_axis=0, tiled...]
    unnamed x40 -> x2, local copies, waits for them, and re-layouts: 10.8 us -> 0.01 us
    all_to_all x1 -> x0, starting transfers between devices: 5.53 us -> none  [exchange(): lax.all_to_all(packed, ('row', 'col'), split_axis=0, concat_axis=0, tiled...]
  transfers between devices with their start and end apart: 6 -> 5, of which waited for: 3 -> 2; matrix products, arithmetic and copies ran while one was open for 0% -> 0% of each run, Pallas kernels for 0% -> 0%
where the time goes in v6:
time: 374 us; the launch traced here: 373 us
  blocking collectives  318 us (85%)
  waiting for transfers between devices  27.7 us (7%)
  Pallas kernels  18.7 us (5%)
  starting transfers between devices  7.03 us (2%)
    all_to_all x16, blocking collectives, exchange(): lax.all_to_all(packed, ('row', 'col'), split_axis=0, concat_axis=0, tiled...  304 us
    ppermute x4, waiting for transfers between devices, per_device(): lax.ppermute(top, 'row', [(n, n + far) for n in range(0, 16, 2 * far)])  19 us
    pallas_call x16, Pallas kernels, step(): pl.pallas_call(functools.partial(step_body, j), out_shape=out, in_specs=[...  15.3 us
    all_to_all x1, blocking collectives, per_device(): lax.all_to_all(jnp.broadcast_to(matrix[:2], (ways, 2, tile_cols)), 'col',...  14.1 us
    all_to_all x1, waiting for transfers between devices, per_device(): lax.all_to_all(matrix_after.reshape(ways, OWN, tile_cols), 'col', split_a...  8.67 us
  transfers between devices with their start and end apart: 5, of which 2 were waited for; matrix products, arithmetic and copies ran while one was open for 0% of the time, Pallas kernels for 0%

profile of v6, /device:TPU:1, one launch (start us, length us, event | category | flops | bytes accessed | tf_op | source)
XLA Modules:
  0.0 373.2 jit_solution(12927287082398504160)
XLA Ops:
  1.4 14.1 %all_to_all.186 = f32[16,2,768]{2,1,0:T(2,128)S(1)} all-to-all(f32[16,2,768]{2,1,0:T(2,128)S(1)} %broadcast_in_dim.7), channel_id=1, replica_groups=mesh['row'=16,'col'=16] {'col'}, dimensions={0} | all-to-all | bytes 196608 | tf_op jit(solution)/shard_map/all_to_all | solution.py:220
  15.6 3.7 %all-to-all-start.1 = ((f32[16,48,768]{2,1,0:T(8,128)}), f32[16,48,768]{2,1,0:T(8,128)S(1)}, u32[]{:S(2)}, u32[]{:S(2)}) async-start(f32[16,48,768]{2,1,0:T(8,128)} %bitcast.65), calls=%async_computation.1 | async-start | bytes 4718592 | tf_op jit(solution)/shard_map/all_to_all | solution.py:227
  21.5 1.3 collective-permute-start.3
  22.8 19.0 %collective-permute-done.3 = f32[32,768]{1,0:T(8,128)S(1)} collective-permute-done((f32[32,768]{1,0:T(8,128)S(1)}, f32[32,768]{1,0:T(8,128)S(1)}, u32[]{:S(2)}, u32[]{:S(2)}) %collective-permute-start.3) | collective-permute-done | bytes 98336 | tf_op jit(solution)/shard_map/ppermute | solution.py:226
  42.0 8.7 %all-to-all-done.1.refs_1_ = f32[16,48,768]{2,1,0:T(8,128)S(1)} async-done(((f32[16,48,768]{2,1,0:T(8,128)}), f32[16,48,768]{2,1,0:T(8,128)S(1)}, u32[]{:S(2)}, u32[]{:S(2)}) %all-to-all-start.1) | async-done | bytes 2359328 | tf_op jit(solution)/shard_map/all_to_all | solution.py:227
  51.2 26.6 %all_to_all.187 = f32[256,1,128]{2,1,0:T(1,128)S(1)} all-to-all(f32[256,1,128]{2,1,0:T(1,128)S(1)} %bitcast.97), channel_id=1, replica_groups=mesh['row'=16,'col'=16] {'row','col'}, dimensions={0} | all-to-all | bytes 262144 | tf_op jit(solution)/shard_map/all_to_all | solution.py:232
  78.7 18.4 %all_to_all.188 = f32[256,1,128]{2,1,0:T(1,128)S(1)} all-to-all(f32[256,1,128]{2,1,0:T(1,128)S(1)} %bitcast.82), channel_id=1, replica_groups=mesh['row'=16,'col'=16] {'row','col'}, dimensions={0} | all-to-all | bytes 262144 | tf_op jit(solution)/shard_map/all_to_all | solution.py:232
  98.0 18.4 %all_to_all.189 = f32[256,1,128]{2,1,0:T(1,128)S(1)} all-to-all(f32[256,1,128]{2,1,0:T(1,128)S(1)} %bitcast.83), channel_id=1, replica_groups=mesh['row'=16,'col'=16] {'row','col'}, dimensions={0} | all-to-all | bytes 262144 | tf_op jit(solution)/shard_map/all_to_all | solution.py:232
  117.3 18.4 %all_to_all.190 = f32[256,1,128]{2,1,0:T(1,128)S(1)} all-to-all(f32[256,1,128]{2,1,0:T(1,128)S(1)} %bitcast.84), channel_id=1, replica_groups=mesh['row'=16,'col'=16] {'row','col'}, dimensions={0} | all-to-all | bytes 262144 | tf_op jit(solution)/shard_map/all_to_all | solution.py:232
  136.7 18.4 %all_to_all.191 = f32[256,1,128]{2,1,0:T(1,128)S(1)} all-to-all(f32[256,1,128]{2,1,0:T(1,128)S(1)} %bitcast.85), channel_id=1, replica_groups=mesh['row'=16,'col'=16] {'row','col'}, dimensions={0} | all-to-all | bytes 262144 | tf_op jit(solution)/shard_map/all_to_all | solution.py:232
  156.1 18.4 %all_to_all.192 = f32[256,1,128]{2,1,0:T(1,128)S(1)} all-to-all(f32[256,1,128]{2,1,0:T(1,128)S(1)} %bitcast.86), channel_id=1, replica_groups=mesh['row'=16,'col'=16] {'row','col'}, dimensions={0} | all-to-all | bytes 262144 | tf_op jit(solution)/shard_map/all_to_all | solution.py:232
  174.5 0.9 step6.1
  175.4 18.6 %all_to_all.193 = f32[256,1,128]{2,1,0:T(1,128)S(1)} all-to-all(f32[256,1,128]{2,1,0:T(1,128)S(1)} %bitcast.87), channel_id=1, replica_groups=mesh['row'=16,'col'=16] {'row','col'}, dimensions={0} | all-to-all | bytes 262144 | tf_op jit(solution)/shard_map/all_to_all | solution.py:232
  194.1 0.9 step7.1
  195.0 18.4 %all_to_all.194 = f32[256,1,128]{2,1,0:T(1,128)S(1)} all-to-all(f32[256,1,128]{2,1,0:T(1,128)S(1)} %bitcast.88), channel_id=1, replica_groups=mesh['row'=16,'col'=16] {'row','col'}, dimensions={0} | all-to-all | bytes 262144 | tf_op jit(solution)/shard_map/all_to_all | solution.py:232
  213.4 1.0 step8.1
  214.4 18.4 %all_to_all.195 = f32[256,1,128]{2,1,0:T(1,128)S(1)} all-to-all(f32[256,1,128]{2,1,0:T(1,128)S(1)} %bitcast.89), channel_id=1, replica_groups=mesh['row'=16,'col'=16] {'row','col'}, dimensions={0} | all-to-all | bytes 262144 | tf_op jit(solution)/shard_map/all_to_all | solution.py:232
  232.9 1.0 step9.1
  233.9 18.4 %all_to_all.196 = f32[256,1,128]{2,1,0:T(1,128)S(1)} all-to-all(f32[256,1,128]{2,1,0:T(1,128)S(1)} %bitcast.90), channel_id=1, replica_groups=mesh['row'=16,'col'=16] {'row','col'}, dimensions={0} | all-to-all | bytes 262144 | tf_op jit(solution)/shard_map/all_to_all | solution.py:232
  252.3 1.0 step10.1
  253.3 18.4 %all_to_all.197 = f32[256,1,128]{2,1,0:T(1,128)S(1)} all-to-all(f32[256,1,128]{2,1,0:T(1,128)S(1)} %bitcast.91), channel_id=1, replica_groups=mesh['row'=16,'col'=16] {'row','col'}, dimensions={0} | all-to-all | bytes 262144 | tf_op jit(solution)/shard_map/all_to_all | solution.py:232
  271.8 1.1 step11.1
  272.8 18.4 %all_to_all.198 = f32[256,1,128]{2,1,0:T(1,128)S(1)} all-to-all(f32[256,1,128]{2,1,0:T(1,128)S(1)} %bitcast.92), channel_id=1, replica_groups=mesh['row'=16,'col'=16] {'row','col'}, dimensions={0} | all-to-all | bytes 262144 | tf_op jit(solution)/shard_map/all_to_all | solution.py:232
  291.3 1.1 step12.1
  292.3 18.7 %all_to_all.199 = f32[256,1,128]{2,1,0:T(1,128)S(1)} all-to-all(f32[256,1,128]{2,1,0:T(1,128)S(1)} %bitcast.93), channel_id=1, replica_groups=mesh['row'=16,'col'=16] {'row','col'}, dimensions={0} | all-to-all | bytes 262144 | tf_op jit(solution)/shard_map/all_to_all | solution.py:232
  311.0 1.1 step13.1
  312.1 18.4 %all_to_all.200 = f32[256,1,128]{2,1,0:T(1,128)S(1)} all-to-all(f32[256,1,128]{2,1,0:T(1,128)S(1)} %bitcast.94), channel_id=1, replica_groups=mesh['row'=16,'col'=16] {'row','col'}, dimensions={0} | all-to-all | bytes 262144 | tf_op jit(solution)/shard_map/all_to_all | solution.py:232
  330.5 1.1 step14.1
  331.6 18.6 %all_to_all.201 = f32[256,1,128]{2,1,0:T(1,128)S(1)} all-to-all(f32[256,1,128]{2,1,0:T(1,128)S(1)} %bitcast.95), channel_id=1, replica_groups=mesh['row'=16,'col'=16] {'row','col'}, dimensions={0} | all-to-all | bytes 262144 | tf_op jit(solution)/shard_map/all_to_all | solution.py:232
  350.2 1.1 step15.1
  351.4 18.4 %all_to_all.202 = f32[256,1,128]{2,1,0:T(1,128)S(1)} all-to-all(f32[256,1,128]{2,1,0:T(1,128)S(1)} %bitcast.96), channel_id=1, replica_groups=mesh['row'=16,'col'=16] {'row','col'}, dimensions={0} | all-to-all | bytes 262144 | tf_op jit(solution)/shard_map/all_to_all | solution.py:232
  369.8 3.3 last.1
  (23 shorter events, 8.0 us)
Async XLA Ops:
  15.6 35.1 %all-to-all-start.1 = ((f32[16,48,768]{2,1,0:T(8,128)}), f32[16,48,768]{2,1,0:T(8,128)S(1)}, u32[]{:S(2)}, u32[]{:S(2)}) async-start(f32[16,48,768]{2,1,0:T(8,128)} %bitcast.65), calls=%async_computation.1 | async-start | bytes 4718592 | tf_op jit(solution)/shard_map/all_to_all | solution.py:227
  19.3 0.7 collective-permute-start
  20.1 0.7 collective-permute-start.1
  20.8 0.7 collective-permute-start.2
  21.5 20.3 %collective-permute-start.3 = (f32[32,768]{1,0:T(8,128)S(1)}, f32[32,768]{1,0:T(8,128)S(1)}, u32[]{:S(2)}, u32[]{:S(2)}) collective-permute-start(f32[32,768]{1,0:T(8,128)S(1)} %add.14), channel_id=1, source_target_pairs={{0,16},{32,48},{64,80},{96,112},{128,144},{160,176},{192,208},{224... | collective-permute-start | bytes 294920 | tf_op jit(solution)/shard_map/ppermute | solution.py:226
  331.6 38.2 %copy-start = (f32[768,768]{1,0:T(8,128)S(1)}, f32[768,768]{1,0:T(8,128)}, u32[]{:S(2)}) copy-start(f32[768,768]{1,0:T(8,128)} %refs_31_.1) | copy-start | bytes 7077892

commit v7 on v6

--- a/solution.py
+++ b/solution.py
@@ -25,8 +25,8 @@
     return lax.broadcasted_iota(jnp.int32, shape, dim)
 
 
-def unpack(load):
-    lane = iota((8, LANES), 1)
+def unpack(load, turn=0):
+    lane = (iota((8, LANES), 1) - turn) & (LANES - 1)
     tiles = []
     for gm in range(4):
         q = [load(8 * gm + k) for k in range(8)]
@@ -149,9 +149,9 @@
         r = column[m] * inverse
         un_ref[m] = jnp.where(position(0) == j + 1, 1.0, r) if m == 0 else r
     if j < PANEL_COLUMNS - 1:
-        after = unpack(lambda first: pltpu.roll(got_ref[pl.ds(first, 8, stride=32), :], LANES - OWN, 1))
-        for m in range(TILES):
-            outs[2][m] = after[m]
+        after = unpack(lambda first: got_ref[pl.ds(first, 8, stride=32), :], OWN)
+        for m in range(TILES):
+            outs[2][m] = pltpu.roll(after[m], LANES - OWN, 1)
     un_ref[SCALE] = jnp.broadcast_to(scale_now, (8, LANES))
     lane, row = iota((8, LANES), 1), iota((8, LANES), 0)
     before = jnp.zeros((8, LANES), jnp.float32) if j == 0 else u_ref[COEF]

time: 374 us -> 374 us (level)
  no operation moved by 1% of the time
where the time goes in v7:
time: 374 us; the launch traced here: 373 us
  blocking collectives  318 us (85%)
  waiting for transfers between devices  27.7 us (7%)
  Pallas kernels  18.7 us (5%)
  starting transfers between devices  7.03 us (2%)
    all_to_all x16, blocking collectives, exchange(): lax.all_to_all(packed, ('row', 'col'), split_axis=0, concat_axis=0, tiled...  304 us
    ppermute x4, waiting for transfers between devices, per_device(): lax.ppermute(top, 'row', [(n, n + far) for n in range(0, 16, 2 * far)])  19 us
    pallas_call x16, Pallas kernels, step(): pl.pallas_call(functools.partial(step_body, j), out_shape=out, in_specs=[...  15.3 us
    all_to_all x1, blocking collectives, per_device(): lax.all_to_all(jnp.broadcast_to(matrix[:2], (ways, 2, tile_cols)), 'col',...  14.1 us
    all_to_all x1, waiting for transfers between devices, per_device(): lax.all_to_all(matrix_after.reshape(ways, OWN, tile_cols), 'col', split_a...  8.67 us
  transfers between devices with their start and end apart: 5, of which 2 were waited for; matrix products, arithmetic and copies ran while one was open for 0% of the time, Pallas kernels for 0%

profile of v7, /device:TPU:1, one launch (start us, length us, event | category | flops | bytes accessed | tf_op | source)
XLA Modules:
  0.0 373.2 jit_solution(18198923193009060641)
XLA Ops:
  1.4 14.1 %all_to_all.186 = f32[16,2,768]{2,1,0:T(2,128)S(1)} all-to-all(f32[16,2,768]{2,1,0:T(2,128)S(1)} %broadcast_in_dim.7), channel_id=1, replica_groups=mesh['row'=16,'col'=16] {'col'}, dimensions={0} | all-to-all | bytes 196608 | tf_op jit(solution)/shard_map/all_to_all | solution.py:220
  15.6 3.7 %all-to-all-start.1 = ((f32[16,48,768]{2,1,0:T(8,128)}), f32[16,48,768]{2,1,0:T(8,128)S(1)}, u32[]{:S(2)}, u32[]{:S(2)}) async-start(f32[16,48,768]{2,1,0:T(8,128)} %bitcast.65), calls=%async_computation.1 | async-start | bytes 4718592 | tf_op jit(solution)/shard_map/all_to_all | solution.py:227
  21.5 1.3 collective-permute-start.3
  22.8 19.0 %collective-permute-done.3 = f32[32,768]{1,0:T(8,128)S(1)} collective-permute-done((f32[32,768]{1,0:T(8,128)S(1)}, f32[32,768]{1,0:T(8,128)S(1)}, u32[]{:S(2)}, u32[]{:S(2)}) %collective-permute-start.3) | collective-permute-done | bytes 98336 | tf_op jit(solution)/shard_map/ppermute | solution.py:226
  42.0 8.7 %all-to-all-done.1.refs_1_ = f32[16,48,768]{2,1,0:T(8,128)S(1)} async-done(((f32[16,48,768]{2,1,0:T(8,128)}), f32[16,48,768]{2,1,0:T(8,128)S(1)}, u32[]{:S(2)}, u32[]{:S(2)}) %all-to-all-start.1) | async-done | bytes 2359328 | tf_op jit(solution)/shard_map/all_to_all | solution.py:227
  51.2 26.6 %all_to_all.187 = f32[256,1,128]{2,1,0:T(1,128)S(1)} all-to-all(f32[256,1,128]{2,1,0:T(1,128)S(1)} %bitcast.97), channel_id=1, replica_groups=mesh['row'=16,'col'=16] {'row','col'}, dimensions={0} | all-to-all | bytes 262144 | tf_op jit(solution)/shard_map/all_to_all | solution.py:232
  78.7 18.4 %all_to_all.188 = f32[256,1,128]{2,1,0:T(1,128)S(1)} all-to-all(f32[256,1,128]{2,1,0:T(1,128)S(1)} %bitcast.82), channel_id=1, replica_groups=mesh['row'=16,'col'=16] {'row','col'}, dimensions={0} | all-to-all | bytes 262144 | tf_op jit(solution)/shard_map/all_to_all | solution.py:232
  98.0 18.4 %all_to_all.189 = f32[256,1,128]{2,1,0:T(1,128)S(1)} all-to-all(f32[256,1,128]{2,1,0:T(1,128)S(1)} %bitcast.83), channel_id=1, replica_groups=mesh['row'=16,'col'=16] {'row','col'}, dimensions={0} | all-to-all | bytes 262144 | tf_op jit(solution)/shard_map/all_to_all | solution.py:232
  117.3 18.4 %all_to_all.190 = f32[256,1,128]{2,1,0:T(1,128)S(1)} all-to-all(f32[256,1,128]{2,1,0:T(1,128)S(1)} %bitcast.84), channel_id=1, replica_groups=mesh['row'=16,'col'=16] {'row','col'}, dimensions={0} | all-to-all | bytes 262144 | tf_op jit(solution)/shard_map/all_to_all | solution.py:232
  136.7 18.4 %all_to_all.191 = f32[256,1,128]{2,1,0:T(1,128)S(1)} all-to-all(f32[256,1,128]{2,1,0:T(1,128)S(1)} %bitcast.85), channel_id=1, replica_groups=mesh['row'=16,'col'=16] {'row','col'}, dimensions={0} | all-to-all | bytes 262144 | tf_op jit(solution)/shard_map/all_to_all | solution.py:232
  156.1 18.4 %all_to_all.192 = f32[256,1,128]{2,1,0:T(1,128)S(1)} all-to-all(f32[256,1,128]{2,1,0:T(1,128)S(1)} %bitcast.86), channel_id=1, replica_groups=mesh['row'=16,'col'=16] {'row','col'}, dimensions={0} | all-to-all | bytes 262144 | tf_op jit(solution)/shard_map/all_to_all | solution.py:232
  174.5 0.9 step6.1
  175.4 18.6 %all_to_all.193 = f32[256,1,128]{2,1,0:T(1,128)S(1)} all-to-all(f32[256,1,128]{2,1,0:T(1,128)S(1)} %bitcast.87), channel_id=1, replica_groups=mesh['row'=16,'col'=16] {'row','col'}, dimensions={0} | all-to-all | bytes 262144 | tf_op jit(solution)/shard_map/all_to_all | solution.py:232
  194.1 0.9 step7.1
  195.0 18.4 %all_to_all.194 = f32[256,1,128]{2,1,0:T(1,128)S(1)} all-to-all(f32[256,1,128]{2,1,0:T(1,128)S(1)} %bitcast.88), channel_id=1, replica_groups=mesh['row'=16,'col'=16] {'row','col'}, dimensions={0} | all-to-all | bytes 262144 | tf_op jit(solution)/shard_map/all_to_all | solution.py:232
  213.4 1.0 step8.1
  214.4 18.4 %all_to_all.195 = f32[256,1,128]{2,1,0:T(1,128)S(1)} all-to-all(f32[256,1,128]{2,1,0:T(1,128)S(1)} %bitcast.89), channel_id=1, replica_groups=mesh['row'=16,'col'=16] {'row','col'}, dimensions={0} | all-to-all | bytes 262144 | tf_op jit(solution)/shard_map/all_to_all | solution.py:232
  232.9 1.0 step9.1
  233.9 18.4 %all_to_all.196 = f32[256,1,128]{2,1,0:T(1,128)S(1)} all-to-all(f32[256,1,128]{2,1,0:T(1,128)S(1)} %bitcast.90), channel_id=1, replica_groups=mesh['row'=16,'col'=16] {'row','col'}, dimensions={0} | all-to-all | bytes 262144 | tf_op jit(solution)/shard_map/all_to_all | solution.py:232
  252.3 1.0 step10.1
  253.3 18.4 %all_to_all.197 = f32[256,1,128]{2,1,0:T(1,128)S(1)} all-to-all(f32[256,1,128]{2,1,0:T(1,128)S(1)} %bitcast.91), channel_id=1, replica_groups=mesh['row'=16,'col'=16] {'row','col'}, dimensions={0} | all-to-all | bytes 262144 | tf_op jit(solution)/shard_map/all_to_all | solution.py:232
  271.8 1.1 step11.1
  272.8 18.4 %all_to_all.198 = f32[256,1,128]{2,1,0:T(1,128)S(1)} all-to-all(f32[256,1,128]{2,1,0:T(1,128)S(1)} %bitcast.92), channel_id=1, replica_groups=mesh['row'=16,'col'=16] {'row','col'}, dimensions={0} | all-to-all | bytes 262144 | tf_op jit(solution)/shard_map/all_to_all | solution.py:232
  291.3 1.1 step12.1
  292.3 18.7 %all_to_all.199 = f32[256,1,128]{2,1,0:T(1,128)S(1)} all-to-all(f32[256,1,128]{2,1,0:T(1,128)S(1)} %bitcast.93), channel_id=1, replica_groups=mesh['row'=16,'col'=16] {'row','col'}, dimensions={0} | all-to-all | bytes 262144 | tf_op jit(solution)/shard_map/all_to_all | solution.py:232
  311.0 1.1 step13.1
  312.1 18.4 %all_to_all.200 = f32[256,1,128]{2,1,0:T(1,128)S(1)} all-to-all(f32[256,1,128]{2,1,0:T(1,128)S(1)} %bitcast.94), channel_id=1, replica_groups=mesh['row'=16,'col'=16] {'row','col'}, dimensions={0} | all-to-all | bytes 262144 | tf_op jit(solution)/shard_map/all_to_all | solution.py:232
  330.5 1.1 step14.1
  331.6 18.6 %all_to_all.201 = f32[256,1,128]{2,1,0:T(1,128)S(1)} all-to-all(f32[256,1,128]{2,1,0:T(1,128)S(1)} %bitcast.95), channel_id=1, replica_groups=mesh['row'=16,'col'=16] {'row','col'}, dimensions={0} | all-to-all | bytes 262144 | tf_op jit(solution)/shard_map/all_to_all | solution.py:232
  350.2 1.1 step15.1
  351.4 18.4 %all_to_all.202 = f32[256,1,128]{2,1,0:T(1,128)S(1)} all-to-all(f32[256,1,128]{2,1,0:T(1,128)S(1)} %bitcast.96), channel_id=1, replica_groups=mesh['row'=16,'col'=16] {'row','col'}, dimensions={0} | all-to-all | bytes 262144 | tf_op jit(solution)/shard_map/all_to_all | solution.py:232
  369.8 3.3 last.1
  (23 shorter events, 8.0 us)
Async XLA Ops:
  15.6 35.1 %all-to-all-start.1 = ((f32[16,48,768]{2,1,0:T(8,128)}), f32[16,48,768]{2,1,0:T(8,128)S(1)}, u32[]{:S(2)}, u32[]{:S(2)}) async-start(f32[16,48,768]{2,1,0:T(8,128)} %bitcast.65), calls=%async_computation.1 | async-start | bytes 4718592 | tf_op jit(solution)/shard_map/all_to_all | solution.py:227
  19.3 0.7 collective-permute-start
  20.1 0.7 collective-permute-start.1
  20.8 0.7 collective-permute-start.2
  21.5 20.3 %collective-permute-start.3 = (f32[32,768]{1,0:T(8,128)S(1)}, f32[32,768]{1,0:T(8,128)S(1)}, u32[]{:S(2)}, u32[]{:S(2)}) collective-permute-start(f32[32,768]{1,0:T(8,128)S(1)} %add.14), channel_id=1, source_target_pairs={{0,16},{32,48},{64,80},{96,112},{128,144},{160,176},{192,208},{224... | collective-permute-start | bytes 294920 | tf_op jit(solution)/shard_map/ppermute | solution.py:226
  331.6 38.2 %copy-start = (f32[768,768]{1,0:T(8,128)S(1)}, f32[768,768]{1,0:T(8,128)}, u32[]{:S(2)}) copy-start(f32[768,768]{1,0:T(8,128)} %refs_31_.1) | copy-start | bytes 7077892
